TPU v7x, 32 devices: a whole 2x2x4 slice. The times are simulated.
32 devices in a mesh: dp: 8 (over z, core), mp: 4 (over y, x).
Axes of the slice: x: 2, y: 2, z: 4, core: 2. Of those that a mesh axis runs over, the one named last changes fastest.
Arguments:
- image_input: bfloat16 [16384, 1536], P(('dp', 'mp')), may hold values from -16 to 16
- text_input: bfloat16 [2560, 1536], P(('dp', 'mp')), may hold values from -16 to 16
- timesteps: int32 [16], replicated, may hold values from 0 to 999
- key_mask: int32 [16, 160], P('dp'), may hold values from 0 to 1, as said below
- mod_weight: bfloat16 [2, 2, 1536, 6, 1536], P(None, None, 'dp', None, 'mp'), may hold values from -0.21875 to 0.21875
- qkv_weight: bfloat16 [2, 2, 3, 1536, 1536], P(None, None, None, 'dp', 'mp'), may hold values from -0.15625 to 0.15625
- out_weight: bfloat16 [2, 2, 1536, 1536], P(None, None, 'mp', 'dp'), may hold values from -2.5 to 2.5
- up_weight: bfloat16 [2, 2, 1536, 6144], P(None, None, 'dp', 'mp'), may hold values from -0.15625 to 0.15625
- down_weight: bfloat16 [2, 2, 6144, 1536], P(None, None, 'mp', 'dp'), may hold values from -0.078125 to 0.078125
- image_cotangent: bfloat16 [16384, 1536], P(('dp', 'mp')), may hold values from -6 to 6
- text_cotangent: bfloat16 [2560, 1536], P(('dp', 'mp')), may hold values from -6 to 6
Outputs:
- image_output: bfloat16 [16384, 1536], P(('dp', 'mp'))
- text_output: bfloat16 [2560, 1536], P(('dp', 'mp'))
- image_grad: float32 [16384, 1536], P(('dp', 'mp'))
- text_grad: float32 [2560, 1536], P(('dp', 'mp'))
- grad_mod: float32 [2, 2, 1536, 6, 1536], P(None, None, 'dp', None, 'mp')
- grad_qkv: float32 [2, 2, 3, 1536, 1536], P(None, None, None, 'dp', 'mp')
- grad_out: float32 [2, 2, 1536, 1536], P(None, None, 'mp', 'dp')
- grad_up: float32 [2, 2, 1536, 6144], P(None, None, 'dp', 'mp')
- grad_down: float32 [2, 2, 6144, 1536], P(None, None, 'mp', 'dp')
Inputs may be any that keep to these rules, and one draw needn't show every extreme that they name: `key_mask`: every row holds exactly 154 ones.
All inputs are finite; a program needn't handle non-finite values.
Results may differ from a plain program's by a relative error of at most 0.03.
Values may be sent and summed in bfloat16 or wider, within the bound.
A program may use at most 512 MiB of HBM per device.

v0:
```python
import math

import jax
import jax.numpy as jnp
from jax import lax
from jax.sharding import PartitionSpec as P

D = 1536
HEAD_DIM = 64
IMG = 1024
TXT = 160
LAYERS = 2


HIGHEST = lax.Precision.HIGHEST
EPSILON = 1e-06


def conditioning(steps):
    half_width = D // 2
    frequency = jnp.exp(-math.log(10000.0) * jnp.arange(half_width, dtype=jnp.float32) / half_width)
    phases = steps.astype(jnp.float32)[..., None] * frequency
    embedded = jnp.concatenate([jnp.cos(phases), jnp.sin(phases)], axis=-1)
    return embedded / (1.0 + jnp.exp(-embedded))


def norm_mod(values, offset, stretch):
    centred = values - jnp.mean(values, axis=-1, keepdims=True)
    variance = jnp.mean(centred * centred, axis=-1, keepdims=True)
    return centred * lax.rsqrt(variance + EPSILON) * (1.0 + stretch) + offset


def gelu_tanh(values):
    return (
        0.5
        * values
        * (1.0 + jnp.tanh(0.7978845608028654 * (values + 0.044715 * values * values * values)))
    )


def row_table(row_count, length, seq_count):
    position = lax.axis_index("mp") * row_count + jnp.arange(row_count, dtype=jnp.int32)
    owner = position // length
    return (owner[:, None] == jnp.arange(seq_count, dtype=jnp.int32)[None, :]).astype(jnp.float32)


def spread_rows(streams_pair):
    return (
        lax.all_gather(streams_pair[0], "mp", axis=0, tiled=True),
        lax.all_gather(streams_pair[1], "mp", axis=0, tiled=True),
    )


def collect_rows(streams_pair):
    return (
        lax.psum_scatter(
            streams_pair[0].astype(jnp.bfloat16), "mp", scatter_dimension=0, tiled=True
        ).astype(jnp.float32),
        lax.psum_scatter(
            streams_pair[1].astype(jnp.bfloat16), "mp", scatter_dimension=0, tiled=True
        ).astype(jnp.float32),
    )


def spread_grads(streams_pair):
    return (
        lax.all_gather(streams_pair[0], "mp", axis=0, tiled=True),
        lax.all_gather(streams_pair[1], "mp", axis=0, tiled=True),
    )


def collect_grads(streams_pair):
    return (
        lax.psum_scatter(
            streams_pair[0].astype(jnp.bfloat16), "mp", scatter_dimension=0, tiled=True
        ).astype(jnp.float32),
        lax.psum_scatter(
            streams_pair[1].astype(jnp.bfloat16), "mp", scatter_dimension=0, tiled=True
        ).astype(jnp.float32),
    )


def join_heads(projected, seq_count):
    heads_local = projected[0].shape[2] // HEAD_DIM
    image_part = projected[0].reshape(3, seq_count, IMG, heads_local, HEAD_DIM)
    text_part = projected[1].reshape(3, seq_count, TXT, heads_local, HEAD_DIM)
    return jnp.moveaxis(jnp.concatenate([image_part, text_part], axis=2), 1, 0)


def join_rows(streams_pair, seq_count):
    heads_local = streams_pair[0].shape[1] // HEAD_DIM
    image_part = streams_pair[0].reshape(seq_count, IMG, heads_local, HEAD_DIM)
    text_part = streams_pair[1].reshape(seq_count, TXT, heads_local, HEAD_DIM)
    return jnp.concatenate([image_part, text_part], axis=1)


def split_rows(joined, seq_count):
    return (
        joined[:, :IMG].reshape(seq_count * IMG, -1),
        joined[:, IMG:].reshape(seq_count * TXT, -1),
    )


def split_heads(joined, seq_count):
    moved = jnp.moveaxis(joined, 0, 1)
    return (
        moved[:, :, :IMG].reshape(3, seq_count * IMG, -1),
        moved[:, :, IMG:].reshape(3, seq_count * TXT, -1),
    )


def attend(parts, valid_row, score_scale):
    raw_scores = jnp.einsum("qhd,khd->hqk", parts[0], parts[1], preferred_element_type=jnp.float32)
    scores = jnp.where(valid_row[None, None, :], raw_scores * score_scale, -1e30)
    row_max = jnp.max(scores, axis=-1, keepdims=True)
    exponent = jnp.exp(scores - row_max)
    totals = jnp.sum(exponent, axis=-1, keepdims=True)
    softmax_low = (exponent / totals).astype(jnp.bfloat16)
    mixture = jnp.einsum(
        "hqk,khd->qhd", softmax_low, parts[2], preferred_element_type=jnp.float32
    ).astype(jnp.bfloat16)
    return (mixture, (row_max + jnp.log(totals))[..., 0])


def attend_back(parts, valid_row, log_total, grad_mixture, score_scale):
    raw_scores = jnp.einsum("qhd,khd->hqk", parts[0], parts[1], preferred_element_type=jnp.float32)
    scores = jnp.where(valid_row[None, None, :], raw_scores * score_scale, -1e30)
    softmax = jnp.exp(scores - log_total[..., None])
    grad_values = jnp.einsum(
        "hqk,qhd->khd",
        softmax.astype(jnp.bfloat16),
        grad_mixture,
        preferred_element_type=jnp.float32,
    )
    grad_softmax = jnp.einsum(
        "qhd,khd->hqk", grad_mixture, parts[2], preferred_element_type=jnp.float32
    )
    grad_scores = softmax * (grad_softmax - jnp.sum(softmax * grad_softmax, axis=-1, keepdims=True))
    grad_raw = (grad_scores * score_scale).astype(jnp.bfloat16)
    grad_query = jnp.einsum("hqk,khd->qhd", grad_raw, parts[1], preferred_element_type=jnp.float32)
    grad_keys = jnp.einsum("hqk,qhd->khd", grad_raw, parts[0], preferred_element_type=jnp.float32)
    return jnp.stack([grad_query, grad_keys, grad_values]).astype(jnp.bfloat16)


def row_modulation(tables, modulation):
    return tuple(
        (
            jnp.einsum("rn,nkd->rkd", tables[stream], modulation[stream], precision=HIGHEST)
            for stream in range(2)
        )
    )


def layer_forward(streams, local_mod, gathered, tables, valid, seq_count, score_scale):
    qkv_full, out_full, up_full, down_full = gathered
    modulation = (
        lax.all_gather(local_mod[0], "mp", axis=2, tiled=True),
        lax.all_gather(local_mod[1], "mp", axis=2, tiled=True),
    )
    gates = row_modulation(tables, modulation)
    normed_one = tuple(
        (
            norm_mod(streams[stream], gates[stream][:, 0], gates[stream][:, 1]).astype(jnp.bfloat16)
            for stream in range(2)
        )
    )
    first_rows = spread_rows(normed_one)
    projected = tuple(
        (
            jnp.einsum(
                "nd,kdc->knc",
                first_rows[stream],
                qkv_full[stream],
                preferred_element_type=jnp.float32,
            ).astype(jnp.bfloat16)
            for stream in range(2)
        )
    )
    joined = join_heads(projected, seq_count)

    def forward_element(element):
        return attend(element[0], element[1], score_scale)

    mixture_all, log_total = lax.map(forward_element, (joined, valid))
    mixtures = split_rows(mixture_all, seq_count)
    branch_one = collect_rows(
        tuple(
            (
                jnp.dot(mixtures[stream], out_full[stream], preferred_element_type=jnp.float32)
                for stream in range(2)
            )
        )
    )
    middle = tuple(
        (streams[stream] + gates[stream][:, 2] * branch_one[stream] for stream in range(2))
    )
    normed_two = tuple(
        (
            norm_mod(middle[stream], gates[stream][:, 3], gates[stream][:, 4]).astype(jnp.bfloat16)
            for stream in range(2)
        )
    )
    second_rows = spread_rows(normed_two)
    pre_act = tuple(
        (
            jnp.dot(second_rows[stream], up_full[stream], preferred_element_type=jnp.float32)
            for stream in range(2)
        )
    )
    branch_two = collect_rows(
        tuple(
            (
                jnp.dot(
                    gelu_tanh(pre_act[stream]).astype(jnp.bfloat16),
                    down_full[stream],
                    preferred_element_type=jnp.float32,
                )
                for stream in range(2)
            )
        )
    )
    outputs = tuple(
        (middle[stream] + gates[stream][:, 5] * branch_two[stream] for stream in range(2))
    )
    kept = (
        streams,
        modulation,
        first_rows,
        joined,
        log_total,
        mixtures,
        branch_one,
        middle,
        second_rows,
        pre_act,
        branch_two,
    )
    return (outputs, kept)


def layer_backward(upstream, kept, gathered, tables, valid, seq_count, score_scale):
    qkv_full, out_full, up_full, down_full = gathered
    (
        inputs,
        modulation,
        first_rows,
        joined,
        log_total,
        mixtures,
        branch_one,
        middle,
        second_rows,
        pre_act,
        branch_two,
    ) = kept
    gates = row_modulation(tables, modulation)
    grad_branch_two = spread_grads(
        tuple(
            ((upstream[stream] * gates[stream][:, 5]).astype(jnp.bfloat16) for stream in range(2))
        )
    )
    grad_down = []
    grad_up = []
    partial_two = []
    for stream in range(2):
        activation = gelu_tanh(pre_act[stream]).astype(jnp.bfloat16)
        grad_down.append(
            jnp.einsum(
                "nf,nd->fd", activation, grad_branch_two[stream], preferred_element_type=jnp.float32
            )
        )
        grad_act = jnp.einsum(
            "nd,fd->nf",
            grad_branch_two[stream],
            down_full[stream],
            preferred_element_type=jnp.float32,
        )
        grad_pre = jax.vjp(gelu_tanh, pre_act[stream])[1](grad_act)[0].astype(jnp.bfloat16)
        grad_up.append(
            jnp.einsum(
                "nd,nf->df", second_rows[stream], grad_pre, preferred_element_type=jnp.float32
            )
        )
        partial_two.append(
            jnp.einsum("nf,df->nd", grad_pre, up_full[stream], preferred_element_type=jnp.float32)
        )
    grad_normed_two = collect_grads(tuple(partial_two))
    grad_middle = []
    norm_two_grads = []
    for stream in range(2):
        pullback = jax.vjp(norm_mod, middle[stream], gates[stream][:, 3], gates[stream][:, 4])[1]
        grad_rows, grad_offset, grad_stretch = pullback(grad_normed_two[stream])
        grad_middle.append(upstream[stream] + grad_rows)
        norm_two_grads.append((grad_offset, grad_stretch))
    grad_branch_one = spread_grads(
        tuple(
            (
                (grad_middle[stream] * gates[stream][:, 2]).astype(jnp.bfloat16)
                for stream in range(2)
            )
        )
    )
    grad_out = []
    grad_mixtures = []
    for stream in range(2):
        grad_out.append(
            jnp.einsum(
                "nc,nd->cd",
                mixtures[stream],
                grad_branch_one[stream],
                preferred_element_type=jnp.float32,
            )
        )
        grad_mixtures.append(
            jnp.einsum(
                "nd,cd->nc",
                grad_branch_one[stream],
                out_full[stream],
                preferred_element_type=jnp.float32,
            ).astype(jnp.bfloat16)
        )
    grad_joined_mixture = join_rows(tuple(grad_mixtures), seq_count)

    def backward_element(element):
        return attend_back(element[0], element[1], element[2], element[3], score_scale)

    grad_parts = lax.map(backward_element, (joined, valid, log_total, grad_joined_mixture))
    grad_projected = split_heads(grad_parts, seq_count)
    grad_qkv = []
    partial_one = []
    for stream in range(2):
        grad_qkv.append(
            jnp.einsum(
                "nd,knc->kdc",
                first_rows[stream],
                grad_projected[stream],
                preferred_element_type=jnp.float32,
            )
        )
        partial_one.append(
            jnp.einsum(
                "knc,kdc->nd",
                grad_projected[stream],
                qkv_full[stream],
                preferred_element_type=jnp.float32,
            )
        )
    grad_normed_one = collect_grads(tuple(partial_one))
    grad_inputs = []
    sequence_grads = []
    for stream in range(2):
        pullback = jax.vjp(norm_mod, inputs[stream], gates[stream][:, 0], gates[stream][:, 1])[1]
        grad_rows, grad_offset, grad_stretch = pullback(grad_normed_one[stream])
        grad_inputs.append(grad_middle[stream] + grad_rows)
        row_grad = jnp.stack(
            [
                grad_offset,
                grad_stretch,
                grad_middle[stream] * branch_one[stream],
                norm_two_grads[stream][0],
                norm_two_grads[stream][1],
                upstream[stream] * branch_two[stream],
            ],
            axis=1,
        )
        sequence_grads.append(
            jnp.einsum("rn,rkd->nkd", tables[stream], row_grad, precision=HIGHEST)
        )
    mod_sums = (
        lax.psum_scatter(
            sequence_grads[0].astype(jnp.bfloat16), "mp", scatter_dimension=2, tiled=True
        ).astype(jnp.float32),
        lax.psum_scatter(
            sequence_grads[1].astype(jnp.bfloat16), "mp", scatter_dimension=2, tiled=True
        ).astype(jnp.float32),
    )
    four_grads = (
        jnp.stack(grad_qkv),
        jnp.stack(grad_out),
        jnp.stack(grad_up),
        jnp.stack(grad_down),
    )
    return (tuple(grad_inputs), mod_sums, four_grads)


def on_device(
    image_input,
    text_input,
    timesteps,
    key_mask,
    mod_weight,
    qkv_weight,
    out_weight,
    up_weight,
    down_weight,
    image_cotangent,
    text_cotangent,
):
    seq_count = key_mask.shape[0]
    score_scale = HEAD_DIM ** (-0.5)
    own_steps = lax.dynamic_slice_in_dim(timesteps, lax.axis_index("dp") * seq_count, seq_count)
    condition = conditioning(own_steps).astype(jnp.bfloat16)
    condition_wide = condition.astype(jnp.float32)
    valid = jnp.concatenate([jnp.ones((seq_count, IMG), dtype=bool), key_mask > 0], axis=1)
    tables = (
        row_table(image_input.shape[0], IMG, seq_count),
        row_table(text_input.shape[0], TXT, seq_count),
    )
    streams = (image_input.astype(jnp.float32), text_input.astype(jnp.float32))
    stored = []
    for layer_index in range(LAYERS):
        whole_block = (
            mod_weight[layer_index],
            qkv_weight[layer_index],
            out_weight[layer_index],
            up_weight[layer_index],
            down_weight[layer_index],
        )
        gathered_all = (
            lax.all_gather(whole_block[0], "dp", axis=1, tiled=True),
            lax.all_gather(whole_block[1], "dp", axis=2, tiled=True),
            lax.all_gather(whole_block[2], "dp", axis=2, tiled=True),
            lax.all_gather(whole_block[3], "dp", axis=1, tiled=True),
            lax.all_gather(whole_block[4], "dp", axis=2, tiled=True),
        )
        gathered = (gathered_all[1], gathered_all[2], gathered_all[3], gathered_all[4])
        local_mod = tuple(
            (
                jnp.einsum(
                    "nd,dkc->nkc",
                    condition,
                    gathered_all[0][stream],
                    preferred_element_type=jnp.float32,
                )
                for stream in range(2)
            )
        )
        held = whole_block
        streams, kept = layer_forward(
            streams, local_mod, gathered, tables, valid, seq_count, score_scale
        )
        stored.append((held, kept))
    upstream = (image_cotangent.astype(jnp.float32), text_cotangent.astype(jnp.float32))
    reduced_blocks = []
    for layer_index in reversed(range(LAYERS)):
        held, kept = stored[layer_index]
        again_all = (
            lax.all_gather(held[0], "dp", axis=1, tiled=True),
            lax.all_gather(held[1], "dp", axis=2, tiled=True),
            lax.all_gather(held[2], "dp", axis=2, tiled=True),
            lax.all_gather(held[3], "dp", axis=1, tiled=True),
            lax.all_gather(held[4], "dp", axis=2, tiled=True),
        )
        gathered = (again_all[1], again_all[2], again_all[3], again_all[4])
        upstream, mod_sums, four_grads = layer_backward(
            upstream, kept, gathered, tables, valid, seq_count, score_scale
        )
        grad_mod = jnp.stack(
            [
                jnp.einsum("nd,nkc->dkc", condition_wide, mod_sums[stream], precision=HIGHEST)
                for stream in range(2)
            ]
        )
        reduced = (
            lax.psum_scatter(
                grad_mod.astype(jnp.bfloat16), "dp", scatter_dimension=1, tiled=True
            ).astype(jnp.float32),
            lax.psum_scatter(
                four_grads[0].astype(jnp.bfloat16), "dp", scatter_dimension=2, tiled=True
            ).astype(jnp.float32),
            lax.psum_scatter(
                four_grads[1].astype(jnp.bfloat16), "dp", scatter_dimension=2, tiled=True
            ).astype(jnp.float32),
            lax.psum_scatter(
                four_grads[2].astype(jnp.bfloat16), "dp", scatter_dimension=1, tiled=True
            ).astype(jnp.float32),
            lax.psum_scatter(
                four_grads[3].astype(jnp.bfloat16), "dp", scatter_dimension=2, tiled=True
            ).astype(jnp.float32),
        )
        reduced_blocks.insert(0, reduced)
    results = [
        jnp.stack([block_sums[member] for block_sums in reduced_blocks]) for member in range(5)
    ]
    return (
        streams[0].astype(jnp.bfloat16),
        streams[1].astype(jnp.bfloat16),
        upstream[0],
        upstream[1],
        results[0],
        results[1],
        results[2],
        results[3],
        results[4],
    )


def solution(mesh):
    return jax.shard_map(
        on_device,
        mesh=mesh,
        in_specs=(
            P(("dp", "mp"), None),
            P(("dp", "mp"), None),
            P(),
            P("dp", None),
            P(None, None, "dp", None, "mp"),
            P(None, None, None, "dp", "mp"),
            P(None, None, "mp", "dp"),
            P(None, None, "dp", "mp"),
            P(None, None, "mp", "dp"),
            P(("dp", "mp"), None),
            P(("dp", "mp"), None),
        ),
        out_specs=(
            P(("dp", "mp"), None),
            P(("dp", "mp"), None),
            P(("dp", "mp"), None),
            P(("dp", "mp"), None),
            P(None, None, "dp", None, "mp"),
            P(None, None, None, "dp", "mp"),
            P(None, None, "mp", "dp"),
            P(None, None, "dp", "mp"),
            P(None, None, "mp", "dp"),
        ),
        check_vma=False,
    )
```

profile of v0, /device:TPU:0, one launch (start us, length us, event | category | flops | bytes accessed | tf_op | source)
XLA Modules:
  0.0 4551.3 jit_solution(9849040126425723890)
XLA Ops:
  14.6 129.5 %all-gather.45.cloned.1.call-done = bf16[1,2,1536,6,384]{4,2,3,1,0:T(8,128)(2,1)} async-done(((bf16[1,2,192,6,384]{4,2,3,1,0:T(8,128)(2,1)}), bf16[1,2,1536,6,384]{4,2,3,1,0:T(8,128)(2,1)}) %all-gather.45.cloned.1.call-update) | async-done | bytes 14155792 | tf_op jit(solution)/shard_map/all_gather | solution.py:420
  221.6 65.1 %all-gather.29.cloned.1.call-done = bf16[2048,1536]{1,0:T(8,128)(2,1)} async-done(((bf16[512,1536]{1,0:T(8,128)(2,1)}), bf16[2048,1536]{1,0:T(8,128)(2,1)}) %all-gather.29.cloned.1.call-update) | async-done | bytes 6291472 | tf_op jit(solution)/shard_map/all_gather | solution.py:49
  325.5 93.5 %while.44 = (s32[]{:T(128)}, bf16[2,1184,6,64]{1,3,2,0:T(8,128)(2,1)S(1)}, f32[2,6,1184]{2,1,0:T(8,128)S(1)}, bf16[2,3,1184,6,64]{2,4,3,1,0:T(8,128)(2,1)}, pred...) while((s32[]{:T(128)}, bf16[2,1184,6,64]{1,3,2,0:T(8,128)(2,1)S(1)}, ...), condition=%wide.region_7.8_spmd, body=%wide.region_4.7_spmd.sunk | while | flops 2220987392 | bytes 107890528 | solution.py:184
  433.7 66.9 %reduce-scatter.33.cloned.1.call-done = bf16[512,1536]{1,0:T(8,128)(2,1)} async-done(((bf16[2048,1536]{1,0:T(8,128)(2,1)}), bf16[512,1536]{1,0:T(8,128)(2,1)}) %reduce-scatter.33.cloned.1.call-update) | async-done | bytes 1572880 | tf_op jit(solution)/shard_map/reduce_scatter | solution.py:56
  520.5 72.8 %all-gather.51.cloned.1.call-done = bf16[1,2,1536,1536]{3,2,1,0:T(8,128)(2,1)} async-done(((bf16[1,2,192,1536]{3,2,1,0:T(8,128)(2,1)}), bf16[1,2,1536,1536]{3,2,1,0:T(8,128)(2,1)}) %all-gather.51.cloned.1.call-update) | async-done | bytes 9437200 | tf_op jit(solution)/shard_map/all_gather | solution.py:423
  593.3 70.9 %all-gather.31.cloned.1.call-done = bf16[2048,1536]{1,0:T(8,128)(2,1)} async-done(((bf16[512,1536]{1,0:T(8,128)(2,1)}), bf16[2048,1536]{1,0:T(8,128)(2,1)}) %all-gather.31.cloned.1.call-update) | async-done | bytes 6291472 | tf_op jit(solution)/shard_map/all_gather | solution.py:49
  680.4 76.8 %all-gather.53.cloned.1.call-done = bf16[1,2,1536,1536]{2,3,1,0:T(8,128)(2,1)} async-done(((bf16[1,2,1536,192]{2,3,1,0:T(8,128)(2,1)}), bf16[1,2,1536,1536]{2,3,1,0:T(8,128)(2,1)}) %all-gather.53.cloned.1.call-update) | async-done | bytes 9437200 | tf_op jit(solution)/shard_map/all_gather | solution.py:424
  815.0 103.3 %all-gather.55.cloned.1.call-done = bf16[1,2,1536,6,384]{4,2,3,1,0:T(8,128)(2,1)} async-done(((bf16[1,2,192,6,384]{4,2,3,1,0:T(8,128)(2,1)}), bf16[1,2,1536,6,384]{4,2,3,1,0:T(8,128)(2,1)}) %all-gather.55.cloned.1.call-update) | async-done | bytes 14155792 | tf_op jit(solution)/shard_map/all_gather | solution.py:420
  1203.5 93.1 %while.45 = (s32[]{:T(128)}, bf16[2,1184,6,64]{1,3,2,0:T(8,128)(2,1)S(1)}, f32[2,6,1184]{2,1,0:T(8,128)S(1)}, bf16[2,3,1184,6,64]{2,4,3,1,0:T(8,128)(2,1)}, pred...) while((s32[]{:T(128)}, bf16[2,1184,6,64]{1,3,2,0:T(8,128)(2,1)S(1)}, ...), condition=%wide.region_23.24_spmd, body=%wide.region_20.23_spmd.sunk | while | flops 2220987392 | bytes 107890528 | solution.py:184
  1308.7 69.6 %reduce-scatter.41.cloned.1.call-done = bf16[512,1536]{1,0:T(8,128)(2,1)} async-done(((bf16[2048,1536]{1,0:T(8,128)(2,1)}), bf16[512,1536]{1,0:T(8,128)(2,1)}) %reduce-scatter.41.cloned.1.call-update) | async-done | bytes 1572880 | tf_op jit(solution)/shard_map/reduce_scatter | solution.py:56
  1395.0 75.6 %all-gather.61.cloned.1.call-done = bf16[1,2,1536,1536]{3,2,1,0:T(8,128)(2,1)} async-done(((bf16[1,2,192,1536]{3,2,1,0:T(8,128)(2,1)}), bf16[1,2,1536,1536]{3,2,1,0:T(8,128)(2,1)}) %all-gather.61.cloned.1.call-update) | async-done | bytes 9437200 | tf_op jit(solution)/shard_map/all_gather | solution.py:423
  1470.5 70.7 %all-gather.35.cloned.1.call-done = bf16[2048,1536]{1,0:T(8,128)(2,1)} async-done(((bf16[512,1536]{1,0:T(8,128)(2,1)}), bf16[2048,1536]{1,0:T(8,128)(2,1)}) %all-gather.35.cloned.1.call-update) | async-done | bytes 6291472 | tf_op jit(solution)/shard_map/all_gather | solution.py:49
  1557.7 76.5 %all-gather.63.cloned.1.call-done = bf16[1,2,1536,1536]{2,3,1,0:T(8,128)(2,1)} async-done(((bf16[1,2,1536,192]{2,3,1,0:T(8,128)(2,1)}), bf16[1,2,1536,1536]{2,3,1,0:T(8,128)(2,1)}) %all-gather.63.cloned.1.call-update) | async-done | bytes 9437200 | tf_op jit(solution)/shard_map/all_gather | solution.py:424
  1634.2 70.7 %all-gather.37.cloned.1.call-done = bf16[2048,1536]{1,0:T(8,128)(2,1)} async-done(((bf16[512,1536]{1,0:T(8,128)(2,1)}), bf16[2048,1536]{1,0:T(8,128)(2,1)}) %all-gather.37.cloned.1.call-update) | async-done | bytes 6291472 | tf_op jit(solution)/shard_map/all_gather | solution.py:67
  1829.6 69.8 %reduce-scatter.43.cloned.1.call-done = bf16[512,1536]{1,0:T(8,128)(2,1)} async-done(((bf16[2048,1536]{1,0:T(8,128)(2,1)}), bf16[512,1536]{1,0:T(8,128)(2,1)}) %reduce-scatter.43.cloned.1.call-update) | async-done | bytes 1572880 | tf_op jit(solution)/shard_map/reduce_scatter | solution.py:56
  2049.4 286.8 %while.46 = (s32[]{:T(128)}, bf16[2,3,1184,6,64]{2,4,3,1,0:T(8,128)(2,1)}, bf16[2,3,1184,6,64]{2,4,3,1,0:T(8,128)(2,1)}, pred[2,1184]{1,0:T(4,128)(4,1)S(1)}, f3...) while((s32[]{:T(128)}, ...), condition=%wide.region_40.41_spmd, body=%wide.region_38.40_spmd.sunk | while | flops 5510447104 | bytes 407439232 | solution.py:327
  2373.6 69.7 %reduce-scatter.53.cloned.1.call-done = bf16[512,1536]{1,0:T(8,128)(2,1)} async-done(((bf16[2048,1536]{1,0:T(8,128)(2,1)}), bf16[512,1536]{1,0:T(8,128)(2,1)}) %reduce-scatter.53.cloned.1.call-update) | async-done | bytes 1572880 | tf_op jit(solution)/shard_map/reduce_scatter | solution.py:74
  2463.1 61.8 %all-gather.41.cloned.1.call-done = bf16[2048,1536]{1,0:T(8,128)(2,1)} async-done(((bf16[512,1536]{1,0:T(8,128)(2,1)}), bf16[2048,1536]{1,0:T(8,128)(2,1)}) %all-gather.41.cloned.1.call-update) | async-done | bytes 6291472 | tf_op jit(solution)/shard_map/all_gather | solution.py:67
  2764.9 286.9 %while.47 = (s32[]{:T(128)}, bf16[2,3,1184,6,64]{2,4,3,1,0:T(8,128)(2,1)}, bf16[2,3,1184,6,64]{2,4,3,1,0:T(8,128)(2,1)}, pred[2,1184]{1,0:T(4,128)(4,1)S(1)}, f3...) while((s32[]{:T(128)}, ...), condition=%wide.region_55.56_spmd, body=%wide.region_53.55_spmd.sunk | while | flops 5510447104 | bytes 407439232 | solution.py:327
  3499.5 95.8 %reduce-scatter.71.cloned.1.call-done = bf16[2,192,1536]{2,1,0:T(8,128)(2,1)} async-done(((bf16[2,1536,1536]{2,1,0:T(8,128)(2,1)}), bf16[2,192,1536]{2,1,0:T(8,128)(2,1)}) %reduce-scatter.71.cloned.1.call-update) | async-done | bytes 1179664 | tf_op jit(solution)/shard_map/reduce_scatter | solution.py:474
  3595.3 100.2 %reduce-scatter.69.cloned.1.call-done = bf16[2,192,1536]{2,1,0:T(8,128)(2,1)} async-done(((bf16[2,1536,1536]{2,1,0:T(8,128)(2,1)}), bf16[2,192,1536]{2,1,0:T(8,128)(2,1)}) %reduce-scatter.69.cloned.1.call-update) | async-done | bytes 1179664 | tf_op jit(solution)/shard_map/reduce_scatter | solution.py:474
  3712.3 535.7 %all-reduce.13.cloned.1.call-done = (bf16[2,3,1536,384]{3,0,1,2:T(2,128)(2,1)}, bf16[2,3,1536,384]{3,0,1,2:T(2,128)(2,1)}, bf16[2,384,1536]{1,0,2:T(2,128)(2,1)}...) async-done(((bf16[2,3,1536,384]{3,0,1,2:T(2,128)(2,1)}, bf16[2,3,1536,384]{3,0,1,2:T(2,128)(2,1)}, bf16[2,384,1536]{1,0,2:T(2,128)(2,1)}, ...) | async-done | bytes 28311568
  4266.8 127.6 %reduce-scatter.67.cloned.1.call-done = bf16[2,192,6,384]{3,1,2,0:T(8,128)(2,1)} async-done(((bf16[2,1536,6,384]{3,1,2,0:T(8,128)(2,1)}), bf16[2,192,6,384]{3,1,2,0:T(8,128)(2,1)}) %reduce-scatter.67.cloned.1.call-update) | async-done | bytes 1769488 | tf_op jit(solution)/shard_map/reduce_scatter | solution.py:465
  4394.4 144.8 %reduce-scatter.65.cloned.1.call-done = bf16[2,192,6,384]{3,1,2,0:T(8,128)(2,1)} async-done(((bf16[2,1536,6,384]{3,1,2,0:T(8,128)(2,1)}), bf16[2,192,6,384]{3,1,2,0:T(8,128)(2,1)}) %reduce-scatter.65.cloned.1.call-update) | async-done | bytes 1769488 | tf_op jit(solution)/shard_map/reduce_scatter | solution.py:465
  (855 shorter events, 2377.1 us)
Async XLA Ops:
  13.1 273.7 %all-gather.29.cloned.1.call-start = ((), (), s32[]{:S(2)}) async-start(), calls=%async_computation.24 | async-start | bytes 7864320 | tf_op jit(solution)/shard_map/all_gather | solution.py:49
  173.6 327.0 %reduce-scatter.33.cloned.1.call-start = ((), (), s32[]{:S(2)}) async-start(), calls=%async_computation.25 | async-start | bytes 7864320 | tf_op jit(solution)/shard_map/reduce_scatter | solution.py:56
  513.3 273.3 %reduce-scatter.37.cloned.1.call-start = ((), (), s32[]{:S(2)}) async-start(), calls=%async_computation.29 | async-start | bytes 1228800 | tf_op jit(solution)/shard_map/reduce_scatter | solution.py:59
  519.9 398.4 %all-gather.55.cloned.1.call-start = ((), (), s32[]{:S(2)}) async-start(), calls=%async_computation.57 | async-start | bytes 15925248 | tf_op jit(solution)/shard_map/all_gather | solution.py:420
  520.5 469.6 %reduce-scatter.35.cloned.1.call-start = ((), (), s32[]{:S(2)}) async-start(), calls=%async_computation.27 | async-start | bytes 7864320 | tf_op jit(solution)/shard_map/reduce_scatter | solution.py:56
  814.1 279.7 %all-gather.57.cloned.1.call-start = ((), (), s32[]{:S(2)}) async-start(), calls=%async_computation.58 | async-start | bytes 7962624 | tf_op jit(solution)/shard_map/all_gather | solution.py:421
  814.9 349.8 %all-gather.33.cloned.1.call-start = ((), (), s32[]{:S(2)}) async-start(), calls=%async_computation.28 | async-start | bytes 7864320 | tf_op jit(solution)/shard_map/all_gather | solution.py:49
  999.9 300.2 %all-gather.59.cloned.1.call-start = ((), (), s32[]{:S(2)}) async-start(), calls=%async_computation.59 | async-start | bytes 2654208 | tf_op jit(solution)/shard_map/all_gather | solution.py:422
  1000.5 377.8 %reduce-scatter.41.cloned.1.call-start = ((), (), s32[]{:S(2)}) async-start(), calls=%async_computation.31 | async-start | bytes 7864320 | tf_op jit(solution)/shard_map/reduce_scatter | solution.py:56
  1390.9 314.0 %all-gather.37.cloned.1.call-start = ((), (), s32[]{:S(2)}) async-start(), calls=%async_computation.36 | async-start | bytes 7864320 | tf_op jit(solution)/shard_map/all_gather | solution.py:67
  1391.5 371.1 %reduce-scatter.45.cloned.1.call-start = ((), (), s32[]{:S(2)}) async-start(), calls=%async_computation.34 | async-start | bytes 1228800 | tf_op jit(solution)/shard_map/reduce_scatter | solution.py:59
  1394.9 431.6 %reduce-scatter.49.cloned.1.call-start = ((), (), s32[]{:S(2)}) async-start(), calls=%async_computation.37 | async-start | bytes 7864320 | tf_op jit(solution)/shard_map/reduce_scatter | solution.py:74
  1910.5 532.8 %reduce-scatter.53.cloned.1.call-start = ((), (), s32[]{:S(2)}) async-start(), calls=%async_computation.40 | async-start | bytes 7864320 | tf_op jit(solution)/shard_map/reduce_scatter | solution.py:74
  2654.8 507.4 %reduce-scatter.63.cloned.1.call-start = ((), (), s32[]{:S(2)}) async-start(), calls=%async_computation.47 | async-start | bytes 1228800 | tf_op jit(solution)/shard_map/reduce_scatter | solution.py:77
  3097.2 363.9 %reduce-scatter.79.cloned.1.call-start = ((), (), s32[]{:S(2)}) async-start(), calls=%async_computation.65 | async-start | bytes 491520
  3111.7 355.9 %reduce-scatter.77.cloned.1.call-start = ((), (), s32[]{:S(2)}) async-start(), calls=%async_computation.64 | async-start | bytes 491520
  3144.3 333.9 %reduce-scatter.75.cloned.1.call-start = ((), (), s32[]{:S(2)}) async-start(), calls=%async_computation.63 | async-start | bytes 491520
  3173.7 310.8 %reduce-scatter.73.cloned.1.call-start = ((), (), s32[]{:S(2)}) async-start(), calls=%async_computation.62 | async-start | bytes 491520
  3217.3 280.1 %all-reduce.11.cloned.1.call-start = ((), (), s32[]{:S(2)}) async-start(), calls=%async_computation.66 | async-start | bytes 18874368
  3249.6 345.7 %reduce-scatter.71.cloned.1.call-start = ((), (), s32[]{:S(2)}) async-start(), calls=%async_computation.51 | async-start | bytes 10616832 | tf_op jit(solution)/shard_map/reduce_scatter | solution.py:474
  3279.1 416.5 %reduce-scatter.69.cloned.1.call-start = ((), (), s32[]{:S(2)}) async-start(), calls=%async_computation.50 | async-start | bytes 10616832 | tf_op jit(solution)/shard_map/reduce_scatter | solution.py:474
  3309.1 938.9 %all-reduce.13.cloned.1.call-start = ((), (), s32[]{:S(2)}) async-start(), calls=%async_computation.67 | async-start | bytes 56623104
  3460.9 933.5 %reduce-scatter.67.cloned.1.call-start = ((), (), s32[]{:S(2)}) async-start(), calls=%async_computation.49 | async-start | bytes 15925248 | tf_op jit(solution)/shard_map/reduce_scatter | solution.py:465
  3478.1 1061.1 %reduce-scatter.65.cloned.1.call-start = ((), (), s32[]{:S(2)}) async-start(), calls=%async_computation.48 | async-start | bytes 15925248 | tf_op jit(solution)/shard_map/reduce_scatter | solution.py:465
  (221 other events, 9022.0 us)
Sparse Core Ops, SparseCore 0:
  11.7 132.3 all-gather.44
  146.2 69.3 all-gather.46
  430.5 70.0 reduce-scatter.32
  502.6 90.6 all-gather.50
  666.4 90.6 all-gather.52
  788.6 129.5 all-gather.54
  1022.6 71.1 all-gather.56
  1308.2 70.0 reduce-scatter.40
  1379.8 90.7 all-gather.60
  1543.4 90.6 all-gather.62
  1745.8 80.5 reduce-scatter.48
  1829.4 70.0 reduce-scatter.42
  1963.6 71.9 all-gather.38
  2373.2 70.0 reduce-scatter.52
  2454.8 70.0 all-gather.40
  2565.6 77.8 reduce-scatter.54
  2677.1 73.1 all-gather.42
  3114.8 70.0 reduce-scatter.60
  3298.1 195.2 all-reduce.10
  3495.7 99.5 reduce-scatter.70
  3597.6 97.8 reduce-scatter.68
  3699.8 548.1 all-reduce.12
  4250.2 144.1 reduce-scatter.66
  4396.7 142.4 reduce-scatter.64
  (20 shorter events, 789.5 us)
where the time goes:
time: 4570 us; the launch traced here: 4550 us
  waiting for transfers between devices  2580 us (56%)
  matrix products  1170 us (26%)
  local copies, waits for them, and re-layouts  321 us (7%)
  other arithmetic  290 us (6%)
  blocking collectives  168 us (4%)
    unnamed x50, waiting for transfers between devices  540 us
    reduce_scatter x2, waiting for transfers between devices, on_device(): lax.psum_scatter(grad_mod.astype(jnp.bfloat16), 'dp', scatter_dimension=1...  272 us
    all_gather x4, waiting for transfers between devices, spread_rows(): lax.all_gather(streams_pair[0], 'mp', axis=0, tiled=True)  267 us
    reduce_scatter x4, waiting for transfers between devices, collect_rows(): lax.psum_scatter(streams_pair[0].astype(jnp.bfloat16), 'mp', scatter_dime...  254 us
    all_gather x4, waiting for transfers between devices, spread_grads(): lax.all_gather(streams_pair[0], 'mp', axis=0, tiled=True)  235 us
    all_gather x2, waiting for transfers between devices, on_device(): lax.all_gather(whole_block[0], 'dp', axis=1, tiled=True)  233 us
    reduce_scatter x2, waiting for transfers between devices, on_device(): lax.psum_scatter(four_grads[2].astype(jnp.bfloat16), 'dp', scatter_dimens...  196 us
    dot_general x4, matrix products, attend_back(): jnp.einsum('hqk,qhd->khd', grad_raw, parts[0], preferred_element_type=jnp...  184 us
  transfers between devices with their start and end apart: 44, of which 33 were waited for; matrix products, arithmetic and copies ran while one was open for 23% of the time, Pallas kernels for 0%

commit v1 on v0

v1 whole, which is shorter than its diff:
```python
import functools
import math

import jax
import jax.numpy as jnp
from jax import lax
from jax.experimental import pallas as pl
from jax.experimental.pallas import tpu as pltpu
from jax.sharding import PartitionSpec as P

HEAD_DIM = 64
LAYERS = 2
EPSILON = 1e-06
LOW = jnp.bfloat16
F32 = jnp.float32
PAIR=128
NT=(((1,),(1,)),((),()))
TN=(((0,),(0,)),((),()))
NN=(((1,),(0,)),((),()))
def dot(a,b,dims):
    return lax.dot_general(a,b,dims,preferred_element_type=jnp.float32)

def attn_fwd_kernel(scale,qb,mask_ref,qi,ki,vi,qt,kt,vt,oi,ot,li,lt):
    low = lax.broadcasted_iota(jnp.int32,(1,PAIR),1)<HEAD_DIM
    live = mask_ref[0:1,:]>0
    k_img,k_txt,v_img,v_txt=ki[...],kt[...],vi[...],vt[...]
    def block(q,store):
        q=q*jnp.asarray(scale,q.dtype)
        outs=[];lses=[]
        for h in range(2):
            keep = low if h==0 else jnp.logical_not(low)
            qm=jnp.where(keep,q,jnp.zeros_like(q))
            si=dot(qm,k_img,NT); st=jnp.where(live,dot(qm,k_txt,NT),-1e30)
            m=jnp.maximum(jnp.max(si,axis=-1,keepdims=True),jnp.max(st,axis=-1,keepdims=True))
            pi=jnp.exp(si-m); pt=jnp.exp(st-m)
            l=jnp.sum(pi,axis=-1,keepdims=True)+jnp.sum(pt,axis=-1,keepdims=True)
            o=dot(pi.astype(jnp.bfloat16),v_img,NN)+dot(pt.astype(jnp.bfloat16),v_txt,NN)
            outs.append(o/l); lses.append(m+jnp.log(l))
        store(jnp.where(low,outs[0],outs[1]).astype(jnp.bfloat16), jnp.where(low,lses[0],lses[1]))
    nb=qi.shape[0]//qb
    def body(b,c):
        r=pl.ds(pl.multiple_of(b*qb,qb),qb)
        def store(o,l):
            oi[r,:]=o; li[r,:]=l
        block(qi[r,:],store)
        return c
    lax.fori_loop(0,nb,body,0)
    def store(o,l):
        ot[...]=o; lt[...]=l
    block(qt[...],store)

def attn_fwd(img,txt,mask,qb=256):
    ri,c3=img.shape; rt=txt.shape[0]; c=c3//3; np_=c//PAIR
    spec=lambda r,off: pl.BlockSpec((r,PAIR),lambda j,off=off:(0,j+off*np_))
    f=pl.pallas_call(functools.partial(attn_fwd_kernel,HEAD_DIM**-0.5,qb),
        grid=(np_,),
        in_specs=[pl.BlockSpec((8,rt),lambda j:(0,0))]+[spec(ri,o) for o in range(3)]+[spec(rt,o) for o in range(3)],
        out_specs=[spec(ri,0),spec(rt,0),spec(ri,0),spec(rt,0)],
        out_shape=[jax.ShapeDtypeStruct((ri,c),jnp.bfloat16),jax.ShapeDtypeStruct((rt,c),jnp.bfloat16),
                   jax.ShapeDtypeStruct((ri,c),jnp.float32),jax.ShapeDtypeStruct((rt,c),jnp.float32)],
        compiler_params=pltpu.CompilerParams(vmem_limit_bytes=56<<20),
        cost_estimate=pl.CostEstimate(flops=4*(ri+rt)**2*c,bytes_accessed=(ri+rt)*c*12,transcendentals=(ri+rt)**2*c//HEAD_DIM),
        name="attn_fwd")
    return f(mask,img,img,img,txt,txt,txt)

def attn_bwd_kernel(scale,qb,mask_ref,qi,ki,vi,qt,kt,vt,oi,ot,li,lt,gi,gt,dqi,dki,dvi,dqt,dkt,dvt,aki,avi,akt,avt):
    low = lax.broadcasted_iota(jnp.int32,(1,PAIR),1)<HEAD_DIM
    live = mask_ref[:,0:1]>0
    k_img,k_txt,v_img,v_txt=ki[...],kt[...],vi[...],vt[...]
    for a in (aki,avi,akt,avt): a[...]=jnp.zeros_like(a)
    keeps=[low,jnp.logical_not(low)]
    kim=[jnp.where(k,k_img,jnp.zeros_like(k_img)) for k in keeps]
    ktm=[jnp.where(k,k_txt,jnp.zeros_like(k_txt)) for k in keeps]
    def block(q,o,l,g,store):
        q=q*jnp.asarray(scale,q.dtype)
        lT=l.T
        dT=(g.astype(jnp.float32)*o.astype(jnp.float32)).T
        dq=None
        for h in range(2):
            qm=jnp.where(keeps[h],q,jnp.zeros_like(q)); gm=jnp.where(keeps[h],g,jnp.zeros_like(g))
            lr=lT[h*HEAD_DIM:h*HEAD_DIM+1,:]
            dr=jnp.sum(dT[h*HEAD_DIM:(h+1)*HEAD_DIM,:],axis=0,keepdims=True)
            pi=jnp.exp(dot(k_img,qm,NT)-lr)
            pt=jnp.exp(jnp.where(live,dot(k_txt,qm,NT),-1e30)-lr)
            avi[...]+=dot(pi.astype(jnp.bfloat16),gm,NN)
            avt[...]+=dot(pt.astype(jnp.bfloat16),gm,NN)
            si=(pi*(dot(v_img,gm,NT)-dr)).astype(jnp.bfloat16)
            st=(pt*(dot(v_txt,gm,NT)-dr)).astype(jnp.bfloat16)
            aki[...]+=dot(si,qm,NN)
            akt[...]+=dot(st,qm,NN)
            d=dot(si,kim[h],TN)+dot(st,ktm[h],TN)
            dq=d if dq is None else dq+d
        store((dq*scale).astype(jnp.bfloat16))
    nb=qi.shape[0]//qb
    def body(b,c):
        r=pl.ds(pl.multiple_of(b*qb,qb),qb)
        def store(v): dqi[r,:]=v
        block(qi[r,:],oi[r,:],li[r,:],gi[r,:],store)
        return c
    lax.fori_loop(0,nb,body,0)
    def store(v): dqt[...]=v
    block(qt[...],ot[...],lt[...],gt[...],store)
    dki[...]=aki[...].astype(jnp.bfloat16); dvi[...]=avi[...].astype(jnp.bfloat16)
    dkt[...]=akt[...].astype(jnp.bfloat16); dvt[...]=avt[...].astype(jnp.bfloat16)

def attn_bwd(img,txt,mask,oi,ot,li,lt,gi,gt,qb=256):
    ri,c3=img.shape; rt=txt.shape[0]; c=c3//3; np_=c//PAIR
    spec=lambda r,off=0: pl.BlockSpec((r,PAIR),lambda j,off=off:(0,j+off*np_))
    f=pl.pallas_call(functools.partial(attn_bwd_kernel,HEAD_DIM**-0.5,qb),
        grid=(np_,),
        in_specs=[pl.BlockSpec((rt,128),lambda j:(0,0))]+[spec(ri,o) for o in range(3)]+[spec(rt,o) for o in range(3)]
            +[spec(ri),spec(rt)]*3,
        out_specs=[spec(ri)]*3+[spec(rt)]*3,
        out_shape=[jax.ShapeDtypeStruct((ri,c),jnp.bfloat16)]*3+[jax.ShapeDtypeStruct((rt,c),jnp.bfloat16)]*3,
        scratch_shapes=[pltpu.VMEM((ri,PAIR),jnp.float32)]*2+[pltpu.VMEM((rt,PAIR),jnp.float32)]*2,
        compiler_params=pltpu.CompilerParams(vmem_limit_bytes=56<<20),
        cost_estimate=pl.CostEstimate(flops=10*(ri+rt)**2*c,bytes_accessed=(ri+rt)*c*26,transcendentals=(ri+rt)**2*c//HEAD_DIM),
        name="attn_bwd")
    return f(mask,img,img,img,txt,txt,txt,oi,ot,li,lt,gi,gt)


def attention(img, txt, mask):
    c = img.shape[1] // 3
    pad = -c % PAIR
    if pad:
        img, txt = (jnp.pad(a.reshape(-1, 3, c), ((0, 0), (0, 0), (0, pad))).reshape(-1, 3 * (c + pad)) for a in (img, txt))
    mask_rows = jnp.broadcast_to(mask[None, :], (8, mask.shape[0]))
    oi, ot, li, lt = attn_fwd(img, txt, mask_rows, query_block(img.shape[0]))
    return (oi[:, :c], ot[:, :c]), (img, txt, oi, ot, li, lt)


def attention_back(kept, mask, grads):
    img, txt, oi, ot, li, lt = kept
    c = grads[0].shape[1]
    pad = oi.shape[1] - c
    gi, gt = (jnp.pad(g, ((0, 0), (0, pad))) for g in grads) if pad else grads
    mask_columns = jnp.broadcast_to(mask[:, None], (mask.shape[0], 128))
    out = attn_bwd(img, txt, mask_columns, oi, ot, li, lt, gi, gt, query_block(img.shape[0]))
    return tuple(jnp.concatenate([piece[:, :c] for piece in part], axis=1) for part in (out[:3], out[3:]))


def query_block(rows):
    return 256 if rows % 256 == 0 else rows


def conditioning(steps, width):
    half = width // 2
    frequency = jnp.exp(-math.log(10000.0) * jnp.arange(half, dtype=F32) / half)
    phases = steps.astype(F32)[..., None] * frequency
    embedded = jnp.concatenate([jnp.cos(phases), jnp.sin(phases)], axis=-1)
    return embedded / (1.0 + jnp.exp(-embedded))


def gelu(v):
    return 0.5 * v * (1.0 + jnp.tanh(0.7978845608028654 * (v + 0.044715 * v * v * v)))


def gelu_slope(v):
    inner = jnp.tanh(0.7978845608028654 * (v + 0.044715 * v * v * v))
    return 0.5 * (1.0 + inner) + 0.5 * v * (1.0 - inner * inner) * 0.7978845608028654 * (1.0 + 0.134145 * v * v)


def normed(v):
    centred = v - jnp.mean(v, axis=-1, keepdims=True)
    r = lax.rsqrt(jnp.mean(centred * centred, axis=-1, keepdims=True) + EPSILON)
    return centred * r, r


def norm_back(v, e):
    n, r = normed(v)
    return r * (e - jnp.mean(e, axis=-1, keepdims=True) - n * jnp.mean(e * n, axis=-1, keepdims=True)), n


def matmul(a, b, dims):
    return lax.dot_general(a, b, (dims, ((), ())), preferred_element_type=F32)


class Ring:
    def __init__(self, size):
        self.size = size
        half = size // 2
        self.order = list(range(half)) + list(range(size - 1, half - 1, -1))
        self.up = [(self.order[i], self.order[(i + 1) % size]) for i in range(size)]
        self.down = [(self.order[i], self.order[(i - 1) % size]) for i in range(size)]

    def offsets(self):
        out = [0]
        for t in range(1, self.size // 2):
            out += [-t, t]
        return out + [self.size // 2]

    def owners(self):
        place = {device: i for i, device in enumerate(self.order)}
        return [
            [self.order[(place[device] + offset) % self.size] for offset in self.offsets()]
            for device in range(self.size)
        ]

    def gather(self, x):
        cut = x.shape[0] // 16 * 8
        blocks, a, b = [x], x, x
        for _ in range(1, self.size // 2):
            a = lax.ppermute(a, "mp", self.up)
            b = lax.ppermute(b, "mp", self.down)
            blocks += [a, b]
        first = lax.ppermute(a[:cut], "mp", self.up)
        second = lax.ppermute(b[cut:], "mp", self.down)
        return blocks + [jnp.concatenate([first, second], axis=0)]

    def scatter(self, blocks):
        far = blocks[-1]
        cut = far.shape[0] // 16 * 8
        up = lax.ppermute(far[:cut], "mp", self.up)
        down = lax.ppermute(far[cut:], "mp", self.down)
        half = self.size // 2
        for t in range(half - 1, 0, -1):
            ahead, behind = blocks[2 * t], blocks[2 * t - 1]
            if t == half - 1:
                ahead = jnp.concatenate([add_low(ahead[:cut], up), ahead[cut:]], axis=0)
                behind = jnp.concatenate([behind[:cut], add_low(behind[cut:], down)], axis=0)
            else:
                ahead, behind = add_low(ahead, up), add_low(behind, down)
            up = lax.ppermute(ahead, "mp", self.up)
            down = lax.ppermute(behind, "mp", self.down)
        if half == 1:
            return blocks[0].astype(F32) + jnp.concatenate([up, down], axis=0).astype(F32)
        return blocks[0].astype(F32) + up.astype(F32) + down.astype(F32)


def add_low(a, b):
    return (a.astype(F32) + b.astype(F32)).astype(LOW)


class Step:
    def __init__(self, ring, image_rows, text_rows, keep):
        self.ring, self.image_rows, self.text_rows, self.keep = ring, image_rows, text_rows, keep

    def pick(self, modulation, member):
        return jnp.where(self.keep, modulation[0, member][None, :], modulation[1, member][None, :])

    def gather(self, x):
        blocks = self.ring.gather(x)
        r = self.image_rows
        return (
            jnp.concatenate([block[:r] for block in blocks], axis=0),
            jnp.concatenate([block[r:] for block in blocks], axis=0),
        )

    def scatter(self, parts):
        r, t = self.image_rows, self.text_rows
        return self.ring.scatter(
            [
                jnp.concatenate([parts[0][k * r : k * r + r], parts[1][k * t : k * t + t]], axis=0)
                for k in range(self.ring.size)
            ]
        )

    def forward(self, x, modulation, weights, mask):
        qkv, out, up, down = weights
        n1 = normed(x)[0] * (1.0 + self.pick(modulation, 1)) + self.pick(modulation, 0)
        rows1 = self.gather(n1.astype(LOW))
        proj = [matmul(rows1[s], qkv[s], ((1,), (0,))).astype(LOW) for s in range(2)]
        mixture, kept = attention(proj[0], proj[1], mask)
        branch1 = self.scatter([matmul(mixture[s], out[s], ((1,), (1,))).astype(LOW) for s in range(2)])
        middle = x + self.pick(modulation, 2) * branch1
        n2 = normed(middle)[0] * (1.0 + self.pick(modulation, 4)) + self.pick(modulation, 3)
        rows2 = self.gather(n2.astype(LOW))
        pre = [matmul(rows2[s], up[s], ((1,), (0,))) for s in range(2)]
        act = [gelu(pre[s]).astype(LOW) for s in range(2)]
        branch2 = self.scatter([matmul(act[s], down[s], ((1,), (1,))).astype(LOW) for s in range(2)])
        y = middle + self.pick(modulation, 5) * branch2
        return y, (x, modulation, rows1, kept, mixture, branch1, middle, rows2, pre, act, branch2)

    def sums(self, v):
        r = self.image_rows
        return jnp.stack([jnp.sum(v[:r], axis=0), jnp.sum(v[r:], axis=0)])

    def backward_mlp(self, g, saved, weights):
        qkv, out, up, down = weights
        x, modulation, rows1, kept, mixture, branch1, middle, rows2, pre, act, branch2 = saved
        db2 = self.gather((self.pick(modulation, 5) * g).astype(LOW))
        grad_act = [matmul(db2[s], down[s], ((1,), (0,))) for s in range(2)]
        d_pre = [(grad_act[s] * gelu_slope(pre[s])).astype(LOW) for s in range(2)]
        dn2 = self.scatter([matmul(d_pre[s], up[s], ((1,), (1,))).astype(LOW) for s in range(2)])
        inner, n = norm_back(middle, dn2 * (1.0 + self.pick(modulation, 4)))
        d_middle = g + inner
        mods = [self.sums(dn2), self.sums(dn2 * n), self.sums(g * branch2)]
        grads_down = [matmul(db2[s], act[s], ((0,), (0,))) for s in range(2)]
        grads_up = [matmul(rows2[s], d_pre[s], ((0,), (0,))) for s in range(2)]
        return d_middle, mods, grads_up, grads_down

    def backward_attention(self, d_middle, saved, weights, mask):
        qkv, out, up, down = weights
        x, modulation, rows1, kept, mixture, branch1, middle, rows2, pre, act, branch2 = saved
        db1 = self.gather((self.pick(modulation, 2) * d_middle).astype(LOW))
        d_mixture = [matmul(db1[s], out[s], ((1,), (0,))).astype(LOW) for s in range(2)]
        d_proj = attention_back(kept, mask, d_mixture)
        dn1 = self.scatter([matmul(d_proj[s], qkv[s], ((1,), (1,))).astype(LOW) for s in range(2)])
        inner, n = norm_back(x, dn1 * (1.0 + self.pick(modulation, 1)))
        mods = [self.sums(dn1), self.sums(dn1 * n), self.sums(d_middle * branch1)]
        grads_out = [matmul(db1[s], mixture[s], ((0,), (0,))) for s in range(2)]
        grads_qkv = [matmul(rows1[s], d_proj[s], ((0,), (0,))) for s in range(2)]
        return d_middle + inner, mods, grads_qkv, grads_out


def gather_weight(w):
    return lax.all_gather(w, "dp", axis=1, tiled=True)


def reduce_weight(parts):
    total = jnp.stack([sum(part[s] for part in parts).astype(LOW) for s in range(2)])
    return lax.psum_scatter(total, "dp", scatter_dimension=1, tiled=True).astype(F32)


def device_program(
    mp_size,
    image_input,
    text_input,
    timesteps,
    key_mask,
    mod_weight,
    qkv_weight,
    out_weight,
    up_weight,
    down_weight,
    image_cotangent,
    text_cotangent,
):
    seqs = key_mask.shape[0]
    assert seqs == 2
    width = image_input.shape[1]
    ring = Ring(mp_size)
    half = mp_size // 2
    side = lax.axis_index("mp") // half
    swap = [(i, (i + half) % mp_size) for i in range(mp_size)]
    ri, rt = image_input.shape[0] // 2, text_input.shape[0] // 2
    here = side == 0

    def deal(image, text):
        pieces = [jnp.concatenate([image[p * ri : p * ri + ri], text[p * rt : p * rt + rt]], axis=0) for p in range(2)]
        got = lax.ppermute(jnp.where(here, pieces[1], pieces[0]), "mp", swap)
        return [jnp.where(here, pieces[0], got).astype(F32), jnp.where(here, got, pieces[1]).astype(F32)]

    def undeal(rows):
        got = lax.ppermute(jnp.where(here, rows[1], rows[0]), "mp", swap)
        pieces = [jnp.where(here, rows[0], got), jnp.where(here, got, rows[1])]
        return (
            jnp.concatenate([piece[:ri] for piece in pieces], axis=0),
            jnp.concatenate([piece[ri:] for piece in pieces], axis=0),
        )

    condition = conditioning(timesteps, width).astype(LOW)
    depth = mod_weight.shape[2]
    own_condition = lax.dynamic_slice_in_dim(condition, lax.axis_index("dp") * depth, depth, axis=1)
    partial = jnp.einsum("nd,lsdkc->nlskc", own_condition, mod_weight, preferred_element_type=F32)
    own_mod = lax.psum_scatter(partial, "dp", scatter_dimension=0, tiled=True)
    modulation = lax.all_gather(own_mod, "mp", axis=4, tiled=True)

    owners = jnp.array(ring.owners(), dtype=jnp.int32)[lax.axis_index("mp")]
    segments = (owners % half) * 2 + owners // half
    masks = jnp.take(key_mask.reshape(seqs, mp_size, rt), segments, axis=1).reshape(seqs, -1)

    weights = []
    for l in range(LAYERS):
        weights.append(
            (
                gather_weight(jnp.swapaxes(qkv_weight[l], 1, 2).reshape(2, qkv_weight.shape[3], -1)),
                gather_weight(jnp.swapaxes(out_weight[l], 1, 2)),
                gather_weight(up_weight[l]),
                gather_weight(jnp.swapaxes(down_weight[l], 1, 2)),
            )
        )

    keep = (jnp.arange(ri + rt) < ri)[:, None]
    step = Step(ring, ri, rt, keep)
    rows = deal(image_input, text_input)
    upstream = deal(image_cotangent, text_cotangent)
    saved = []
    for l in range(LAYERS):
        done = [step.forward(rows[s], modulation[s, l], weights[l], masks[s]) for s in range(seqs)]
        rows = [d[0] for d in done]
        saved.append([d[1] for d in done])
    image_output, text_output = undeal([row.astype(LOW) for row in rows])

    reduced, mod_rows = [], []
    for l in reversed(range(LAYERS)):
        mlp = [step.backward_mlp(upstream[s], saved[l][s], weights[l]) for s in range(seqs)]
        grad_down = reduce_weight([m[3] for m in mlp])
        grad_up = reduce_weight([m[2] for m in mlp])
        att = [step.backward_attention(mlp[s][0], saved[l][s], weights[l], masks[s]) for s in range(seqs)]
        grad_out = reduce_weight([a[3] for a in att])
        grad_qkv = reduce_weight([a[2] for a in att])
        upstream = [a[0] for a in att]
        mod_rows.insert(0, jnp.stack([jnp.stack(att[s][1] + mlp[s][1], axis=1) for s in range(seqs)]))
        reduced.insert(0, (grad_qkv, grad_out, grad_up, grad_down))
    image_grad, text_grad = undeal(upstream)

    mod_sums = lax.psum_scatter(jnp.stack(mod_rows, axis=1), "mp", scatter_dimension=4, tiled=True)
    all_mods = lax.all_gather(mod_sums, "dp", axis=0, tiled=True)
    grad_mod = jnp.einsum("nd,nlskc->lsdkc", own_condition.astype(F32), all_mods, precision=lax.Precision.HIGHEST)
    columns = qkv_weight.shape[4]
    grad_qkv = jnp.stack(
        [jnp.swapaxes(r[0].reshape(2, -1, 3, columns), 1, 2) for r in reduced]
    )
    return (
        image_output,
        text_output,
        image_grad,
        text_grad,
        grad_mod,
        grad_qkv,
        jnp.stack([jnp.swapaxes(r[1], 1, 2) for r in reduced]),
        jnp.stack([r[2] for r in reduced]),
        jnp.stack([jnp.swapaxes(r[3], 1, 2) for r in reduced]),
    )


def solution(mesh):
    rows = P(("dp", "mp"), None)
    grads = (
        P(None, None, "dp", None, "mp"),
        P(None, None, None, "dp", "mp"),
        P(None, None, "mp", "dp"),
        P(None, None, "dp", "mp"),
        P(None, None, "mp", "dp"),
    )
    return jax.shard_map(
        functools.partial(device_program, mesh.shape["mp"]),
        mesh=mesh,
        in_specs=(rows, rows, P(), P("dp", None)) + grads + (rows, rows),
        out_specs=(rows, rows, rows, rows) + grads,
        check_vma=False,
    )
```

time: 4570 us -> 2430 us (0.53)
  waiting for transfers between devices: 2580 us -> 1180 us
  matrix products: 1170 us -> 481 us
  Pallas kernels: 0 us -> 224 us
  other arithmetic: 290 us -> 142 us
  starting transfers between devices: 4.44 us -> 147 us
  blocking collectives: 168 us -> 27.9 us
  local copies, waits for them, and re-layouts: 321 us -> 200 us
    all_gather x18 -> x8, waiting for transfers between devices: 1110 us -> 113 us  [gather_weight(): return lax.all_gather(w, 'dp', axis=1, tiled=True)]
    dot_general x92 -> x98, matrix products: 1170 us -> 481 us  [the longest x96 474 us: matmul(): return lax.dot_general(a, b, (dims, ((), ())), preferred_element_type=F32)]
    ppermute x0 -> x132, waiting for transfers between devices: none -> 624 us  [the longest x16 204 us: gather(): b = lax.ppermute(b, 'mp', self.down)]
    reduce_scatter x20 -> x8, waiting for transfers between devices: 929 us -> 400 us  [reduce_weight(): lax.psum_scatter(total, 'dp', scatter_dimension=1, tiled=True).astype(F32)]
    unnamed x50 -> x20, waiting for transfers between devices: 540 us -> 42.7 us
    pallas_call x0 -> x8, Pallas kernels: none -> 224 us  [the longest x4 135 us: attn_bwd(): return f(mask, img, img, img, txt, txt, txt, oi, ot, li, lt, gi, gt)]
    ppermute x0 -> x132, starting transfers between devices: none -> 144 us  [the longest x16 18.7 us: gather(): second = lax.ppermute(b[cut:], 'mp', self.down)]
    all_gather x12 -> x2, blocking collectives: 168 us -> 27.9 us  [the longest x1 17.6 us: device_program(): all_mods = lax.all_gather(mod_sums, 'dp', axis=0, tiled=True)]
  transfers between devices with their start and end apart: 44 -> 150, of which waited for: 33 -> 85; matrix products, arithmetic and copies ran while one was open for 23% -> 25% of each run, Pallas kernels for 0% -> 6%
where the time goes in v1:
time: 2430 us
  waiting for transfers between devices  1180 us (49%)
  matrix products  481 us (20%)
  Pallas kernels  224 us (9%)
  local copies, waits for them, and re-layouts  200 us (8%)
  starting transfers between devices  147 us (6%)
  other arithmetic  142 us (6%)
  blocking collectives  27.9 us (1%)
  between operations  25 us (1%)
    dot_general x96, matrix products, matmul(): return lax.dot_general(a, b, (dims, ((), ())), preferred_element_type=F32)  474 us
    reduce_scatter x8, waiting for transfers between devices, reduce_weight(): lax.psum_scatter(total, 'dp', scatter_dimension=1, tiled=True).astype(F32)  400 us
    ppermute x16, waiting for transfers between devices, gather(): b = lax.ppermute(b, 'mp', self.down)  204 us
    ppermute x16, waiting for transfers between devices, scatter(): up = lax.ppermute(ahead, 'mp', self.up)  197 us
    pallas_call x4, Pallas kernels, attn_bwd(): return f(mask, img, img, img, txt, txt, txt, oi, ot, li, lt, gi, gt)  135 us
    all_gather x8, waiting for transfers between devices, gather_weight(): return lax.all_gather(w, 'dp', axis=1, tiled=True)  113 us
    unnamed x1195, local copies, waits for them, and re-layouts  95.8 us
    ppermute x16, waiting for transfers between devices, scatter(): up = lax.ppermute(far[:cut], 'mp', self.up)  91.8 us
  transfers between devices with their start and end apart: 150, of which 85 were waited for; matrix products, arithmetic and copies ran while one was open for 25% of the time, Pallas kernels for 6%

profile of v1, /device:TPU:0, one launch (start us, length us, event | category | flops | bytes accessed | tf_op | source)
XLA Modules:
  0.0 2425.6 jit_solution(5433550753327942316)
XLA Ops:
  28.2 42.4 %all-reduce.3.cloned.1.call-done = f32[16,2,2,6,384]{4,0,3,2,1:T(8,128)} async-done(((f32[16,2,2,6,384]{4,0,3,2,1:T(8,128)}), f32[16,2,2,6,384]{4,0,3,2,1:T(8,128)}) %all-reduce.3.cloned.1.call-update) | async-done | bytes 589840
  122.5 20.6 all-gather.11.cloned.1.call-done
  154.8 22.2 attn_fwd.6
  196.4 18.4 collective-permute-done.38
  278.0 80.0 %all-gather.15.cloned.1.call-done = bf16[2,1536,1536]{2,1,0:T(8,128)(2,1)} async-done(((bf16[2,192,1536]{2,1,0:T(8,128)(2,1)}), bf16[2,1536,1536]{2,1,0:T(8,128)(2,1)}) %all-gather.15.cloned.1.call-update) | async-done | bytes 9437200 | tf_op jit(solution)/shard_map/all_gather | solution.py:307
  414.0 18.8 collective-permute-done.50
  456.8 22.3 attn_fwd.7
  557.5 22.4 attn_fwd.4
  750.5 22.4 attn_fwd.5
  819.4 18.9 collective-permute-done.26
  949.6 19.5 collective-permute-done.62
  1151.3 18.5 collective-permute-done.76
  1188.3 33.7 %attn_bwd.4 = (bf16[1024,384]{1,0:T(8,128)(2,1)}, bf16[1024,384]{1,0:T(8,128)(2,1)}, bf16[1024,384]{1,0:T(8,128)(2,1)}, bf16[160,384]{1,0:T(8,128)(2,1)}, bf16[1...) custom-call(s32[160,128]{1,0:T(8,128)} %broadcast_in_dim.809.mask_ref, ...), custom_call_target="tpu_custom_call" | custom-call | flops 5383127040 | bytes 11821056 | tf_op jit(solution)/shard_map/attn_bwd/pallas_call | solution.py:119
  1241.4 33.8 %attn_bwd.6 = (bf16[1024,384]{1,0:T(8,128)(2,1)}, bf16[1024,384]{1,0:T(8,128)(2,1)}, bf16[1024,384]{1,0:T(8,128)(2,1)}, bf16[160,384]{1,0:T(8,128)(2,1)}, bf16[1...) custom-call(s32[160,128]{1,0:T(8,128)} %broadcast_in_dim.810.mask_ref, ...), custom_call_target="tpu_custom_call" | custom-call | flops 5383127040 | bytes 11821056 | tf_op jit(solution)/shard_map/attn_bwd/pallas_call | solution.py:119
  1360.2 18.4 collective-permute-done.84
  1531.9 18.5 collective-permute-done.92
  1566.8 33.6 %attn_bwd.5 = (bf16[1024,384]{1,0:T(8,128)(2,1)}, bf16[1024,384]{1,0:T(8,128)(2,1)}, bf16[1024,384]{1,0:T(8,128)(2,1)}, bf16[160,384]{1,0:T(8,128)(2,1)}, bf16[1...) custom-call(s32[160,128]{1,0:T(8,128)} %broadcast_in_dim.809.mask_ref, ...), custom_call_target="tpu_custom_call" | custom-call | flops 5383127040 | bytes 11821056 | tf_op jit(solution)/shard_map/attn_bwd/pallas_call | solution.py:119
  1618.3 33.8 %attn_bwd.7 = (bf16[1024,384]{1,0:T(8,128)(2,1)}, bf16[1024,384]{1,0:T(8,128)(2,1)}, bf16[1024,384]{1,0:T(8,128)(2,1)}, bf16[160,384]{1,0:T(8,128)(2,1)}, bf16[1...) custom-call(s32[160,128]{1,0:T(8,128)} %broadcast_in_dim.810.mask_ref, ...), custom_call_target="tpu_custom_call" | custom-call | flops 5383127040 | bytes 11821056 | tf_op jit(solution)/shard_map/attn_bwd/pallas_call | solution.py:119
  1712.9 20.2 copy.60
  1733.1 19.4 reshape.404
  2019.7 94.3 %reduce-scatter.27.cloned.1.call-done = bf16[2,192,1536]{2,1,0:T(8,128)(2,1)} async-done(((bf16[2,1536,1536]{2,1,0:T(8,128)(2,1)}), bf16[2,192,1536]{2,1,0:T(8,128)(2,1)}) %reduce-scatter.27.cloned.1.call-update) | async-done | bytes 1179664 | tf_op jit(solution)/shard_map/reduce_scatter | solution.py:312
  2114.0 100.1 %reduce-scatter.25.cloned.1.call-done = bf16[2,192,1536]{2,1,0:T(8,128)(2,1)} async-done(((bf16[2,1536,1536]{2,1,0:T(8,128)(2,1)}), bf16[2,192,1536]{2,1,0:T(8,128)(2,1)}) %reduce-scatter.25.cloned.1.call-update) | async-done | bytes 1179664 | tf_op jit(solution)/shard_map/reduce_scatter | solution.py:312
  2218.2 96.0 %reduce-scatter.23.cloned.1.call-done = bf16[2,192,1536]{2,1,0:T(8,128)(2,1)} async-done(((bf16[2,1536,1536]{2,1,0:T(8,128)(2,1)}), bf16[2,192,1536]{2,1,0:T(8,128)(2,1)}) %reduce-scatter.23.cloned.1.call-update) | async-done | bytes 1179664 | tf_op jit(solution)/shard_map/reduce_scatter | solution.py:312
  2314.1 100.1 %reduce-scatter.21.cloned.1.call-done = bf16[2,192,1536]{2,1,0:T(8,128)(2,1)} async-done(((bf16[2,1536,1536]{2,1,0:T(8,128)(2,1)}), bf16[2,192,1536]{2,1,0:T(8,128)(2,1)}) %reduce-scatter.21.cloned.1.call-update) | async-done | bytes 1179664 | tf_op jit(solution)/shard_map/reduce_scatter | solution.py:312
  (2149 shorter events, 1472.4 us)
Async XLA Ops:
  7.2 63.4 %all-reduce.3.cloned.1.call-start = ((), (), s32[]{:S(2)}) async-start(), calls=%async_computation.26 | async-start | bytes 1179648
  10.7 132.3 %all-gather.11.cloned.1.call-start = ((), (), s32[]{:S(2)}) async-start(), calls=%async_computation.9 | async-start | bytes 7962624 | tf_op jit(solution)/shard_map/all_gather | solution.py:307
  13.5 163.6 %all-gather.13.cloned.1.call-start = ((), (), s32[]{:S(2)}) async-start(), calls=%async_computation.10 | async-start | bytes 2654208 | tf_op jit(solution)/shard_map/all_gather | solution.py:307
  14.4 252.3 %all-gather.23.cloned.1.call-start = ((), (), s32[]{:S(2)}) async-start(), calls=%async_computation.23 | async-start | bytes 10616832 | tf_op jit(solution)/shard_map/all_gather | solution.py:307
  17.9 340.1 %all-gather.15.cloned.1.call-start = ((), (), s32[]{:S(2)}) async-start(), calls=%async_computation.11 | async-start | bytes 10616832 | tf_op jit(solution)/shard_map/all_gather | solution.py:307
  19.5 426.4 %all-gather.17.cloned.1.call-start = ((), (), s32[]{:S(2)}) async-start(), calls=%async_computation.12 | async-start | bytes 7962624 | tf_op jit(solution)/shard_map/all_gather | solution.py:307
  22.3 61.9 %collective-permute-start = (bf16[296,1536]{1,0:T(8,128)(2,1)}, bf16[296,1536]{1,0:T(8,128)(2,1)}, u32[]{:S(2)}, u32[]{:S(2)}) collective-permute-start(bf16[296,1536]{1,0:T(8,128)(2,1)} %broadcast_select_fusion.11), channel_id=1, source_target_pairs={{0,2},{1,3},{2,0},{3,1},{4,6},{5,7},{6,4},{7,5},{8,10},{9,11},{10,... | collective-permute-start | bytes 2727944 | tf_op jit(solution)/shard_map/ppermute | solution.py:341
  26.4 452.7 %all-gather.19.cloned.1.call-start = ((), (), s32[]{:S(2)}) async-start(), calls=%async_computation.13 | async-start | bytes 2654208 | tf_op jit(solution)/shard_map/all_gather | solution.py:307
  244.9 619.6 %all-gather.25.cloned.1.call-start = ((), (), s32[]{:S(2)}) async-start(), calls=%async_computation.24 | async-start | bytes 10616832 | tf_op jit(solution)/shard_map/all_gather | solution.py:307
  437.4 437.7 %all-gather.21.cloned.1.call-start = ((), (), s32[]{:S(2)}) async-start(), calls=%async_computation.14 | async-start | bytes 10616832 | tf_op jit(solution)/shard_map/all_gather | solution.py:307
  642.0 1317.9 %reduce-scatter.29.cloned.1.call-start = ((), (), s32[]{:S(2)}) async-start(), calls=%async_computation.25 | async-start | bytes 983040
  843.1 99.9 %collective-permute-start.66 = (bf16[296,1536]{1,0:T(8,128)(2,1)}, bf16[296,1536]{1,0:T(8,128)(2,1)}, u32[]{:S(2)}, u32[]{:S(2)}) collective-permute-start(bf16[296,1536]{1,0:T(8,128)(2,1)} %broadcast_select_fusion.5), channel_id=1, source_target_pairs={{0,2},{1,3},{2,0},{3,1},{4,6},{5,7},{6,4},{7,5},{8,10},{9,11},{10,... | collective-permute-start | bytes 2727944 | tf_op jit(solution)/shard_map/ppermute | solution.py:341
  1174.3 59.3 %collective-permute-start.110 = (bf16[152,1536]{1,0:T(8,128)(2,1)}, bf16[152,1536]{1,0:T(8,128)(2,1)}, u32[]{:S(2)}, u32[]{:S(2)}) collective-permute-start(bf16[152,1536]{1,0:T(8,128)(2,1)} %slice.2584), channel_id=1, source_target_pairs={{0,2},{1,0},{3,1},{2,3},{4,6},{5,4},{7,5},{6,7},{8,10},{9,8},{11,9... | collective-permute-start | bytes 1400840 | tf_op jit(solution)/shard_map/ppermute | solution.py:207
  1175.7 61.1 %collective-permute-start.109 = (bf16[144,1536]{1,0:T(8,128)(2,1)}, bf16[144,1536]{1,0:T(8,128)(2,1)}, u32[]{:S(2)}, u32[]{:S(2)}) collective-permute-start(bf16[144,1536]{1,0:T(8,128)(2,1)} %slice.2583), channel_id=1, source_target_pairs={{0,1},{1,3},{3,2},{2,0},{4,5},{5,7},{7,6},{6,4},{8,9},{9,11},{11,1... | collective-permute-start | bytes 1327112 | tf_op jit(solution)/shard_map/ppermute | solution.py:206
  1554.1 56.7 %collective-permute-start.126 = (bf16[152,1536]{1,0:T(8,128)(2,1)}, bf16[152,1536]{1,0:T(8,128)(2,1)}, u32[]{:S(2)}, u32[]{:S(2)}) collective-permute-start(bf16[152,1536]{1,0:T(8,128)(2,1)} %slice.2624), channel_id=1, source_target_pairs={{0,2},{1,0},{3,1},{2,3},{4,6},{5,4},{7,5},{6,7},{8,10},{9,8},{11,9... | collective-permute-start | bytes 1400840 | tf_op jit(solution)/shard_map/ppermute | solution.py:207
  1556.0 58.4 %collective-permute-start.125 = (bf16[144,1536]{1,0:T(8,128)(2,1)}, bf16[144,1536]{1,0:T(8,128)(2,1)}, u32[]{:S(2)}, u32[]{:S(2)}) collective-permute-start(bf16[144,1536]{1,0:T(8,128)(2,1)} %slice.2623), channel_id=1, source_target_pairs={{0,1},{1,3},{3,2},{2,0},{4,5},{5,7},{7,6},{6,4},{8,9},{9,11},{11,1... | collective-permute-start | bytes 1327112 | tf_op jit(solution)/shard_map/ppermute | solution.py:206
  1752.5 247.3 %reduce-scatter.19.cloned.1.call-start = ((), (), s32[]{:S(2)}) async-start(), calls=%async_computation.18 | async-start | bytes 2654208 | tf_op jit(solution)/shard_map/reduce_scatter | solution.py:312
  1756.8 243.1 %reduce-scatter.17.cloned.1.call-start = ((), (), s32[]{:S(2)}) async-start(), calls=%async_computation.17 | async-start | bytes 2654208 | tf_op jit(solution)/shard_map/reduce_scatter | solution.py:312
  1767.8 234.2 %reduce-scatter.15.cloned.1.call-start = ((), (), s32[]{:S(2)}) async-start(), calls=%async_computation.16 | async-start | bytes 7962624 | tf_op jit(solution)/shard_map/reduce_scatter | solution.py:312
  1786.7 227.2 %reduce-scatter.13.cloned.1.call-start = ((), (), s32[]{:S(2)}) async-start(), calls=%async_computation.15 | async-start | bytes 7962624 | tf_op jit(solution)/shard_map/reduce_scatter | solution.py:312
  1806.6 307.4 %reduce-scatter.27.cloned.1.call-start = ((), (), s32[]{:S(2)}) async-start(), calls=%async_computation.22 | async-start | bytes 10616832 | tf_op jit(solution)/shard_map/reduce_scatter | solution.py:312
  1842.4 371.7 %reduce-scatter.25.cloned.1.call-start = ((), (), s32[]{:S(2)}) async-start(), calls=%async_computation.21 | async-start | bytes 10616832 | tf_op jit(solution)/shard_map/reduce_scatter | solution.py:312
  1878.9 435.2 %reduce-scatter.23.cloned.1.call-start = ((), (), s32[]{:S(2)}) async-start(), calls=%async_computation.20 | async-start | bytes 10616832 | tf_op jit(solution)/shard_map/reduce_scatter | solution.py:312
  1908.7 505.6 %reduce-scatter.21.cloned.1.call-start = ((), (), s32[]{:S(2)}) async-start(), calls=%async_computation.19 | async-start | bytes 10616832 | tf_op jit(solution)/shard_map/reduce_scatter | solution.py:312
  (712 other events, 11091.4 us)
Sparse Core Ops, SparseCore 0:
  10.9 59.6 all-reduce.2
  72.8 70.2 all-gather.10
  144.7 30.0 all-gather.12
  176.8 89.9 all-gather.22
  268.8 89.1 all-gather.14
  359.4 69.5 all-gather.16
  430.7 30.0 all-gather.18
  462.9 89.9 all-gather.24
  642.1 88.5 all-gather.20
  1752.6 22.8 reduce-scatter.28
  1777.8 37.0 reduce-scatter.18
  1817.1 35.8 reduce-scatter.16
  1855.3 75.9 reduce-scatter.14
  1933.5 80.3 reduce-scatter.12
  2016.0 97.8 reduce-scatter.26
  2116.1 97.8 reduce-scatter.24
  2216.2 97.8 reduce-scatter.22
  2316.3 97.8 reduce-scatter.20

commit v2 on v1

--- a/solution.py
+++ b/solution.py
@@ -7,6 +7,7 @@
 from jax.experimental import pallas as pl
 from jax.experimental.pallas import tpu as pltpu
 from jax.sharding import PartitionSpec as P
+
 
 HEAD_DIM = 64
 LAYERS = 2
@@ -17,13 +18,17 @@
 NT=(((1,),(1,)),((),()))
 TN=(((0,),(0,)),((),()))
 NN=(((1,),(0,)),((),()))
+
+
 def dot(a,b,dims):
     return lax.dot_general(a,b,dims,preferred_element_type=jnp.float32)
+
 
 def attn_fwd_kernel(scale,qb,mask_ref,qi,ki,vi,qt,kt,vt,oi,ot,li,lt):
     low = lax.broadcasted_iota(jnp.int32,(1,PAIR),1)<HEAD_DIM
     live = mask_ref[0:1,:]>0
     k_img,k_txt,v_img,v_txt=ki[...],kt[...],vi[...],vt[...]
+
     def block(q,store):
         q=q*jnp.asarray(scale,q.dtype)
         outs=[];lses=[]
@@ -37,17 +42,25 @@
             o=dot(pi.astype(jnp.bfloat16),v_img,NN)+dot(pt.astype(jnp.bfloat16),v_txt,NN)
             outs.append(o/l); lses.append(m+jnp.log(l))
         store(jnp.where(low,outs[0],outs[1]).astype(jnp.bfloat16), jnp.where(low,lses[0],lses[1]))
+
     nb=qi.shape[0]//qb
+
     def body(b,c):
         r=pl.ds(pl.multiple_of(b*qb,qb),qb)
+
         def store(o,l):
             oi[r,:]=o; li[r,:]=l
+
         block(qi[r,:],store)
         return c
+
     lax.fori_loop(0,nb,body,0)
+
     def store(o,l):
         ot[...]=o; lt[...]=l
+
     block(qt[...],store)
+
 
 def attn_fwd(img,txt,mask,qb=256):
     ri,c3=img.shape; rt=txt.shape[0]; c=c3//3; np_=c//PAIR
@@ -63,6 +76,7 @@
         name="attn_fwd")
     return f(mask,img,img,img,txt,txt,txt)
 
+
 def attn_bwd_kernel(scale,qb,mask_ref,qi,ki,vi,qt,kt,vt,oi,ot,li,lt,gi,gt,dqi,dki,dvi,dqt,dkt,dvt,aki,avi,akt,avt):
     low = lax.broadcasted_iota(jnp.int32,(1,PAIR),1)<HEAD_DIM
     live = mask_ref[:,0:1]>0
@@ -71,6 +85,7 @@
     keeps=[low,jnp.logical_not(low)]
     kim=[jnp.where(k,k_img,jnp.zeros_like(k_img)) for k in keeps]
     ktm=[jnp.where(k,k_txt,jnp.zeros_like(k_txt)) for k in keeps]
+
     def block(q,o,l,g,store):
         q=q*jnp.asarray(scale,q.dtype)
         lT=l.T
@@ -91,17 +106,25 @@
             d=dot(si,kim[h],TN)+dot(st,ktm[h],TN)
             dq=d if dq is None else dq+d
         store((dq*scale).astype(jnp.bfloat16))
+
     nb=qi.shape[0]//qb
+
     def body(b,c):
         r=pl.ds(pl.multiple_of(b*qb,qb),qb)
+
         def store(v): dqi[r,:]=v
+
         block(qi[r,:],oi[r,:],li[r,:],gi[r,:],store)
         return c
+
     lax.fori_loop(0,nb,body,0)
+
     def store(v): dqt[...]=v
+
     block(qt[...],ot[...],lt[...],gt[...],store)
     dki[...]=aki[...].astype(jnp.bfloat16); dvi[...]=avi[...].astype(jnp.bfloat16)
     dkt[...]=akt[...].astype(jnp.bfloat16); dvt[...]=avt[...].astype(jnp.bfloat16)
+
 
 def attn_bwd(img,txt,mask,oi,ot,li,lt,gi,gt,qb=256):
     ri,c3=img.shape; rt=txt.shape[0]; c=c3//3; np_=c//PAIR
@@ -166,11 +189,6 @@
     return centred * r, r
 
 
-def norm_back(v, e):
-    n, r = normed(v)
-    return r * (e - jnp.mean(e, axis=-1, keepdims=True) - n * jnp.mean(e * n, axis=-1, keepdims=True)), n
-
-
 def matmul(a, b, dims):
     return lax.dot_general(a, b, (dims, ((), ())), preferred_element_type=F32)
 
@@ -196,39 +214,178 @@
             for device in range(self.size)
         ]
 
+    def shift(self, up, down):
+        return lax.ppermute(up, "mp", self.up), lax.ppermute(down, "mp", self.down)
+
     def gather(self, x):
-        cut = x.shape[0] // 16 * 8
+        cut = cut_of(x.shape[0])
         blocks, a, b = [x], x, x
         for _ in range(1, self.size // 2):
-            a = lax.ppermute(a, "mp", self.up)
-            b = lax.ppermute(b, "mp", self.down)
+            a, b = self.shift(a, b)
             blocks += [a, b]
-        first = lax.ppermute(a[:cut], "mp", self.up)
-        second = lax.ppermute(b[cut:], "mp", self.down)
-        return blocks + [jnp.concatenate([first, second], axis=0)]
-
-    def scatter(self, blocks):
-        far = blocks[-1]
-        cut = far.shape[0] // 16 * 8
-        up = lax.ppermute(far[:cut], "mp", self.up)
-        down = lax.ppermute(far[cut:], "mp", self.down)
+        first, second = self.shift(a[:cut], b[cut:])
+        return blocks, (first, second)
+
+    def scatter(self, image, text):
+        rows, extra = image.shape[0] // self.size, text.shape[0] // self.size
+        cut = cut_of(rows + extra)
+        far = (self.size - 1) * rows
+        second = jnp.concatenate([image[far + cut :], text[(self.size - 1) * extra :]], axis=0)
+        up, down = self.shift(image[far : far + cut], second)
         half = self.size // 2
+        if half == 1:
+            full = jnp.concatenate([up, down], axis=0)
+            return full, jnp.zeros_like(full)
         for t in range(half - 1, 0, -1):
-            ahead, behind = blocks[2 * t], blocks[2 * t - 1]
-            if t == half - 1:
-                ahead = jnp.concatenate([add_low(ahead[:cut], up), ahead[cut:]], axis=0)
-                behind = jnp.concatenate([behind[:cut], add_low(behind[cut:], down)], axis=0)
-            else:
-                ahead, behind = add_low(ahead, up), add_low(behind, down)
-            up = lax.ppermute(ahead, "mp", self.up)
-            down = lax.ppermute(behind, "mp", self.down)
-        if half == 1:
-            return blocks[0].astype(F32) + jnp.concatenate([up, down], axis=0).astype(F32)
-        return blocks[0].astype(F32) + up.astype(F32) + down.astype(F32)
-
-
-def add_low(a, b):
-    return (a.astype(F32) + b.astype(F32)).astype(LOW)
+            ahead, behind = ring_add(image, text, up, down, 2 * t, 2 * t - 1, rows, extra, t == half - 1)
+            up, down = self.shift(ahead, behind)
+        return up, down
+
+
+def cut_of(rows):
+    return rows // 32 * 16
+
+
+def ring_add_kernel(halves, ia, ib, text, up, down, ahead, behind, ka, kb):
+    rows, cut = ia.shape[0], up.shape[0]
+    extra = ahead.shape[0] - rows
+    wide = lambda v: v.astype(F32)
+    ta = text[ka * extra : (ka + 1) * extra, :]
+    tb = text[kb * extra : (kb + 1) * extra, :]
+    if halves:
+        ahead[:cut, :] = (wide(ia[:cut, :]) + wide(up[...])).astype(LOW)
+        ahead[cut:rows, :] = ia[cut:, :]
+        ahead[rows:, :] = ta
+        behind[:cut, :] = ib[:cut, :]
+        behind[cut:rows, :] = (wide(ib[cut:, :]) + wide(down[: rows - cut, :])).astype(LOW)
+        behind[rows:, :] = (wide(tb) + wide(down[rows - cut :, :])).astype(LOW)
+    else:
+        for out, image, words, got in ((ahead, ia, ta, up), (behind, ib, tb, down)):
+            out[:rows, :] = (wide(image[...]) + wide(got[:rows, :])).astype(LOW)
+            out[rows:, :] = (wide(words) + wide(got[rows:, :])).astype(LOW)
+
+
+def whole(a):
+    return pl.BlockSpec(a.shape, lambda i: (0,) * len(a.shape))
+
+
+def ring_add(image, text, up, down, ka, kb, rows, extra, halves):
+    width = image.shape[1]
+    out = jax.ShapeDtypeStruct((rows + extra, width), LOW)
+    return pl.pallas_call(
+        lambda *refs: ring_add_kernel(halves, *refs, ka, kb),
+        grid=(1,),
+        in_specs=[
+            pl.BlockSpec((rows, width), lambda i: (ka, 0)),
+            pl.BlockSpec((rows, width), lambda i: (kb, 0)),
+            whole(text),
+            whole(up),
+            whole(down),
+        ],
+        out_specs=[whole(out)] * 2,
+        out_shape=[out] * 2,
+        cost_estimate=pl.CostEstimate(flops=rows * width, bytes_accessed=rows * width * 10, transcendentals=0),
+        name="ring_add",
+    )(image, image, text, up, down)
+
+
+def row_loop(rows, extra, body):
+    for stream, start, count in ((0, 0, rows), (1, rows, extra)):
+        chunk = 16 if count % 16 == 0 else 8 if count % 8 == 0 else count
+        if chunk == count:
+            body(stream, pl.ds(start, count), pl.ds(0, count))
+            continue
+
+        def one(i, carry, stream=stream, start=start, chunk=chunk):
+            off = pl.multiple_of(i * chunk, chunk)
+            body(stream, pl.ds(pl.multiple_of(start + off, 8), chunk), pl.ds(off, chunk))
+            return carry
+
+        lax.fori_loop(0, count // chunk, one, 0)
+
+
+def mean(v):
+    return jnp.mean(v, axis=-1, keepdims=True)
+
+
+def settle_kernel(rows, gate, norm, x, own, text, up, down, gates, norms, branch, y, n):
+    def body(s, r, q):
+        mine = own if s == 0 else text
+        b = mine[q, :].astype(F32) + up[r, :].astype(F32) + down[r, :].astype(F32)
+        branch[r, :] = b.astype(LOW)
+        v = x[r, :] + gates[s, gate : gate + 1, :] * b
+        y[r, :] = v.astype(y.dtype)
+        if norm is not None:
+            centred = v - mean(v)
+            unit = centred * lax.rsqrt(mean(centred * centred) + EPSILON)
+            n[r, :] = (unit * (1.0 + norms[s, norm + 1 : norm + 2, :]) + norms[s, norm : norm + 1, :]).astype(LOW)
+
+    row_loop(rows, x.shape[0] - rows, body)
+
+
+def settle(rows, gate, norm, x, image, text, up, down, gates, norms):
+    height, width = x.shape
+    shape = lambda kind: jax.ShapeDtypeStruct((height, width), kind)
+    outs = [shape(LOW), shape(LOW if norm is None else F32)] + ([] if norm is None else [shape(LOW)])
+    kernel = functools.partial(settle_kernel, rows, gate, norm)
+    if norm is None:
+        kernel = lambda *refs: settle_kernel(rows, gate, None, *refs, None)
+    return pl.pallas_call(
+        kernel,
+        grid=(1,),
+        in_specs=[whole(x), pl.BlockSpec((rows, width), lambda i: (0, 0))]
+        + [whole(a) for a in (text, up, down, gates, norms)],
+        out_specs=[whole(o) for o in outs],
+        out_shape=outs,
+        compiler_params=pltpu.CompilerParams(vmem_limit_bytes=40 << 20),
+        cost_estimate=pl.CostEstimate(flops=20 * height * width, bytes_accessed=18 * height * width, transcendentals=0),
+        name="settle",
+    )(x, image, text, up, down, gates, norms)
+
+
+def unsettle_kernel(rows, norm, gate, x, g, branch, own, text, up, down, norms, gates, d, low_out, sums):
+    sums[...] = jnp.zeros_like(sums)
+
+    def body(s, r, q):
+        mine = own if s == 0 else text
+        dn = mine[q, :].astype(F32) + up[r, :].astype(F32) + down[r, :].astype(F32)
+        v, upstream = x[r, :], g[r, :]
+        centred = v - mean(v)
+        inverse = lax.rsqrt(mean(centred * centred) + EPSILON)
+        n = centred * inverse
+        e = dn * (1.0 + norms[s, norm + 1 : norm + 2, :])
+        total = upstream + inverse * (e - mean(e) - n * mean(e * n))
+        d[r, :] = total
+        if gate is not None:
+            low_out[r, :] = (gates[s, gate : gate + 1, :] * total).astype(LOW)
+        for k, term in enumerate((dn, dn * n, upstream * branch[r, :].astype(F32))):
+            sums[s * 3 + k : s * 3 + k + 1, :] += jnp.sum(term, axis=0, keepdims=True)
+
+    row_loop(rows, x.shape[0] - rows, body)
+
+
+def unsettle(rows, norm, gate, x, g, branch, image, text, up, down, norms, gates):
+    height, width = x.shape
+    outs = [jax.ShapeDtypeStruct((height, width), F32)]
+    if gate is not None:
+        outs.append(jax.ShapeDtypeStruct((height, width), LOW))
+    outs.append(jax.ShapeDtypeStruct((8, width), F32))
+    kernel = functools.partial(unsettle_kernel, rows, norm, gate)
+    if gate is None:
+        kernel = lambda *refs: unsettle_kernel(rows, norm, None, *refs[:-1], None, refs[-1])
+    got = pl.pallas_call(
+        kernel,
+        grid=(1,),
+        in_specs=[whole(x), whole(g), whole(branch), pl.BlockSpec((rows, width), lambda i: (0, 0))]
+        + [whole(a) for a in (text, up, down, norms, gates)],
+        out_specs=[whole(o) for o in outs],
+        out_shape=outs,
+        compiler_params=pltpu.CompilerParams(vmem_limit_bytes=40 << 20),
+        cost_estimate=pl.CostEstimate(flops=40 * height * width, bytes_accessed=24 * height * width, transcendentals=0),
+        name="unsettle",
+    )(x, g, branch, image, text, up, down, norms, gates)
+    sums = got[-1][:6].reshape(2, 3, width)
+    return got[0], (got[1] if gate is not None else None), sums
 
 
 class Step:
@@ -239,77 +396,105 @@
         return jnp.where(self.keep, modulation[0, member][None, :], modulation[1, member][None, :])
 
     def gather(self, x):
-        blocks = self.ring.gather(x)
+        blocks, (first, second) = self.ring.gather(x)
         r = self.image_rows
+        rest = r - first.shape[0]
         return (
-            jnp.concatenate([block[:r] for block in blocks], axis=0),
-            jnp.concatenate([block[r:] for block in blocks], axis=0),
+            jnp.concatenate([block[:r] for block in blocks] + [first, second[:rest]], axis=0),
+            jnp.concatenate([block[r:] for block in blocks] + [second[rest:]], axis=0),
         )
 
-    def scatter(self, parts):
-        r, t = self.image_rows, self.text_rows
-        return self.ring.scatter(
-            [
-                jnp.concatenate([parts[0][k * r : k * r + r], parts[1][k * t : k * t + t]], axis=0)
-                for k in range(self.ring.size)
-            ]
+    def product(self, a, b, dims):
+        image = matmul(a[0], b[0], dims)
+        return [image, matmul(a[1], b[1], dims)]
+
+    def start(self, x, modulation):
+        return normed(x)[0] * (1.0 + self.pick(modulation, 1)) + self.pick(modulation, 0)
+
+    def forward(self, x, n1, modulation, following, weights, mask, held=None):
+        qkv, out, up, down = weights
+        rows1 = self.gather(n1)
+        proj = low(self.product(rows1, qkv, ((1,), (0,))))
+        mixture, kept = attention(proj[0], proj[1], mask)
+        partial = low(self.product(mixture, out, ((1,), (1,))))
+        got = self.ring.scatter(*partial)
+        branch1, middle, n2 = settle(self.image_rows, 2, 3, x, *partial, *got, modulation, modulation)
+        rows2 = self.gather(n2)
+        if held is not None:
+            image, held = tie(rows2[0], held)
+            rows2 = (image, rows2[1])
+        pre = self.product(rows2, up, ((1,), (0,)))
+        act = low([gelu(p) for p in pre])
+        partial = low(self.product(act, down, ((1,), (1,))))
+        got = self.ring.scatter(*partial)
+        if following is None:
+            branch2, y = settle(self.image_rows, 5, None, middle, *partial, *got, modulation, modulation)
+            n = None
+        else:
+            branch2, y, n = settle(self.image_rows, 5, 0, middle, *partial, *got, modulation, following)
+        return y, n, (x, modulation, rows1, kept, mixture, branch1, middle, rows2, pre, act, branch2), held
+
+    def backward_mlp(self, g, db2, saved, weights):
+        _, _, up, down = weights
+        _, modulation, _, _, _, _, middle, rows2, pre, act, branch2 = saved
+        db2 = self.gather(db2)
+        grad_act = self.product(db2, down, ((1,), (0,)))
+        d_pre = low([grad_act[s] * gelu_slope(pre[s]) for s in range(2)])
+        partial = low(self.product(d_pre, up, ((1,), (1,))))
+        got = self.ring.scatter(*partial)
+        d_middle, db1, mods = unsettle(
+            self.image_rows, 3, 2, middle, g, branch2, *partial, *got, modulation, modulation
         )
-
-    def forward(self, x, modulation, weights, mask):
-        qkv, out, up, down = weights
-        n1 = normed(x)[0] * (1.0 + self.pick(modulation, 1)) + self.pick(modulation, 0)
-        rows1 = self.gather(n1.astype(LOW))
-        proj = [matmul(rows1[s], qkv[s], ((1,), (0,))).astype(LOW) for s in range(2)]
-        mixture, kept = attention(proj[0], proj[1], mask)
-        branch1 = self.scatter([matmul(mixture[s], out[s], ((1,), (1,))).astype(LOW) for s in range(2)])
-        middle = x + self.pick(modulation, 2) * branch1
-        n2 = normed(middle)[0] * (1.0 + self.pick(modulation, 4)) + self.pick(modulation, 3)
-        rows2 = self.gather(n2.astype(LOW))
-        pre = [matmul(rows2[s], up[s], ((1,), (0,))) for s in range(2)]
-        act = [gelu(pre[s]).astype(LOW) for s in range(2)]
-        branch2 = self.scatter([matmul(act[s], down[s], ((1,), (1,))).astype(LOW) for s in range(2)])
-        y = middle + self.pick(modulation, 5) * branch2
-        return y, (x, modulation, rows1, kept, mixture, branch1, middle, rows2, pre, act, branch2)
-
-    def sums(self, v):
-        r = self.image_rows
-        return jnp.stack([jnp.sum(v[:r], axis=0), jnp.sum(v[r:], axis=0)])
-
-    def backward_mlp(self, g, saved, weights):
-        qkv, out, up, down = weights
-        x, modulation, rows1, kept, mixture, branch1, middle, rows2, pre, act, branch2 = saved
-        db2 = self.gather((self.pick(modulation, 5) * g).astype(LOW))
-        grad_act = [matmul(db2[s], down[s], ((1,), (0,))) for s in range(2)]
-        d_pre = [(grad_act[s] * gelu_slope(pre[s])).astype(LOW) for s in range(2)]
-        dn2 = self.scatter([matmul(d_pre[s], up[s], ((1,), (1,))).astype(LOW) for s in range(2)])
-        inner, n = norm_back(middle, dn2 * (1.0 + self.pick(modulation, 4)))
-        d_middle = g + inner
-        mods = [self.sums(dn2), self.sums(dn2 * n), self.sums(g * branch2)]
-        grads_down = [matmul(db2[s], act[s], ((0,), (0,))) for s in range(2)]
-        grads_up = [matmul(rows2[s], d_pre[s], ((0,), (0,))) for s in range(2)]
-        return d_middle, mods, grads_up, grads_down
-
-    def backward_attention(self, d_middle, saved, weights, mask):
-        qkv, out, up, down = weights
-        x, modulation, rows1, kept, mixture, branch1, middle, rows2, pre, act, branch2 = saved
-        db1 = self.gather((self.pick(modulation, 2) * d_middle).astype(LOW))
-        d_mixture = [matmul(db1[s], out[s], ((1,), (0,))).astype(LOW) for s in range(2)]
+        db1 = self.gather(db1)
+        return d_middle, mods, db1, (rows2, d_pre), (db2, act)
+
+    def backward_attention(self, d_middle, db1, saved, below, weights, mask):
+        qkv, out, _, _ = weights
+        x, modulation, rows1, kept, mixture, branch1, _, _, _, _, _ = saved
+        d_mixture = low(self.product(db1, out, ((1,), (0,))))
         d_proj = attention_back(kept, mask, d_mixture)
-        dn1 = self.scatter([matmul(d_proj[s], qkv[s], ((1,), (1,))).astype(LOW) for s in range(2)])
-        inner, n = norm_back(x, dn1 * (1.0 + self.pick(modulation, 1)))
-        mods = [self.sums(dn1), self.sums(dn1 * n), self.sums(d_middle * branch1)]
-        grads_out = [matmul(db1[s], mixture[s], ((0,), (0,))) for s in range(2)]
-        grads_qkv = [matmul(rows1[s], d_proj[s], ((0,), (0,))) for s in range(2)]
-        return d_middle + inner, mods, grads_qkv, grads_out
+        partial = low(self.product(d_proj, qkv, ((1,), (1,))))
+        got = self.ring.scatter(*partial)
+        g, db2, mods = unsettle(
+            self.image_rows,
+            0,
+            None if below is None else 5,
+            x,
+            d_middle,
+            branch1,
+            *partial,
+            *got,
+            modulation,
+            modulation if below is None else below,
+        )
+        return g, db2, mods, (rows1, d_proj), (db1, mixture)
+
+
+def low(values):
+    return [v.astype(LOW) for v in values]
+
+
+def tie(*values):
+    return lax.optimization_barrier(values)
 
 
 def gather_weight(w):
     return lax.all_gather(w, "dp", axis=1, tiled=True)
 
 
-def reduce_weight(parts):
-    total = jnp.stack([sum(part[s] for part in parts).astype(LOW) for s in range(2)])
-    return lax.psum_scatter(total, "dp", scatter_dimension=1, tiled=True).astype(F32)
+def weight_grads(pairs):
+    out = []
+    for s in range(2):
+        out.append(sum(matmul(a[s], b[s], ((0,), (0,))) for a, b in pairs).astype(LOW))
+    return jnp.stack(out)
+
+
+def reduce_weight(total):
+    return lax.psum_scatter(total, "dp", scatter_dimension=1, tiled=True)
+
+
+def exchange_sum(parts, axis):
+    return jnp.sum(lax.all_to_all(parts, axis, split_axis=0, concat_axis=0, tiled=True), axis=0)
 
 
 def device_program(
@@ -353,8 +538,10 @@
     depth = mod_weight.shape[2]
     own_condition = lax.dynamic_slice_in_dim(condition, lax.axis_index("dp") * depth, depth, axis=1)
     partial = jnp.einsum("nd,lsdkc->nlskc", own_condition, mod_weight, preferred_element_type=F32)
-    own_mod = lax.psum_scatter(partial, "dp", scatter_dimension=0, tiled=True)
-    modulation = lax.all_gather(own_mod, "mp", axis=4, tiled=True)
+    columns = mod_weight.shape[4]
+    own_mod = exchange_sum(partial.reshape(-1, seqs * LAYERS * 12, columns), "dp")
+    modulation = lax.all_gather(own_mod, "mp", axis=0)
+    modulation = jnp.swapaxes(modulation, 0, 1).reshape(seqs, LAYERS, 2, 6, width)
 
     owners = jnp.array(ring.owners(), dtype=jnp.int32)[lax.axis_index("mp")]
     segments = (owners % half) * 2 + owners // half
@@ -376,29 +563,53 @@
     rows = deal(image_input, text_input)
     upstream = deal(image_cotangent, text_cotangent)
     saved = []
+    mods = [[modulation[s, l] for l in range(LAYERS)] + [None] for s in range(seqs)]
+    ready = [low([step.start(rows[s], mods[s][0])])[0] for s in range(seqs)]
+    last = LAYERS - 1
+    db2 = [low([step.pick(mods[s][last], 5) * upstream[s]])[0] for s in range(seqs)]
     for l in range(LAYERS):
-        done = [step.forward(rows[s], modulation[s, l], weights[l], masks[s]) for s in range(seqs)]
-        rows = [d[0] for d in done]
-        saved.append([d[1] for d in done])
-    image_output, text_output = undeal([row.astype(LOW) for row in rows])
-
-    reduced, mod_rows = [], []
+        done = [
+            step.forward(rows[s], ready[s], mods[s][l], mods[s][l + 1], weights[l], masks[s], None if l else db2[s])
+            for s in range(seqs)
+        ]
+        rows, ready = [d[0] for d in done], [d[1] for d in done]
+        saved.append([d[2] for d in done])
+        if l == 0:
+            db2 = [d[3] for d in done]
+    image_output, text_output = undeal(rows)
+
+    reduced, mod_rows = [None] * LAYERS, [None] * LAYERS
     for l in reversed(range(LAYERS)):
-        mlp = [step.backward_mlp(upstream[s], saved[l][s], weights[l]) for s in range(seqs)]
-        grad_down = reduce_weight([m[3] for m in mlp])
-        grad_up = reduce_weight([m[2] for m in mlp])
-        att = [step.backward_attention(mlp[s][0], saved[l][s], weights[l], masks[s]) for s in range(seqs)]
-        grad_out = reduce_weight([a[3] for a in att])
-        grad_qkv = reduce_weight([a[2] for a in att])
-        upstream = [a[0] for a in att]
-        mod_rows.insert(0, jnp.stack([jnp.stack(att[s][1] + mlp[s][1], axis=1) for s in range(seqs)]))
-        reduced.insert(0, (grad_qkv, grad_out, grad_up, grad_down))
+        mlp = [step.backward_mlp(upstream[s], db2[s], saved[l][s], weights[l]) for s in range(seqs)]
+        down_total = weight_grads([m[4] for m in mlp])
+        up_total = weight_grads([m[3] for m in mlp])
+        db1 = [m[2] for m in mlp]
+        grad_down = reduce_weight(down_total)
+        grad_up = reduce_weight(up_total)
+        if l < last:
+            (image, text), above_up, above_down = tie(db1[1], reduced[l + 1][2], reduced[l + 1][3])
+            db1[1] = (image, text)
+            reduced[l + 1][2:] = [above_up, above_down]
+        att = [
+            step.backward_attention(mlp[s][0], db1[s], saved[l][s], mods[s][l - 1] if l else None, weights[l], masks[s])
+            for s in range(seqs)
+        ]
+        out_total = weight_grads([a[4] for a in att])
+        qkv_total = weight_grads([a[3] for a in att])
+        upstream, db2 = [a[0] for a in att], [a[1] for a in att]
+        if l:
+            db2[1], out_total, qkv_total = tie(db2[1], out_total, qkv_total)
+        grad_out = reduce_weight(out_total)
+        grad_qkv = reduce_weight(qkv_total)
+        mod_rows[l] = jnp.stack([jnp.concatenate([att[s][2], mlp[s][1]], axis=1) for s in range(seqs)])
+        reduced[l] = [grad_qkv, grad_out, grad_up, grad_down]
     image_grad, text_grad = undeal(upstream)
-
-    mod_sums = lax.psum_scatter(jnp.stack(mod_rows, axis=1), "mp", scatter_dimension=4, tiled=True)
-    all_mods = lax.all_gather(mod_sums, "dp", axis=0, tiled=True)
+    reduced = [[r.astype(F32) for r in layer] for layer in reduced]
+
+    mod_rows = jnp.stack(mod_rows, axis=1).reshape(-1, mp_size, columns)
+    mod_sums = exchange_sum(jnp.swapaxes(mod_rows, 0, 1).reshape(mp_size, -1, columns), "mp")
+    all_mods = lax.all_gather(mod_sums, "dp", axis=0).reshape(-1, LAYERS, 2, 6, columns)
     grad_mod = jnp.einsum("nd,nlskc->lsdkc", own_condition.astype(F32), all_mods, precision=lax.Precision.HIGHEST)
-    columns = qkv_weight.shape[4]
     grad_qkv = jnp.stack(
         [jnp.swapaxes(r[0].reshape(2, -1, 3, columns), 1, 2) for r in reduced]
     )
@@ -424,8 +635,12 @@
         P(None, None, "dp", "mp"),
         P(None, None, "mp", "dp"),
     )
+
+    def program(*arrays):
+        return device_program(mesh.shape["mp"], *arrays)
+
     return jax.shard_map(
-        functools.partial(device_program, mesh.shape["mp"]),
+        program,
         mesh=mesh,
         in_specs=(rows, rows, P(), P("dp", None)) + grads + (rows, rows),
         out_specs=(rows, rows, rows, rows) + grads,

time: 2430 us -> 1830 us (0.75)
  waiting for transfers between devices: 1180 us -> 539 us
  Pallas kernels: 224 us -> 374 us
  matrix products: 481 us -> 425 us
  other arithmetic: 142 us -> 91.3 us
    reduce_scatter x8, waiting for transfers between devices: 400 us -> 0.01 us  [reduce_weight(): return lax.psum_scatter(total, 'dp', scatter_dimension=1, tiled=True)]
    pallas_call x0 -> x32, Pallas kernels: none -> 149 us  [the longest x8 60.5 us: unsettle(): pl.pallas_call(kernel, grid=(1,), in_specs=[whole(x), whole(g), whole(bra...]
    ppermute x128, waiting for transfers between devices: 619 us -> 494 us  [the longest x64 282 us: shift(): lax.ppermute(up, 'mp', self.up)]
    all_gather x8, waiting for transfers between devices: 113 us -> 0.07 us  [gather_weight(): return lax.all_gather(w, 'dp', axis=1, tiled=True)]
    dot_general x96, matrix products: 474 us -> 419 us  [matmul(): return lax.dot_general(a, b, (dims, ((), ())), preferred_element_type=F32)]
    unnamed x20 -> x16, waiting for transfers between devices: 42.7 us -> 0.77 us
    all_to_all x0 -> x2, waiting for transfers between devices: none -> 34 us  [exchange_sum(): lax.all_to_all(parts, axis, split_axis=0, concat_axis=0, tiled=True)]
    unnamed x1195 -> x926, local copies, waits for them, and re-layouts: 95.8 us -> 123 us
  transfers between devices with their start and end apart: 150 -> 150, of which waited for: 85 -> 63; matrix products, arithmetic and copies ran while one was open for 25% -> 34% of each run, Pallas kernels for 6% -> 20%
where the time goes in v2:
time: 1830 us; the launch traced here: 1820 us
  waiting for transfers between devices  539 us (29%)
  matrix products  425 us (23%)
  Pallas kernels  374 us (20%)
  local copies, waits for them, and re-layouts  196 us (11%)
  starting transfers between devices  151 us (8%)
  other arithmetic  91.3 us (5%)
  blocking collectives  26.7 us (1%)
  between operations  20.7 us (1%)
    dot_general x96, matrix products, matmul(): return lax.dot_general(a, b, (dims, ((), ())), preferred_element_type=F32)  419 us
    ppermute x64, waiting for transfers between devices, shift(): lax.ppermute(up, 'mp', self.up)  282 us
    ppermute x64, waiting for transfers between devices, shift(): lax.ppermute(down, 'mp', self.down)  213 us
    pallas_call x4, Pallas kernels, attn_bwd(): return f(mask, img, img, img, txt, txt, txt, oi, ot, li, lt, gi, gt)  135 us
    unnamed x926, local copies, waits for them, and re-layouts  123 us
    pallas_call x4, Pallas kernels, attn_fwd(): return f(mask, img, img, img, txt, txt, txt)  89.5 us
    ppermute x64, starting transfers between devices, shift(): lax.ppermute(up, 'mp', self.up)  73.8 us
    ppermute x64, starting transfers between devices, shift(): lax.ppermute(down, 'mp', self.down)  63.3 us
  transfers between devices with their start and end apart: 150, of which 63 were waited for; matrix products, arithmetic and copies ran while one was open for 34% of the time, Pallas kernels for 20%

profile of v2, /device:TPU:0, one launch (start us, length us, event | category | flops | bytes accessed | tf_op | source)
XLA Modules:
  0.0 1822.6 jit_solution(13746004348213284736)
XLA Ops:
  54.4 17.3 all-to-all-done
  108.3 17.8 collective-permute-done.2
  158.1 22.3 %attn_fwd.6 = (bf16[1024,384]{1,0:T(8,128)(2,1)}, bf16[160,384]{1,0:T(8,128)(2,1)}, f32[1024,384]{1,0:T(8,128)}, f32[160,384]{1,0:T(8,128)}) custom-call(s32[8,160]{1,0:T(8,128)} %broadcast_in_dim.194.mask_ref, bf16[1024,1152]{1,0:T(8,128)(2,1)} %convolution_convert_fusion.9.qi.ki.vi, bf16[1024,1152]{1,0:T(8,128)(2,1)} %convolution_convert_fusion.9.qi.ki.vi, ...), custom_call_target="tpu_custom_call" | custom-call | flops 2153250816 | bytes 5455872 | tf_op jit(solution)/shard_map/attn_fwd/pallas_call | solution.py:77
  198.6 22.2 %attn_fwd.4 = (bf16[1024,384]{1,0:T(8,128)(2,1)}, bf16[160,384]{1,0:T(8,128)(2,1)}, f32[1024,384]{1,0:T(8,128)}, f32[160,384]{1,0:T(8,128)}) custom-call(s32[8,160]{1,0:T(8,128)} %broadcast_in_dim.179.mask_ref, bf16[1024,1152]{1,0:T(8,128)(2,1)} %convolution_convert_fusion.15.qi.ki.vi, bf16[1024,1152]{1,0:T(8,128)(2,1)} %convolution_convert_fusion.15.qi.ki.vi, ...), custom_call_target="tpu_custom_call" | custom-call | flops 2153250816 | bytes 5455872 | tf_op jit(solution)/shard_map/attn_fwd/pallas_call | solution.py:77
  309.5 16.5 collective-permute-done.10
  352.5 14.3 collective-permute-done.100
  370.4 16.0 collective-permute-done.68
  500.0 21.2 %collective-permute-done.50 = bf16[296,1536]{1,0:T(8,128)(2,1)S(1)} collective-permute-done((bf16[296,1536]{1,0:T(8,128)(2,1)S(1)}, bf16[296,1536]{1,0:T(8,128)(2,1)S(1)}, u32[]{:S(2)}, u32[]{:S(2)}) %collective-permute-start.50) | collective-permute-done | bytes 909344 | tf_op jit(solution)/shard_map/ppermute | solution.py:218
  522.6 13.2 collective-permute-done.18
  583.1 22.7 %attn_fwd.7 = (bf16[1024,384]{1,0:T(8,128)(2,1)}, bf16[160,384]{1,0:T(8,128)(2,1)}, f32[1024,384]{1,0:T(8,128)}, f32[160,384]{1,0:T(8,128)}) custom-call(s32[8,160]{1,0:T(8,128)} %broadcast_in_dim.194.mask_ref, bf16[1024,1152]{1,0:T(8,128)(2,1)} %convolution_convert_fusion.6.qi.ki.vi, bf16[1024,1152]{1,0:T(8,128)(2,1)} %convolution_convert_fusion.6.qi.ki.vi, ...), custom_call_target="tpu_custom_call" | custom-call | flops 2153250816 | bytes 5455872 | tf_op jit(solution)/shard_map/attn_fwd/pallas_call | solution.py:77
  622.0 22.3 %attn_fwd.5 = (bf16[1024,384]{1,0:T(8,128)(2,1)}, bf16[160,384]{1,0:T(8,128)(2,1)}, f32[1024,384]{1,0:T(8,128)}, f32[160,384]{1,0:T(8,128)}) custom-call(s32[8,160]{1,0:T(8,128)} %broadcast_in_dim.179.mask_ref, bf16[1024,1152]{1,0:T(8,128)(2,1)} %convolution_convert_fusion.12.qi.ki.vi, bf16[1024,1152]{1,0:T(8,128)(2,1)} %convolution_convert_fusion.12.qi.ki.vi, ...), custom_call_target="tpu_custom_call" | custom-call | flops 2153250816 | bytes 5455872 | tf_op jit(solution)/shard_map/attn_fwd/pallas_call | solution.py:77
  735.7 15.2 collective-permute-done.27
  945.4 28.4 %collective-permute-done.31.refs_4_ = bf16[152,1536]{1,0:T(8,128)(2,1)S(1)} collective-permute-done((bf16[152,1536]{1,0:T(8,128)(2,1)S(1)}, bf16[152,1536]{1,0:T(8,128)(2,1)S(1)}, u32[]{:S(2)}, u32[]{:S(2)}) %collective-permute-start.31) | collective-permute-done | bytes 466976 | tf_op jit(solution)/shard_map/ppermute | solution.py:218
  1027.0 15.3 collective-permute-done.74.down
  1063.9 15.0 collective-permute-done.76
  1094.2 33.6 %attn_bwd.6 = (bf16[1024,384]{1,0:T(8,128)(2,1)}, bf16[1024,384]{1,0:T(8,128)(2,1)}, bf16[1024,384]{1,0:T(8,128)(2,1)}, bf16[160,384]{1,0:T(8,128)(2,1)}, bf16[1...) custom-call(s32[160,128]{1,0:T(8,128)} %broadcast_in_dim.208.mask_ref, ...), custom_call_target="tpu_custom_call" | custom-call | flops 5383127040 | bytes 11821056 | tf_op jit(solution)/shard_map/attn_bwd/pallas_call | solution.py:142
  1144.4 34.0 %attn_bwd.4 = (bf16[1024,384]{1,0:T(8,128)(2,1)}, bf16[1024,384]{1,0:T(8,128)(2,1)}, bf16[1024,384]{1,0:T(8,128)(2,1)}, bf16[160,384]{1,0:T(8,128)(2,1)}, bf16[1...) custom-call(s32[160,128]{1,0:T(8,128)} %broadcast_in_dim.207.mask_ref, ...), custom_call_target="tpu_custom_call" | custom-call | flops 5383127040 | bytes 11821056 | tf_op jit(solution)/shard_map/attn_bwd/pallas_call | solution.py:142
  1286.5 14.1 collective-permute-done.83
  1388.7 14.3 collective-permute-done.121.up
  1442.6 17.1 collective-permute-done.91
  1547.3 33.6 %attn_bwd.5 = (bf16[1024,384]{1,0:T(8,128)(2,1)}, bf16[1024,384]{1,0:T(8,128)(2,1)}, bf16[1024,384]{1,0:T(8,128)(2,1)}, bf16[160,384]{1,0:T(8,128)(2,1)}, bf16[1...) custom-call(s32[160,128]{1,0:T(8,128)} %broadcast_in_dim.207.mask_ref, ...), custom_call_target="tpu_custom_call" | custom-call | flops 5383127040 | bytes 11821056 | tf_op jit(solution)/shard_map/attn_bwd/pallas_call | solution.py:142
  1590.8 33.8 %attn_bwd.7 = (bf16[1024,384]{1,0:T(8,128)(2,1)}, bf16[1024,384]{1,0:T(8,128)(2,1)}, bf16[1024,384]{1,0:T(8,128)(2,1)}, bf16[160,384]{1,0:T(8,128)(2,1)}, bf16[1...) custom-call(s32[160,128]{1,0:T(8,128)} %broadcast_in_dim.208.mask_ref, ...), custom_call_target="tpu_custom_call" | custom-call | flops 5383127040 | bytes 11821056 | tf_op jit(solution)/shard_map/attn_bwd/pallas_call | solution.py:142
  1752.8 16.6 all-to-all-done.1
  1769.5 17.7 all-gather.3
  (1662 shorter events, 1307.3 us)
Async XLA Ops:
  7.2 139.1 %all-gather.13.cloned.1.call-start = ((), (), s32[]{:S(2)}) async-start(), calls=%async_computation.10 | async-start | bytes 7962624 | tf_op jit(solution)/shard_map/all_gather | solution.py:482
  10.9 169.6 %all-gather.15.cloned.1.call-start = ((), (), s32[]{:S(2)}) async-start(), calls=%async_computation.11 | async-start | bytes 2654208 | tf_op jit(solution)/shard_map/all_gather | solution.py:482
  12.9 377.5 %all-gather.25.cloned.1.call-start = ((), (), s32[]{:S(2)}) async-start(), calls=%async_computation.24 | async-start | bytes 10616832 | tf_op jit(solution)/shard_map/all_gather | solution.py:482
  16.2 384.2 %all-gather.17.cloned.1.call-start = ((), (), s32[]{:S(2)}) async-start(), calls=%async_computation.12 | async-start | bytes 10616832 | tf_op jit(solution)/shard_map/all_gather | solution.py:482
  19.5 553.2 %all-gather.19.cloned.1.call-start = ((), (), s32[]{:S(2)}) async-start(), calls=%async_computation.13 | async-start | bytes 7962624 | tf_op jit(solution)/shard_map/all_gather | solution.py:482
  21.8 588.4 %all-gather.21.cloned.1.call-start = ((), (), s32[]{:S(2)}) async-start(), calls=%async_computation.14 | async-start | bytes 2654208 | tf_op jit(solution)/shard_map/all_gather | solution.py:482
  22.4 742.2 %all-gather.27.cloned.1.call-start = ((), (), s32[]{:S(2)}) async-start(), calls=%async_computation.25 | async-start | bytes 10616832 | tf_op jit(solution)/shard_map/all_gather | solution.py:482
  37.7 777.9 %all-gather.23.cloned.1.call-start = ((), (), s32[]{:S(2)}) async-start(), calls=%async_computation.15 | async-start | bytes 10616832 | tf_op jit(solution)/shard_map/all_gather | solution.py:482
  255.2 1217.4 %reduce-scatter.11.cloned.1.call-start = ((), (), s32[]{:S(2)}) async-start(), calls=%async_computation.17 | async-start | bytes 10616832 | tf_op jit(solution)/shard_map/reduce_scatter | solution.py:493
  367.7 287.2 %collective-permute-start.102 = (bf16[152,1536]{1,0:T(8,128)(2,1)}, bf16[152,1536]{1,0:T(8,128)(2,1)}, u32[]{:S(2)}, u32[]{:S(2)}) collective-permute-start(bf16[152,1536]{1,0:T(8,128)(2,1)} %slice.1335), channel_id=1, source_target_pairs={{0,2},{1,0},{3,1},{2,3},{4,6},{5,4},{7,5},{6,7},{8,10},{9,8},{11,9... | collective-permute-start | bytes 1400840 | tf_op jit(solution)/shard_map/ppermute | solution.py:218
  472.8 180.1 %collective-permute-start.101 = (bf16[144,1536]{1,0:T(8,128)(2,1)}, bf16[144,1536]{1,0:T(8,128)(2,1)}, u32[]{:S(2)}, u32[]{:S(2)}) collective-permute-start(bf16[144,1536]{1,0:T(8,128)(2,1)} %slice.1334), channel_id=1, source_target_pairs={{0,1},{1,3},{3,2},{2,0},{4,5},{5,7},{7,6},{6,4},{8,9},{9,11},{11,1... | collective-permute-start | bytes 1327112 | tf_op jit(solution)/shard_map/ppermute | solution.py:218
  474.5 187.0 %collective-permute-start.70 = (bf16[152,1536]{1,0:T(8,128)(2,1)}, bf16[152,1536]{1,0:T(8,128)(2,1)}, u32[]{:S(2)}, u32[]{:S(2)}) collective-permute-start(bf16[152,1536]{1,0:T(8,128)(2,1)} %slice.1291), channel_id=1, source_target_pairs={{0,2},{1,0},{3,1},{2,3},{4,6},{5,4},{7,5},{6,7},{8,10},{9,8},{11,9... | collective-permute-start | bytes 1400840 | tf_op jit(solution)/shard_map/ppermute | solution.py:218
  568.3 85.9 %collective-permute-start.69 = (bf16[144,1536]{1,0:T(8,128)(2,1)}, bf16[144,1536]{1,0:T(8,128)(2,1)}, u32[]{:S(2)}, u32[]{:S(2)}) collective-permute-start(bf16[144,1536]{1,0:T(8,128)(2,1)} %slice.1290), channel_id=1, source_target_pairs={{0,1},{1,3},{3,2},{2,0},{4,5},{5,7},{7,6},{6,4},{8,9},{9,11},{11,1... | collective-permute-start | bytes 1327112 | tf_op jit(solution)/shard_map/ppermute | solution.py:218
  815.5 657.0 %reduce-scatter.9.cloned.1.call-start = ((), (), s32[]{:S(2)}) async-start(), calls=%async_computation.16 | async-start | bytes 10616832 | tf_op jit(solution)/shard_map/reduce_scatter | solution.py:493
  856.0 76.3 %collective-permute-start.104 = (bf16[152,1536]{1,0:T(8,128)(2,1)}, bf16[152,1536]{1,0:T(8,128)(2,1)}, u32[]{:S(2)}, u32[]{:S(2)}) collective-permute-start(bf16[152,1536]{1,0:T(8,128)(2,1)} %pad_maximum_fusion.43), channel_id=1, source_target_pairs={{0,2},{1,0},{3,1},{2,3},{4,6},{5,4},{7,5},{6,7},{8,10},{9,8},{11,9... | collective-permute-start | bytes 1400840 | tf_op jit(solution)/shard_map/ppermute | solution.py:218
  856.4 74.8 %collective-permute-start.103 = (bf16[144,1536]{1,0:T(8,128)(2,1)}, bf16[144,1536]{1,0:T(8,128)(2,1)}, u32[]{:S(2)}, u32[]{:S(2)}) collective-permute-start(bf16[144,1536]{1,0:T(8,128)(2,1)} %slice.1340), channel_id=1, source_target_pairs={{0,1},{1,3},{3,2},{2,0},{4,5},{5,7},{7,6},{6,4},{8,9},{9,11},{11,1... | collective-permute-start | bytes 1327112 | tf_op jit(solution)/shard_map/ppermute | solution.py:218
  860.7 75.2 %collective-permute-start.63 = (bf16[152,1536]{1,0:T(8,128)(2,1)}, bf16[152,1536]{1,0:T(8,128)(2,1)}, u32[]{:S(2)}, u32[]{:S(2)}) collective-permute-start(bf16[152,1536]{1,0:T(8,128)(2,1)} %pad_maximum_fusion.38), channel_id=1, source_target_pairs={{0,2},{1,0},{3,1},{2,3},{4,6},{5,4},{7,5},{6,7},{8,10},{9,8},{11,9... | collective-permute-start | bytes 1400840 | tf_op jit(solution)/shard_map/ppermute | solution.py:218
  861.1 74.7 %collective-permute-start.62 = (bf16[144,1536]{1,0:T(8,128)(2,1)}, bf16[144,1536]{1,0:T(8,128)(2,1)}, u32[]{:S(2)}, u32[]{:S(2)}) collective-permute-start(bf16[144,1536]{1,0:T(8,128)(2,1)} %slice.1281), channel_id=1, source_target_pairs={{0,1},{1,3},{3,2},{2,0},{4,5},{5,7},{7,6},{6,4},{8,9},{9,11},{11,1... | collective-permute-start | bytes 1327112 | tf_op jit(solution)/shard_map/ppermute | solution.py:218
  910.9 838.8 %reduce-scatter.15.cloned.1.call-start = ((), (), s32[]{:S(2)}) async-start(), calls=%async_computation.19 | async-start | bytes 7962624 | tf_op jit(solution)/shard_map/reduce_scatter | solution.py:493
  1275.8 521.8 %reduce-scatter.19.cloned.1.call-start = ((), (), s32[]{:S(2)}) async-start(), calls=%async_computation.21 | async-start | bytes 2654208 | tf_op jit(solution)/shard_map/reduce_scatter | solution.py:493
  1388.7 408.9 %reduce-scatter.17.cloned.1.call-start = ((), (), s32[]{:S(2)}) async-start(), calls=%async_computation.20 | async-start | bytes 2654208 | tf_op jit(solution)/shard_map/reduce_scatter | solution.py:493
  1482.1 317.7 %reduce-scatter.23.cloned.1.call-start = ((), (), s32[]{:S(2)}) async-start(), calls=%async_computation.23 | async-start | bytes 10616832 | tf_op jit(solution)/shard_map/reduce_scatter | solution.py:493
  1511.7 292.0 %reduce-scatter.21.cloned.1.call-start = ((), (), s32[]{:S(2)}) async-start(), calls=%async_computation.22 | async-start | bytes 10616832 | tf_op jit(solution)/shard_map/reduce_scatter | solution.py:493
  1539.1 268.3 %reduce-scatter.13.cloned.1.call-start = ((), (), s32[]{:S(2)}) async-start(), calls=%async_computation.18 | async-start | bytes 7962624 | tf_op jit(solution)/shard_map/reduce_scatter | solution.py:493
  (559 other events, 8616.1 us)
Sparse Core Ops, SparseCore 0:
  11.1 86.3 all-gather.12
  99.6 29.9 all-gather.14
  131.2 89.9 all-gather.24
  223.2 89.1 all-gather.16
  313.8 69.5 all-gather.18
  385.0 30.0 all-gather.20
  417.2 89.9 all-gather.26
  509.4 89.1 all-gather.22
  815.7 97.0 reduce-scatter.10
  914.9 97.8 reduce-scatter.8
  1275.9 75.2 reduce-scatter.14
  1388.8 34.1 reduce-scatter.18
  1482.2 34.5 reduce-scatter.16
  1518.9 98.3 reduce-scatter.22
  1619.5 97.8 reduce-scatter.20
  1719.6 80.3 reduce-scatter.12

commit v3 on v2

--- a/solution.py
+++ b/solution.py
@@ -159,7 +159,7 @@
     gi, gt = (jnp.pad(g, ((0, 0), (0, pad))) for g in grads) if pad else grads
     mask_columns = jnp.broadcast_to(mask[:, None], (mask.shape[0], 128))
     out = attn_bwd(img, txt, mask_columns, oi, ot, li, lt, gi, gt, query_block(img.shape[0]))
-    return tuple(jnp.concatenate([piece[:, :c] for piece in part], axis=1) for part in (out[:3], out[3:]))
+    return tuple([piece[:, :c] for piece in part] for part in (out[:3], out[3:]))
 
 
 def query_block(rows):
@@ -174,23 +174,10 @@
     return embedded / (1.0 + jnp.exp(-embedded))
 
 
-def gelu(v):
-    return 0.5 * v * (1.0 + jnp.tanh(0.7978845608028654 * (v + 0.044715 * v * v * v)))
-
-
-def gelu_slope(v):
-    inner = jnp.tanh(0.7978845608028654 * (v + 0.044715 * v * v * v))
-    return 0.5 * (1.0 + inner) + 0.5 * v * (1.0 - inner * inner) * 0.7978845608028654 * (1.0 + 0.134145 * v * v)
-
-
 def normed(v):
     centred = v - jnp.mean(v, axis=-1, keepdims=True)
     r = lax.rsqrt(jnp.mean(centred * centred, axis=-1, keepdims=True) + EPSILON)
     return centred * r, r
-
-
-def matmul(a, b, dims):
-    return lax.dot_general(a, b, (dims, ((), ())), preferred_element_type=F32)
 
 
 class Ring:
@@ -226,12 +213,9 @@
         first, second = self.shift(a[:cut], b[cut:])
         return blocks, (first, second)
 
-    def scatter(self, image, text):
+    def scatter(self, image, text, first, second):
         rows, extra = image.shape[0] // self.size, text.shape[0] // self.size
-        cut = cut_of(rows + extra)
-        far = (self.size - 1) * rows
-        second = jnp.concatenate([image[far + cut :], text[(self.size - 1) * extra :]], axis=0)
-        up, down = self.shift(image[far : far + cut], second)
+        up, down = self.shift(first, second)
         half = self.size // 2
         if half == 1:
             full = jnp.concatenate([up, down], axis=0)
@@ -388,6 +372,157 @@
     return got[0], (got[1] if gate is not None else None), sums
 
 
+PARAMS = pltpu.CompilerParams(vmem_limit_bytes=58 << 20)
+
+
+def tile_of(columns):
+    return 384 if columns % 384 == 0 else columns
+
+
+def halves_of(rows):
+    step = rows // 2 if rows % 32 == 0 and rows > 512 else rows
+    return [slice(i, i + step) for i in range(0, rows, step)]
+
+
+def spread_kernel(mode, count, *refs):
+    blocks, (first, second, wi, wt), rest = refs[:count], refs[count : count + 4], refs[count + 4 :]
+    slopes, rest = (rest[:2], rest[2:]) if mode == "slope" else (None, rest)
+    ri, rt, out = rest[0], rest[1], rest[2:]
+
+    @pl.when(pl.program_id(0) == 0)
+    def _():
+        r, e, cut = ri.shape[0] // (count + 1), rt.shape[0] // (count + 1), first.shape[0]
+        for k, block in enumerate(blocks):
+            ri[k * r : (k + 1) * r, :] = block[:r, :]
+            rt[k * e : (k + 1) * e, :] = block[r:, :]
+        ri[count * r : count * r + cut, :] = first[...]
+        ri[count * r + cut :, :] = second[: r - cut, :]
+        rt[count * e :, :] = second[r - cut :, :]
+
+    for s, (rows, w) in enumerate(((ri, wi), (rt, wt))):
+        for part in halves_of(rows.shape[0]):
+            v = dot(rows[part, :], w[...], NN)
+            if mode == "gelu":
+                t = jnp.tanh(0.7978845608028654 * (v + 0.044715 * v * v * v))
+                half = 0.5 * (1.0 + t)
+                out[s][part, :] = (v * half).astype(LOW)
+                bend = 0.7978845608028654 * (1.0 + 0.134145 * v * v)
+                out[2 + s][part, :] = (half + 0.5 * v * (1.0 - t * t) * bend).astype(LOW)
+            elif mode == "slope":
+                out[s][part, :] = (v * slopes[s][part, :].astype(F32)).astype(LOW)
+            else:
+                out[s][part, :] = v.astype(LOW)
+
+
+def spread_product(mode, rows, pieces, weight, slopes=()):
+    blocks, (first, second) = pieces
+    count = len(blocks)
+    size = count + 1
+    height, depth = blocks[0].shape
+    columns = weight.shape[2]
+    tile = tile_of(columns)
+    heights = (rows * size, (height - rows) * size)
+    wide = [pl.BlockSpec((h, tile), lambda j: (0, j)) for h in heights]
+    products = 4 if mode == "gelu" else 2
+    return pl.pallas_call(
+        functools.partial(spread_kernel, mode, count),
+        grid=(columns // tile,),
+        in_specs=[whole(a) for a in (*blocks, first, second)]
+        + [pl.BlockSpec((None, depth, tile), lambda j, s=s: (s, 0, j)) for s in range(2)]
+        + (wide if slopes else []),
+        out_specs=[pl.BlockSpec((h, depth), lambda j: (0, 0)) for h in heights] + wide * (products // 2),
+        out_shape=[jax.ShapeDtypeStruct((h, depth), LOW) for h in heights]
+        + [jax.ShapeDtypeStruct((h, columns), LOW) for h in heights] * (products // 2),
+        compiler_params=PARAMS,
+        cost_estimate=pl.CostEstimate(
+            flops=2 * sum(heights) * depth * columns,
+            bytes_accessed=4 * depth * columns + 4 * sum(heights) * (depth + columns),
+            transcendentals=0,
+        ),
+        name="spread",
+    )(*blocks, first, second, weight, weight, *slopes)
+
+
+def collect_kernel(count, size, *refs):
+    xs = (refs[:count], refs[count : 2 * count])
+    ws = (refs[2 * count : 3 * count], refs[3 * count : 4 * count])
+    pi, pt, first, second = refs[4 * count :]
+    for out, x, w in zip((pi, pt), *zip(*((xs[s], ws[s]) for s in range(2)))):
+        for part in halves_of(out.shape[0]):
+            out[part, :] = sum(dot(a[part, :], b[...], NT) for a, b in zip(x, w)).astype(LOW)
+    r, e, cut = pi.shape[0] // size, pt.shape[0] // size, first.shape[0]
+    far = (size - 1) * r
+    first[...] = pi[far : far + cut, :]
+    second[: r - cut, :] = pi[far + cut :, :]
+    second[r - cut :, :] = pt[(size - 1) * e :, :]
+
+
+def collect_product(size, image, text, weight):
+    count, group = len(image), image[0].shape[1]
+    height, extra = image[0].shape[0], text[0].shape[0]
+    width = weight.shape[1]
+    tile = tile_of(width)
+    cut = cut_of((height + extra) // size)
+    rest = (height + extra) // size - cut
+    outs = (height, extra, cut, rest)
+    return pl.pallas_call(
+        functools.partial(collect_kernel, count, size),
+        grid=(width // tile,),
+        in_specs=[whole(a) for a in (*image, *text)]
+        + [pl.BlockSpec((None, tile, group), lambda j, s=s, k=k: (s, j, k)) for s in range(2) for k in range(count)],
+        out_specs=[pl.BlockSpec((h, tile), lambda j: (0, j)) for h in outs],
+        out_shape=[jax.ShapeDtypeStruct((h, width), LOW) for h in outs],
+        compiler_params=PARAMS,
+        cost_estimate=pl.CostEstimate(
+            flops=2 * (height + extra) * width * group * count,
+            bytes_accessed=4 * width * group * count + 2 * (height + extra) * (width + group * count),
+            transcendentals=0,
+        ),
+        name="collect",
+    )(*image, *text, *([weight] * (2 * count)))
+
+
+def grad_kernel(seqs, count, *refs):
+    out = refs[-1]
+    per = 2 * (1 + count)
+    for s in range(2):
+        for k in range(count):
+            total = None
+            for q in range(seqs):
+                mine = refs[q * per + s * (1 + count) : q * per + (s + 1) * (1 + count)]
+                v = dot(mine[0][...], mine[1 + k][...], TN)
+                total = v if total is None else total + v
+            columns = total.shape[1]
+            out[s, :, k * columns : (k + 1) * columns] = total.astype(LOW)
+
+
+def grad_product(pairs):
+    seqs, count = len(pairs), len(pairs[0][0][1])
+    width = pairs[0][0][0].shape[1]
+    columns = count * pairs[0][0][1][0].shape[1]
+    tile = 256 if width % 256 == 0 else width
+    arrays, specs, rows = [], [], 0
+    for pair in pairs:
+        for a, bs in pair:
+            arrays += [a, *bs]
+            specs += [pl.BlockSpec((a.shape[0], tile), lambda i: (0, i))] + [whole(b) for b in bs]
+            rows += a.shape[0]
+    return pl.pallas_call(
+        functools.partial(grad_kernel, seqs, count),
+        grid=(width // tile,),
+        in_specs=specs,
+        out_specs=pl.BlockSpec((2, tile, columns), lambda i: (0, i, 0)),
+        out_shape=jax.ShapeDtypeStruct((2, width, columns), LOW),
+        compiler_params=PARAMS,
+        cost_estimate=pl.CostEstimate(
+            flops=2 * rows * width * columns,
+            bytes_accessed=4 * width * columns + 2 * rows * (width + columns),
+            transcendentals=0,
+        ),
+        name="grad",
+    )(*arrays)
+
+
 class Step:
     def __init__(self, ring, image_rows, text_rows, keep):
         self.ring, self.image_rows, self.text_rows, self.keep = ring, image_rows, text_rows, keep
@@ -395,65 +530,59 @@
     def pick(self, modulation, member):
         return jnp.where(self.keep, modulation[0, member][None, :], modulation[1, member][None, :])
 
-    def gather(self, x):
-        blocks, (first, second) = self.ring.gather(x)
-        r = self.image_rows
-        rest = r - first.shape[0]
-        return (
-            jnp.concatenate([block[:r] for block in blocks] + [first, second[:rest]], axis=0),
-            jnp.concatenate([block[r:] for block in blocks] + [second[rest:]], axis=0),
-        )
-
-    def product(self, a, b, dims):
-        image = matmul(a[0], b[0], dims)
-        return [image, matmul(a[1], b[1], dims)]
+    def spread(self, mode, pieces, weight, slopes=()):
+        got = spread_product(mode, self.image_rows, pieces, weight, slopes)
+        return got[:2], got[2:]
+
+    def collect(self, image, text, weight):
+        if image[0].shape[1] % 128:
+            image, text = ([jnp.concatenate(a, axis=1)] for a in (image, text))
+        return collect_product(self.ring.size, image, text, weight)
 
     def start(self, x, modulation):
         return normed(x)[0] * (1.0 + self.pick(modulation, 1)) + self.pick(modulation, 0)
 
     def forward(self, x, n1, modulation, following, weights, mask, held=None):
         qkv, out, up, down = weights
-        rows1 = self.gather(n1)
-        proj = low(self.product(rows1, qkv, ((1,), (0,))))
+        pieces = self.ring.gather(n1)
+        rows1, proj = self.spread("", pieces, qkv)
         mixture, kept = attention(proj[0], proj[1], mask)
-        partial = low(self.product(mixture, out, ((1,), (1,))))
+        partial = self.collect(mixture[:1], mixture[1:], out)
         got = self.ring.scatter(*partial)
-        branch1, middle, n2 = settle(self.image_rows, 2, 3, x, *partial, *got, modulation, modulation)
-        rows2 = self.gather(n2)
+        branch1, middle, n2 = settle(self.image_rows, 2, 3, x, *partial[:2], *got, modulation, modulation)
+        pieces = self.ring.gather(n2)
+        rows2, (*act, slope_image, slope_text) = self.spread("gelu", pieces, up)
         if held is not None:
-            image, held = tie(rows2[0], held)
-            rows2 = (image, rows2[1])
-        pre = self.product(rows2, up, ((1,), (0,)))
-        act = low([gelu(p) for p in pre])
-        partial = low(self.product(act, down, ((1,), (1,))))
+            act[0], held = tie(act[0], held)
+        partial = self.collect(act[:1], act[1:], down)
         got = self.ring.scatter(*partial)
         if following is None:
-            branch2, y = settle(self.image_rows, 5, None, middle, *partial, *got, modulation, modulation)
+            branch2, y = settle(self.image_rows, 5, None, middle, *partial[:2], *got, modulation, modulation)
             n = None
         else:
-            branch2, y, n = settle(self.image_rows, 5, 0, middle, *partial, *got, modulation, following)
-        return y, n, (x, modulation, rows1, kept, mixture, branch1, middle, rows2, pre, act, branch2), held
+            branch2, y, n = settle(self.image_rows, 5, 0, middle, *partial[:2], *got, modulation, following)
+        saved = (x, modulation, rows1, kept, mixture, branch1, middle, rows2, (slope_image, slope_text), act, branch2)
+        return y, n, saved, held
 
     def backward_mlp(self, g, db2, saved, weights):
         _, _, up, down = weights
-        _, modulation, _, _, _, _, middle, rows2, pre, act, branch2 = saved
-        db2 = self.gather(db2)
-        grad_act = self.product(db2, down, ((1,), (0,)))
-        d_pre = low([grad_act[s] * gelu_slope(pre[s]) for s in range(2)])
-        partial = low(self.product(d_pre, up, ((1,), (1,))))
+        _, modulation, _, _, _, _, middle, rows2, slopes, act, branch2 = saved
+        pieces = self.ring.gather(db2)
+        db2, d_pre = self.spread("slope", pieces, down, slopes)
+        partial = self.collect(d_pre[:1], d_pre[1:], up)
         got = self.ring.scatter(*partial)
         d_middle, db1, mods = unsettle(
-            self.image_rows, 3, 2, middle, g, branch2, *partial, *got, modulation, modulation
+            self.image_rows, 3, 2, middle, g, branch2, *partial[:2], *got, modulation, modulation
         )
-        db1 = self.gather(db1)
-        return d_middle, mods, db1, (rows2, d_pre), (db2, act)
-
-    def backward_attention(self, d_middle, db1, saved, below, weights, mask):
+        pieces = self.ring.gather(db1)
+        return d_middle, mods, pieces, pair_up(rows2, d_pre), pair_up(db2, act)
+
+    def backward_attention(self, d_middle, pieces, saved, below, weights, mask):
         qkv, out, _, _ = weights
         x, modulation, rows1, kept, mixture, branch1, _, _, _, _, _ = saved
-        d_mixture = low(self.product(db1, out, ((1,), (0,))))
-        d_proj = attention_back(kept, mask, d_mixture)
-        partial = low(self.product(d_proj, qkv, ((1,), (1,))))
+        db1, d_mixture = self.spread("", pieces, out)
+        d_image, d_text = attention_back(kept, mask, d_mixture)
+        partial = self.collect(d_image, d_text, qkv)
         got = self.ring.scatter(*partial)
         g, db2, mods = unsettle(
             self.image_rows,
@@ -462,12 +591,17 @@
             x,
             d_middle,
             branch1,
-            *partial,
+            *partial[:2],
             *got,
             modulation,
             modulation if below is None else below,
         )
-        return g, db2, mods, (rows1, d_proj), (db1, mixture)
+        grouped = [(rows1[0], d_image), (rows1[1], d_text)]
+        return g, db2, mods, grouped, pair_up(db1, mixture)
+
+
+def pair_up(rows, values):
+    return [(a, [b]) for a, b in zip(rows, values)]
 
 
 def low(values):
@@ -483,10 +617,9 @@
 
 
 def weight_grads(pairs):
-    out = []
-    for s in range(2):
-        out.append(sum(matmul(a[s], b[s], ((0,), (0,))) for a, b in pairs).astype(LOW))
-    return jnp.stack(out)
+    if pairs[0][0][1][0].shape[1] % 128:
+        pairs = [[(a, [jnp.concatenate(bs, axis=1)]) for a, bs in pair] for pair in pairs]
+    return grad_product(pairs)
 
 
 def reduce_weight(total):
@@ -587,8 +720,7 @@
         grad_down = reduce_weight(down_total)
         grad_up = reduce_weight(up_total)
         if l < last:
-            (image, text), above_up, above_down = tie(db1[1], reduced[l + 1][2], reduced[l + 1][3])
-            db1[1] = (image, text)
+            db1[1], above_up, above_down = tie(db1[1], reduced[l + 1][2], reduced[l + 1][3])
             reduced[l + 1][2:] = [above_up, above_down]
         att = [
             step.backward_attention(mlp[s][0], db1[s], saved[l][s], mods[s][l - 1] if l else None, weights[l], masks[s])

time: 1830 us -> 1730 us (0.945)
  Pallas kernels: 374 us -> 845 us
  matrix products: 425 us -> 6.01 us
  local copies, waits for them, and re-layouts: 196 us -> 123 us
  other arithmetic: 91.3 us -> 37.9 us
  waiting for transfers between devices: 539 us -> 510 us
    pallas_call x0 -> x40, Pallas kernels: none -> 475 us  [the longest x16 181 us: spread_product(): pl.pallas_call(functools.partial(spread_kernel, mode, count), grid=(colum...]
    dot_general x96 -> x0, matrix products: 419 us -> none  [matmul(): return lax.dot_general(a, b, (dims, ((), ())), preferred_element_type=F32)]
    ppermute x64, waiting for transfers between devices: 282 us -> 189 us  [shift(): lax.ppermute(up, 'mp', self.up)]
    another operation x8 -> x0, other arithmetic: 47.1 us -> none  [weight_grads(): return jnp.stack(out)]
    unnamed x926 -> x434, local copies, waits for them, and re-layouts: 123 us -> 80.9 us
    reduce_scatter x8, waiting for transfers between devices: 0.01 us -> 37.3 us  [reduce_weight(): return lax.psum_scatter(total, 'dp', scatter_dimension=1, tiled=True)]
    ppermute x64, waiting for transfers between devices: 213 us -> 242 us  [shift(): lax.ppermute(down, 'mp', self.down)]
    slice x123 -> x0, local copies, waits for them, and re-layouts: 24.4 us -> none  [the longest x48 10.8 us: gather(): block[r:]]
  transfers between devices with their start and end apart: 150 -> 150, of which waited for: 63 -> 50; matrix products, arithmetic and copies ran while one was open for 34% -> 5% of each run, Pallas kernels for 20% -> 47%
where the time goes in v3:
time: 1730 us; the launch traced here: 1720 us
  Pallas kernels  845 us (49%)
  waiting for transfers between devices  510 us (29%)
  starting transfers between devices  151 us (9%)
  local copies, waits for them, and re-layouts  123 us (7%)
  other arithmetic  37.9 us (2%)
  blocking collectives  30.7 us (2%)
    ppermute x64, waiting for transfers between devices, shift(): lax.ppermute(down, 'mp', self.down)  242 us
    ppermute x64, waiting for transfers between devices, shift(): lax.ppermute(up, 'mp', self.up)  189 us
    pallas_call x16, Pallas kernels, spread_product(): pl.pallas_call(functools.partial(spread_kernel, mode, count), grid=(colum...  181 us
    pallas_call x16, Pallas kernels, collect_product(): pl.pallas_call(functools.partial(collect_kernel, count, size), grid=(widt...  167 us
    pallas_call x4, Pallas kernels, attn_bwd(): return f(mask, img, img, img, txt, txt, txt, oi, ot, li, lt, gi, gt)  134 us
    pallas_call x8, Pallas kernels, grad_product(): pl.pallas_call(functools.partial(grad_kernel, seqs, count), grid=(width /...  128 us
    pallas_call x4, Pallas kernels, attn_fwd(): return f(mask, img, img, img, txt, txt, txt)  89 us
    unnamed x434, local copies, waits for them, and re-layouts  80.9 us
  transfers between devices with their start and end apart: 150, of which 50 were waited for; matrix products, arithmetic and copies ran while one was open for 5% of the time, Pallas kernels for 47%

profile of v3, /device:TPU:0, one launch (start us, length us, event | category | flops | bytes accessed | tf_op | source)
XLA Modules:
  0.0 1720.6 jit_solution(14744275665885892933)
XLA Ops:
  89.6 18.4 %collective-permute-done.2.refs_2_ = bf16[296,1536]{1,0:T(8,128)(2,1)S(1)} collective-permute-done((bf16[296,1536]{1,0:T(8,128)(2,1)}, bf16[296,1536]{1,0:T(8,128)(2,1)S(1)}, u32[]{:S(2)}, u32[]{:S(2)}) %collective-permute-start.2) | collective-permute-done | bytes 909344 | tf_op jit(solution)/shard_map/ppermute | solution.py:205
  150.0 22.2 %attn_fwd.4 = (bf16[1024,384]{1,0:T(8,128)(2,1)}, bf16[160,384]{1,0:T(8,128)(2,1)}, f32[1024,384]{1,0:T(8,128)}, f32[160,384]{1,0:T(8,128)}) custom-call(s32[8,160]{1,0:T(8,128)} %broadcast_in_dim.179.mask_ref, bf16[1024,1152]{1,0:T(8,128)(2,1)} %get-tuple-element.275.qi.ki.vi, bf16[1024,1152]{1,0:T(8,128)(2,1)} %get-tuple-element.275.qi.ki.vi, ...), custom_call_target="tpu_custom_call" | custom-call | flops 2153250816 | bytes 5455872 | tf_op jit(solution)/shard_map/attn_fwd/pallas_call | solution.py:77
  190.9 22.2 %attn_fwd.6 = (bf16[1024,384]{1,0:T(8,128)(2,1)}, bf16[160,384]{1,0:T(8,128)(2,1)}, f32[1024,384]{1,0:T(8,128)}, f32[160,384]{1,0:T(8,128)}) custom-call(s32[8,160]{1,0:T(8,128)} %broadcast_in_dim.194.mask_ref, bf16[1024,1152]{1,0:T(8,128)(2,1)} %get-tuple-element.319.qi.ki.vi, bf16[1024,1152]{1,0:T(8,128)(2,1)} %get-tuple-element.319.qi.ki.vi, ...), custom_call_target="tpu_custom_call" | custom-call | flops 2153250816 | bytes 5455872 | tf_op jit(solution)/shard_map/attn_fwd/pallas_call | solution.py:77
  227.3 23.3 %collective-permute-done.38.refs_3_ = bf16[144,1536]{1,0:T(8,128)(2,1)S(1)} collective-permute-done((bf16[144,1536]{1,0:T(8,128)(2,1)S(1)}, bf16[144,1536]{1,0:T(8,128)(2,1)S(1)}, u32[]{:S(2)}, u32[]{:S(2)}) %collective-permute-start.38) | collective-permute-done | bytes 442400 | tf_op jit(solution)/shard_map/ppermute | solution.py:205
  392.5 22.1 %collective-permute-done.46.refs_3_ = bf16[144,1536]{1,0:T(8,128)(2,1)S(1)} collective-permute-done((bf16[144,1536]{1,0:T(8,128)(2,1)S(1)}, bf16[144,1536]{1,0:T(8,128)(2,1)S(1)}, u32[]{:S(2)}, u32[]{:S(2)}) %collective-permute-start.46) | collective-permute-done | bytes 442400 | tf_op jit(solution)/shard_map/ppermute | solution.py:205
  491.4 22.3 %attn_fwd.5 = (bf16[1024,384]{1,0:T(8,128)(2,1)}, bf16[160,384]{1,0:T(8,128)(2,1)}, f32[1024,384]{1,0:T(8,128)}, f32[160,384]{1,0:T(8,128)}) custom-call(s32[8,160]{1,0:T(8,128)} %broadcast_in_dim.179.mask_ref, bf16[1024,1152]{1,0:T(8,128)(2,1)} %get-tuple-element.298.qi.ki.vi, bf16[1024,1152]{1,0:T(8,128)(2,1)} %get-tuple-element.298.qi.ki.vi, ...), custom_call_target="tpu_custom_call" | custom-call | flops 2153250816 | bytes 5455872 | tf_op jit(solution)/shard_map/attn_fwd/pallas_call | solution.py:77
  532.1 22.3 %attn_fwd.7 = (bf16[1024,384]{1,0:T(8,128)(2,1)}, bf16[160,384]{1,0:T(8,128)(2,1)}, f32[1024,384]{1,0:T(8,128)}, f32[160,384]{1,0:T(8,128)}) custom-call(s32[8,160]{1,0:T(8,128)} %broadcast_in_dim.194.mask_ref, bf16[1024,1152]{1,0:T(8,128)(2,1)} %get-tuple-element.342.qi.ki.vi, bf16[1024,1152]{1,0:T(8,128)(2,1)} %get-tuple-element.342.qi.ki.vi, ...), custom_call_target="tpu_custom_call" | custom-call | flops 2153250816 | bytes 5455872 | tf_op jit(solution)/shard_map/attn_fwd/pallas_call | solution.py:77
  568.8 28.2 %collective-permute-done.54.refs_3_ = bf16[144,1536]{1,0:T(8,128)(2,1)S(1)} collective-permute-done((bf16[144,1536]{1,0:T(8,128)(2,1)S(1)}, bf16[144,1536]{1,0:T(8,128)(2,1)S(1)}, u32[]{:S(2)}, u32[]{:S(2)}) %collective-permute-start.54) | collective-permute-done | bytes 442400 | tf_op jit(solution)/shard_map/ppermute | solution.py:205
  647.8 17.5 %collective-permute-done.27.refs_2_ = bf16[296,1536]{1,0:T(8,128)(2,1)S(1)} collective-permute-done((bf16[296,1536]{1,0:T(8,128)(2,1)S(1)}, bf16[296,1536]{1,0:T(8,128)(2,1)S(1)}, u32[]{:S(2)}, u32[]{:S(2)}) %collective-permute-start.27) | collective-permute-done | bytes 909344 | tf_op jit(solution)/shard_map/ppermute | solution.py:205
  667.5 17.3 %collective-permute-done.100.refs_2_ = bf16[296,1536]{1,0:T(8,128)(2,1)S(1)} collective-permute-done((bf16[296,1536]{1,0:T(8,128)(2,1)S(1)}, bf16[296,1536]{1,0:T(8,128)(2,1)S(1)}, u32[]{:S(2)}, u32[]{:S(2)}) %collective-permute-start.100) | collective-permute-done | bytes 909344 | tf_op jit(solution)/shard_map/ppermute | solution.py:205
  767.6 18.3 %grad.11 = bf16[2,1536,1536]{2,1,0:T(8,128)(2,1)} custom-call(bf16[1024,1536]{1,0:T(8,128)(2,1)} %get-tuple-element.489.refs_0_, bf16[1024,1536]{1,0:T(8,128)(2,1)} %get-tuple-element.310.refs_0_.refs_1_, bf16[160,1536]{1,0:T(8,128)(2,1)} %get-tuple-element.490.refs_2_, bf16[160,1536]{1,0:T(8,128)(2,1)} %get-tuple-element.311.refs_1_.refs_3_, ...), custom_call_target="tpu_custom_call" | custom-call | flops 11173625856 | bytes 23986176 | tf_op jit(solution)/shard_map/grad/pallas_call | solution.py:510
  786.0 18.4 %grad.10 = bf16[2,1536,1536]{2,1,0:T(8,128)(2,1)} custom-call(bf16[1024,1536]{1,0:T(8,128)(2,1)} %get-tuple-element.485.refs_0_, bf16[1024,1536]{1,0:T(8,128)(2,1)} %get-tuple-element.367.refs_0_.refs_1_, bf16[160,1536]{1,0:T(8,128)(2,1)} %get-tuple-element.486.refs_2_, bf16[160,1536]{1,0:T(8,128)(2,1)} %get-tuple-element.368.refs_1_.refs_3_, ...), custom_call_target="tpu_custom_call" | custom-call | flops 11173625856 | bytes 23986176 | tf_op jit(solution)/shard_map/grad/pallas_call | solution.py:510
  882.0 25.0 %collective-permute-done.72.refs_4_ = bf16[152,1536]{1,0:T(8,128)(2,1)S(1)} collective-permute-done((bf16[152,1536]{1,0:T(8,128)(2,1)}, bf16[152,1536]{1,0:T(8,128)(2,1)S(1)}, u32[]{:S(2)}, u32[]{:S(2)}) %collective-permute-start.72) | collective-permute-done | bytes 466976 | tf_op jit(solution)/shard_map/ppermute | solution.py:205
  999.9 33.6 %attn_bwd.6 = (bf16[1024,384]{1,0:T(8,128)(2,1)}, bf16[1024,384]{1,0:T(8,128)(2,1)}, bf16[1024,384]{1,0:T(8,128)(2,1)}, bf16[160,384]{1,0:T(8,128)(2,1)}, bf16[1...) custom-call(s32[160,128]{1,0:T(8,128)} %broadcast_in_dim.208.mask_ref, bf16[1024,1152]{1,0:T(8,128)(2,1)} %get-tuple-element.342.qi.ki.vi, ...), custom_call_target="tpu_custom_call" | custom-call | flops 5383127040 | bytes 11821056 | tf_op jit(solution)/shard_map/attn_bwd/pallas_call | solution.py:142
  1055.2 33.6 %attn_bwd.4 = (bf16[1024,384]{1,0:T(8,128)(2,1)}, bf16[1024,384]{1,0:T(8,128)(2,1)}, bf16[1024,384]{1,0:T(8,128)(2,1)}, bf16[160,384]{1,0:T(8,128)(2,1)}, bf16[1...) custom-call(s32[160,128]{1,0:T(8,128)} %broadcast_in_dim.207.mask_ref, bf16[1024,1152]{1,0:T(8,128)(2,1)} %get-tuple-element.298.qi.ki.vi, ...), custom_call_target="tpu_custom_call" | custom-call | flops 5383127040 | bytes 11821056 | tf_op jit(solution)/shard_map/attn_bwd/pallas_call | solution.py:142
  1104.2 18.0 %grad.9 = bf16[2,1536,1152]{2,1,0:T(8,128)(2,1)} custom-call(bf16[1024,1536]{1,0:T(8,128)(2,1)} %get-tuple-element.465.refs_0_, bf16[1024,384]{1,0:T(8,128)(2,1)} %get-tuple-element.382.refs_0_.refs_1_, bf16[1024,384]{1,0:T(8,128)(2,1)} %get-tuple-element.383.refs_1_.refs_2_, bf16[1024,384]{1,0:T(8,128)(2,1)} %get-tuple-element.384.refs_2_.refs_3_, ...), custom_call_target="tpu_custom_call" | custom-call | flops 8380219392 | bytes 19808256 | tf_op jit(solution)/shard_map/grad/pallas_call | solution.py:510
  1170.0 21.1 %collective-permute-done.81.up = bf16[296,1536]{1,0:T(8,128)(2,1)S(1)} collective-permute-done((bf16[296,1536]{1,0:T(8,128)(2,1)}, bf16[296,1536]{1,0:T(8,128)(2,1)S(1)}, u32[]{:S(2)}, u32[]{:S(2)}) %collective-permute-start.81) | collective-permute-done | bytes 909344 | tf_op jit(solution)/shard_map/ppermute | solution.py:205
  1390.5 18.5 %grad.14 = bf16[2,1536,1536]{2,1,0:T(8,128)(2,1)} custom-call(bf16[1024,1536]{1,0:T(8,128)(2,1)} %get-tuple-element.531.refs_0_, bf16[1024,1536]{1,0:T(8,128)(2,1)} %get-tuple-element.399.refs_0_.refs_1_, bf16[160,1536]{1,0:T(8,128)(2,1)} %get-tuple-element.532.refs_2_, bf16[160,1536]{1,0:T(8,128)(2,1)} %get-tuple-element.400.refs_1_.refs_3_, ...), custom_call_target="tpu_custom_call" | custom-call | flops 11173625856 | bytes 23986176 | tf_op jit(solution)/shard_map/grad/pallas_call | solution.py:510
  1409.1 18.5 %grad.15 = bf16[2,1536,1536]{2,1,0:T(8,128)(2,1)} custom-call(bf16[1024,1536]{1,0:T(8,128)(2,1)} %get-tuple-element.536.refs_0_, bf16[1024,1536]{1,0:T(8,128)(2,1)} %get-tuple-element.288.refs_0_.refs_1_, bf16[160,1536]{1,0:T(8,128)(2,1)} %get-tuple-element.537.refs_2_, bf16[160,1536]{1,0:T(8,128)(2,1)} %get-tuple-element.289.refs_1_.refs_3_, ...), custom_call_target="tpu_custom_call" | custom-call | flops 11173625856 | bytes 23986176 | tf_op jit(solution)/shard_map/grad/pallas_call | solution.py:510
  1427.9 33.6 %attn_bwd.5 = (bf16[1024,384]{1,0:T(8,128)(2,1)}, bf16[1024,384]{1,0:T(8,128)(2,1)}, bf16[1024,384]{1,0:T(8,128)(2,1)}, bf16[160,384]{1,0:T(8,128)(2,1)}, bf16[1...) custom-call(s32[160,128]{1,0:T(8,128)} %broadcast_in_dim.207.mask_ref, bf16[1024,1152]{1,0:T(8,128)(2,1)} %get-tuple-element.275.qi.ki.vi, ...), custom_call_target="tpu_custom_call" | custom-call | flops 5383127040 | bytes 11821056 | tf_op jit(solution)/shard_map/attn_bwd/pallas_call | solution.py:142
  1461.5 33.7 %attn_bwd.7 = (bf16[1024,384]{1,0:T(8,128)(2,1)}, bf16[1024,384]{1,0:T(8,128)(2,1)}, bf16[1024,384]{1,0:T(8,128)(2,1)}, bf16[160,384]{1,0:T(8,128)(2,1)}, bf16[1...) custom-call(s32[160,128]{1,0:T(8,128)} %broadcast_in_dim.208.mask_ref, bf16[1024,1152]{1,0:T(8,128)(2,1)} %get-tuple-element.319.qi.ki.vi, ...), custom_call_target="tpu_custom_call" | custom-call | flops 5383127040 | bytes 11821056 | tf_op jit(solution)/shard_map/attn_bwd/pallas_call | solution.py:142
  1495.1 18.0 %grad.12 = bf16[2,1536,1152]{2,1,0:T(8,128)(2,1)} custom-call(bf16[1024,1536]{1,0:T(8,128)(2,1)} %get-tuple-element.521.refs_0_, bf16[1024,384]{1,0:T(8,128)(2,1)} %get-tuple-element.414.refs_0_.refs_1_, bf16[1024,384]{1,0:T(8,128)(2,1)} %get-tuple-element.415.refs_1_.refs_2_, bf16[1024,384]{1,0:T(8,128)(2,1)} %get-tuple-element.416.refs_2_.refs_3_, ...), custom_call_target="tpu_custom_call" | custom-call | flops 8380219392 | bytes 19808256 | tf_op jit(solution)/shard_map/grad/pallas_call | solution.py:510
  1631.8 17.6 %all-gather.3 = f32[384,384]{1,0:T(8,128)S(1)} all-gather(f32[48,384]{1,0:T(8,128)S(1)} %reduce_sum.59), channel_id=5, replica_groups=mesh['dp'=8,'mp'=4] {'dp'}, dimensions={0}, use_global_device_ids=true | all-gather | bytes 663552 | tf_op jit(solution)/shard_map/all_gather | solution.py:743
  1669.7 37.3 %reduce-scatter.13.cloned.1.call-done = bf16[2,192,1152]{2,1,0:T(8,128)(2,1)} async-done(((bf16[2,1536,1152]{2,1,0:T(8,128)(2,1)}), bf16[2,192,1152]{2,1,0:T(8,128)(2,1)}) %reduce-scatter.13.cloned.1.call-update) | async-done | bytes 884752 | tf_op jit(solution)/shard_map/reduce_scatter | solution.py:626
  (933 shorter events, 1143.5 us)
Async XLA Ops:
  7.2 131.3 %all-gather.13.cloned.1.call-start = ((), (), s32[]{:S(2)}) async-start(), calls=%async_computation.10 | async-start | bytes 7962624 | tf_op jit(solution)/shard_map/all_gather | solution.py:616
  10.9 161.3 %all-gather.15.cloned.1.call-start = ((), (), s32[]{:S(2)}) async-start(), calls=%async_computation.11 | async-start | bytes 2654208 | tf_op jit(solution)/shard_map/all_gather | solution.py:616
  13.0 313.6 %all-gather.25.cloned.1.call-start = ((), (), s32[]{:S(2)}) async-start(), calls=%async_computation.24 | async-start | bytes 10616832 | tf_op jit(solution)/shard_map/all_gather | solution.py:616
  16.2 326.0 %all-gather.17.cloned.1.call-start = ((), (), s32[]{:S(2)}) async-start(), calls=%async_computation.12 | async-start | bytes 10616832 | tf_op jit(solution)/shard_map/all_gather | solution.py:616
  19.5 459.9 %all-gather.19.cloned.1.call-start = ((), (), s32[]{:S(2)}) async-start(), calls=%async_computation.13 | async-start | bytes 7962624 | tf_op jit(solution)/shard_map/all_gather | solution.py:616
  21.8 491.9 %all-gather.21.cloned.1.call-start = ((), (), s32[]{:S(2)}) async-start(), calls=%async_computation.14 | async-start | bytes 2654208 | tf_op jit(solution)/shard_map/all_gather | solution.py:616
  22.4 685.3 %all-gather.27.cloned.1.call-start = ((), (), s32[]{:S(2)}) async-start(), calls=%async_computation.25 | async-start | bytes 10616832 | tf_op jit(solution)/shard_map/all_gather | solution.py:616
  31.7 708.7 %all-gather.23.cloned.1.call-start = ((), (), s32[]{:S(2)}) async-start(), calls=%async_computation.15 | async-start | bytes 10616832 | tf_op jit(solution)/shard_map/all_gather | solution.py:616
  38.6 1336.2 %reduce-scatter.11.cloned.1.call-start = ((), (), s32[]{:S(2)}) async-start(), calls=%async_computation.17 | async-start | bytes 10616832 | tf_op jit(solution)/shard_map/reduce_scatter | solution.py:626
  128.3 52.0 %collective-permute-start.37 = (bf16[152,1536]{1,0:T(8,128)(2,1)}, bf16[152,1536]{1,0:T(8,128)(2,1)}, u32[]{:S(2)}, u32[]{:S(2)}) collective-permute-start(bf16[152,1536]{1,0:T(8,128)(2,1)} %slice.362), channel_id=1, source_target_pairs={{0,2},{1,0},{3,1},{2,3},{4,6},{5,4},{7,5},{6,7},{8,10},{9,8},{11,9... | collective-permute-start | bytes 1400840 | tf_op jit(solution)/shard_map/ppermute | solution.py:205
  626.3 58.5 %collective-permute-start.100 = (bf16[296,1536]{1,0:T(8,128)(2,1)S(1)}, bf16[296,1536]{1,0:T(8,128)(2,1)S(1)}, u32[]{:S(2)}, u32[]{:S(2)}) collective-permute-start(bf16[296,1536]{1,0:T(8,128)(2,1)S(1)} %copy-done.117), channel_id=1, source_target_pairs={{0,2},{1,0},{3,1},{2,3},{4,6},{5,4},{7,5},{6,7},{8,10},{9,8},{11,9... | collective-permute-start | bytes 2727944 | tf_op jit(solution)/shard_map/ppermute | solution.py:205
  688.9 51.5 %collective-permute-start.70 = (bf16[152,1536]{1,0:T(8,128)(2,1)}, bf16[152,1536]{1,0:T(8,128)(2,1)}, u32[]{:S(2)}, u32[]{:S(2)}) collective-permute-start(bf16[152,1536]{1,0:T(8,128)(2,1)} %slice.377), channel_id=1, source_target_pairs={{0,2},{1,0},{3,1},{2,3},{4,6},{5,4},{7,5},{6,7},{8,10},{9,8},{11,9... | collective-permute-start | bytes 1400840 | tf_op jit(solution)/shard_map/ppermute | solution.py:205
  699.5 54.4 %collective-permute-start.102 = (bf16[152,1536]{1,0:T(8,128)(2,1)}, bf16[152,1536]{1,0:T(8,128)(2,1)S(1)}, u32[]{:S(2)}, u32[]{:S(2)}) collective-permute-start(bf16[152,1536]{1,0:T(8,128)(2,1)} %slice.385), channel_id=1, source_target_pairs={{0,2},{1,0},{3,1},{2,3},{4,6},{5,4},{7,5},{6,7},{8,10},{9,8},{11,9... | collective-permute-start | bytes 1400840 | tf_op jit(solution)/shard_map/ppermute | solution.py:205
  786.0 588.8 %reduce-scatter.9.cloned.1.call-start = ((), (), s32[]{:S(2)}) async-start(), calls=%async_computation.16 | async-start | bytes 10616832 | tf_op jit(solution)/shard_map/reduce_scatter | solution.py:626
  804.5 808.1 %reduce-scatter.15.cloned.1.call-start = ((), (), s32[]{:S(2)}) async-start(), calls=%async_computation.19 | async-start | bytes 7962624 | tf_op jit(solution)/shard_map/reduce_scatter | solution.py:626
  816.9 55.0 %collective-permute-start.71 = (bf16[144,1536]{1,0:T(8,128)(2,1)}, bf16[144,1536]{1,0:T(8,128)(2,1)S(1)}, u32[]{:S(2)}, u32[]{:S(2)}) collective-permute-start(bf16[144,1536]{1,0:T(8,128)(2,1)} %get-tuple-element.371), channel_id=1, source_target_pairs={{0,1},{1,3},{3,2},{2,0},{4,5},{5,7},{7,6},{6,4},{8,9},{9,11},{11,1... | collective-permute-start | bytes 1327112 | tf_op jit(solution)/shard_map/ppermute | solution.py:205
  914.7 50.9 %collective-permute-start.74 = (bf16[296,1536]{1,0:T(8,128)(2,1)}, bf16[296,1536]{1,0:T(8,128)(2,1)}, u32[]{:S(2)}, u32[]{:S(2)}) collective-permute-start(bf16[296,1536]{1,0:T(8,128)(2,1)} %get-tuple-element.374), channel_id=1, source_target_pairs={{0,2},{1,0},{3,1},{2,3},{4,6},{5,4},{7,5},{6,7},{8,10},{9,8},{11,9... | collective-permute-start | bytes 2727944 | tf_op jit(solution)/shard_map/ppermute | solution.py:205
  986.3 60.9 %collective-permute-start.78 = (bf16[152,1536]{1,0:T(8,128)(2,1)S(1)}, bf16[152,1536]{1,0:T(8,128)(2,1)S(1)}, u32[]{:S(2)}, u32[]{:S(2)}) collective-permute-start(bf16[152,1536]{1,0:T(8,128)(2,1)S(1)} %slice.379), channel_id=1, source_target_pairs={{0,2},{1,0},{3,1},{2,3},{4,6},{5,4},{7,5},{6,7},{8,10},{9,8},{11,9... | collective-permute-start | bytes 1400840 | tf_op jit(solution)/shard_map/ppermute | solution.py:205
  987.3 59.9 %collective-permute-start.77 = (bf16[144,1536]{1,0:T(8,128)(2,1)S(1)}, bf16[144,1536]{1,0:T(8,128)(2,1)}, u32[]{:S(2)}, u32[]{:S(2)}) collective-permute-start(bf16[144,1536]{1,0:T(8,128)(2,1)S(1)} %slice.378), channel_id=1, source_target_pairs={{0,1},{1,3},{3,2},{2,0},{4,5},{5,7},{7,6},{6,4},{8,9},{9,11},{11,1... | collective-permute-start | bytes 1327112 | tf_op jit(solution)/shard_map/ppermute | solution.py:205
  1137.9 521.9 %reduce-scatter.19.cloned.1.call-start = ((), (), s32[]{:S(2)}) async-start(), calls=%async_computation.21 | async-start | bytes 2654208 | tf_op jit(solution)/shard_map/reduce_scatter | solution.py:626
  1222.7 437.1 %reduce-scatter.17.cloned.1.call-start = ((), (), s32[]{:S(2)}) async-start(), calls=%async_computation.20 | async-start | bytes 2654208 | tf_op jit(solution)/shard_map/reduce_scatter | solution.py:626
  1390.5 271.6 %reduce-scatter.21.cloned.1.call-start = ((), (), s32[]{:S(2)}) async-start(), calls=%async_computation.22 | async-start | bytes 10616832 | tf_op jit(solution)/shard_map/reduce_scatter | solution.py:626
  1409.1 256.8 %reduce-scatter.23.cloned.1.call-start = ((), (), s32[]{:S(2)}) async-start(), calls=%async_computation.23 | async-start | bytes 10616832 | tf_op jit(solution)/shard_map/reduce_scatter | solution.py:626
  1427.6 279.3 %reduce-scatter.13.cloned.1.call-start = ((), (), s32[]{:S(2)}) async-start(), calls=%async_computation.18 | async-start | bytes 7962624 | tf_op jit(solution)/shard_map/reduce_scatter | solution.py:626
  (342 other events, 5856.9 us)
Sparse Core Ops, SparseCore 0:
  11.1 86.3 all-gather.12
  99.0 29.9 all-gather.14
  131.2 89.9 all-gather.24
  223.2 89.1 all-gather.16
  313.8 69.5 all-gather.18
  385.0 30.0 all-gather.20
  417.2 89.9 all-gather.26
  508.8 89.1 all-gather.22
  786.1 96.9 reduce-scatter.10
  885.2 97.8 reduce-scatter.8
  1138.0 74.6 reduce-scatter.14
  1222.8 34.6 reduce-scatter.18
  1390.6 33.9 reduce-scatter.16
  1426.8 98.2 reduce-scatter.20
  1527.2 97.8 reduce-scatter.22
  1627.3 79.5 reduce-scatter.12

commit v4 on v3

--- a/solution.py
+++ b/solution.py
@@ -542,7 +542,7 @@
     def start(self, x, modulation):
         return normed(x)[0] * (1.0 + self.pick(modulation, 1)) + self.pick(modulation, 0)
 
-    def forward(self, x, n1, modulation, following, weights, mask, held=None):
+    def forward(self, x, n1, modulation, following, weights, mask):
         qkv, out, up, down = weights
         pieces = self.ring.gather(n1)
         rows1, proj = self.spread("", pieces, qkv)
@@ -552,8 +552,6 @@
         branch1, middle, n2 = settle(self.image_rows, 2, 3, x, *partial[:2], *got, modulation, modulation)
         pieces = self.ring.gather(n2)
         rows2, (*act, slope_image, slope_text) = self.spread("gelu", pieces, up)
-        if held is not None:
-            act[0], held = tie(act[0], held)
         partial = self.collect(act[:1], act[1:], down)
         got = self.ring.scatter(*partial)
         if following is None:
@@ -562,7 +560,7 @@
         else:
             branch2, y, n = settle(self.image_rows, 5, 0, middle, *partial[:2], *got, modulation, following)
         saved = (x, modulation, rows1, kept, mixture, branch1, middle, rows2, (slope_image, slope_text), act, branch2)
-        return y, n, saved, held
+        return y, n, saved
 
     def backward_mlp(self, g, db2, saved, weights):
         _, _, up, down = weights
@@ -701,14 +699,9 @@
     last = LAYERS - 1
     db2 = [low([step.pick(mods[s][last], 5) * upstream[s]])[0] for s in range(seqs)]
     for l in range(LAYERS):
-        done = [
-            step.forward(rows[s], ready[s], mods[s][l], mods[s][l + 1], weights[l], masks[s], None if l else db2[s])
-            for s in range(seqs)
-        ]
+        done = [step.forward(rows[s], ready[s], mods[s][l], mods[s][l + 1], weights[l], masks[s]) for s in range(seqs)]
         rows, ready = [d[0] for d in done], [d[1] for d in done]
         saved.append([d[2] for d in done])
-        if l == 0:
-            db2 = [d[3] for d in done]
     image_output, text_output = undeal(rows)
 
     reduced, mod_rows = [None] * LAYERS, [None] * LAYERS
@@ -720,8 +713,7 @@
         grad_down = reduce_weight(down_total)
         grad_up = reduce_weight(up_total)
         if l < last:
-            db1[1], above_up, above_down = tie(db1[1], reduced[l + 1][2], reduced[l + 1][3])
-            reduced[l + 1][2:] = [above_up, above_down]
+            db1[0], reduced[l + 1] = tie(db1[0], reduced[l + 1])
         att = [
             step.backward_attention(mlp[s][0], db1[s], saved[l][s], mods[s][l - 1] if l else None, weights[l], masks[s])
             for s in range(seqs)

time: 1730 us -> 1760 us (1.017)
  waiting for transfers between devices: 510 us -> 548 us
    reduce_scatter x8, waiting for transfers between devices: 37.3 us -> 83 us  [reduce_weight(): return lax.psum_scatter(total, 'dp', scatter_dimension=1, tiled=True)]
    all_to_all x2, waiting for transfers between devices: 23.4 us -> 50.1 us  [exchange_sum(): lax.all_to_all(parts, axis, split_axis=0, concat_axis=0, tiled=True)]
    ppermute x64, waiting for transfers between devices: 242 us -> 215 us  [shift(): lax.ppermute(down, 'mp', self.down)]
    unnamed x434 -> x454, local copies, waits for them, and re-layouts: 80.9 us -> 78.8 us
  transfers between devices with their start and end apart: 150 -> 150, of which waited for: 50 -> 54; matrix products, arithmetic and copies ran while one was open for 5% -> 5% of each run, Pallas kernels for 47% -> 47%
where the time goes in v4:
time: 1760 us; the launch traced here: 1750 us
  Pallas kernels  844 us (48%)
  waiting for transfers between devices  548 us (31%)
  starting transfers between devices  148 us (8%)
  local copies, waits for them, and re-layouts  119 us (7%)
  other arithmetic  39.1 us (2%)
  blocking collectives  29.2 us (2%)
    ppermute x64, waiting for transfers between devices, shift(): lax.ppermute(down, 'mp', self.down)  215 us
    ppermute x64, waiting for transfers between devices, shift(): lax.ppermute(up, 'mp', self.up)  187 us
    pallas_call x16, Pallas kernels, spread_product(): pl.pallas_call(functools.partial(spread_kernel, mode, count), grid=(colum...  181 us
    pallas_call x16, Pallas kernels, collect_product(): pl.pallas_call(functools.partial(collect_kernel, count, size), grid=(widt...  166 us
    pallas_call x4, Pallas kernels, attn_bwd(): return f(mask, img, img, img, txt, txt, txt, oi, ot, li, lt, gi, gt)  134 us
    pallas_call x8, Pallas kernels, grad_product(): pl.pallas_call(functools.partial(grad_kernel, seqs, count), grid=(width /...  128 us
    pallas_call x4, Pallas kernels, attn_fwd(): return f(mask, img, img, img, txt, txt, txt)  89.2 us
    reduce_scatter x8, waiting for transfers between devices, reduce_weight(): return lax.psum_scatter(total, 'dp', scatter_dimension=1, tiled=True)  83 us
  transfers between devices with their start and end apart: 150, of which 54 were waited for; matrix products, arithmetic and copies ran while one was open for 5% of the time, Pallas kernels for 47%

profile of v4, /device:TPU:0, one launch (start us, length us, event | category | flops | bytes accessed | tf_op | source)
XLA Modules:
  0.0 1750.1 jit_solution(1083319289879574309)
XLA Ops:
  149.0 22.2 %attn_fwd.6 = (bf16[1024,384]{1,0:T(8,128)(2,1)}, bf16[160,384]{1,0:T(8,128)(2,1)}, f32[1024,384]{1,0:T(8,128)}, f32[160,384]{1,0:T(8,128)}) custom-call(s32[8,160]{1,0:T(8,128)} %broadcast_in_dim.190.mask_ref, bf16[1024,1152]{1,0:T(8,128)(2,1)} %get-tuple-element.316.qi.ki.vi, bf16[1024,1152]{1,0:T(8,128)(2,1)} %get-tuple-element.316.qi.ki.vi, ...), custom_call_target="tpu_custom_call" | custom-call | flops 2153250816 | bytes 5455872 | tf_op jit(solution)/shard_map/attn_fwd/pallas_call | solution.py:77
  189.9 22.3 %attn_fwd.4 = (bf16[1024,384]{1,0:T(8,128)(2,1)}, bf16[160,384]{1,0:T(8,128)(2,1)}, f32[1024,384]{1,0:T(8,128)}, f32[160,384]{1,0:T(8,128)}) custom-call(s32[8,160]{1,0:T(8,128)} %broadcast_in_dim.179.mask_ref, bf16[1024,1152]{1,0:T(8,128)(2,1)} %get-tuple-element.273.qi.ki.vi, bf16[1024,1152]{1,0:T(8,128)(2,1)} %get-tuple-element.273.qi.ki.vi, ...), custom_call_target="tpu_custom_call" | custom-call | flops 2153250816 | bytes 5455872 | tf_op jit(solution)/shard_map/attn_fwd/pallas_call | solution.py:77
  226.5 22.8 %collective-permute-done.5.refs_3_ = bf16[144,1536]{1,0:T(8,128)(2,1)S(1)} collective-permute-done((bf16[144,1536]{1,0:T(8,128)(2,1)S(1)}, bf16[144,1536]{1,0:T(8,128)(2,1)S(1)}, u32[]{:S(2)}, u32[]{:S(2)}) %collective-permute-start.5) | collective-permute-done | bytes 442400 | tf_op jit(solution)/shard_map/ppermute | solution.py:205
  389.9 22.0 %collective-permute-done.13.refs_3_ = bf16[144,1536]{1,0:T(8,128)(2,1)S(1)} collective-permute-done((bf16[144,1536]{1,0:T(8,128)(2,1)S(1)}, bf16[144,1536]{1,0:T(8,128)(2,1)S(1)}, u32[]{:S(2)}, u32[]{:S(2)}) %collective-permute-start.13) | collective-permute-done | bytes 442400 | tf_op jit(solution)/shard_map/ppermute | solution.py:205
  487.9 22.3 %attn_fwd.7 = (bf16[1024,384]{1,0:T(8,128)(2,1)}, bf16[160,384]{1,0:T(8,128)(2,1)}, f32[1024,384]{1,0:T(8,128)}, f32[160,384]{1,0:T(8,128)}) custom-call(s32[8,160]{1,0:T(8,128)} %broadcast_in_dim.190.mask_ref, bf16[1024,1152]{1,0:T(8,128)(2,1)} %get-tuple-element.338.qi.ki.vi, bf16[1024,1152]{1,0:T(8,128)(2,1)} %get-tuple-element.338.qi.ki.vi, ...), custom_call_target="tpu_custom_call" | custom-call | flops 2153250816 | bytes 5455872 | tf_op jit(solution)/shard_map/attn_fwd/pallas_call | solution.py:77
  528.4 22.4 %attn_fwd.5 = (bf16[1024,384]{1,0:T(8,128)(2,1)}, bf16[160,384]{1,0:T(8,128)(2,1)}, f32[1024,384]{1,0:T(8,128)}, f32[160,384]{1,0:T(8,128)}) custom-call(s32[8,160]{1,0:T(8,128)} %broadcast_in_dim.179.mask_ref, bf16[1024,1152]{1,0:T(8,128)(2,1)} %get-tuple-element.295.qi.ki.vi, bf16[1024,1152]{1,0:T(8,128)(2,1)} %get-tuple-element.295.qi.ki.vi, ...), custom_call_target="tpu_custom_call" | custom-call | flops 2153250816 | bytes 5455872 | tf_op jit(solution)/shard_map/attn_fwd/pallas_call | solution.py:77
  565.0 29.7 %collective-permute-done.21.refs_3_ = bf16[144,1536]{1,0:T(8,128)(2,1)S(1)} collective-permute-done((bf16[144,1536]{1,0:T(8,128)(2,1)S(1)}, bf16[144,1536]{1,0:T(8,128)(2,1)S(1)}, u32[]{:S(2)}, u32[]{:S(2)}) %collective-permute-start.21) | collective-permute-done | bytes 442400 | tf_op jit(solution)/shard_map/ppermute | solution.py:205
  644.3 17.5 collective-permute-done.58.refs_2_
  664.0 17.3 collective-permute-done.68.refs_2_
  835.6 26.0 %collective-permute-done.72.refs_4_ = bf16[152,1536]{1,0:T(8,128)(2,1)S(1)} collective-permute-done((bf16[152,1536]{1,0:T(8,128)(2,1)S(1)}, bf16[152,1536]{1,0:T(8,128)(2,1)S(1)}, u32[]{:S(2)}, u32[]{:S(2)}) %collective-permute-start.72) | collective-permute-done | bytes 466976 | tf_op jit(solution)/shard_map/ppermute | solution.py:205
  948.4 33.6 %attn_bwd.5 = (bf16[1024,384]{1,0:T(8,128)(2,1)}, bf16[1024,384]{1,0:T(8,128)(2,1)}, bf16[1024,384]{1,0:T(8,128)(2,1)}, bf16[160,384]{1,0:T(8,128)(2,1)}, bf16[1...) custom-call(s32[160,128]{1,0:T(8,128)} %broadcast_in_dim.208.mask_ref, bf16[1024,1152]{1,0:T(8,128)(2,1)} %get-tuple-element.338.qi.ki.vi, ...), custom_call_target="tpu_custom_call" | custom-call | flops 5383127040 | bytes 11821056 | tf_op jit(solution)/shard_map/attn_bwd/pallas_call | solution.py:142
  1003.4 33.6 %attn_bwd.4 = (bf16[1024,384]{1,0:T(8,128)(2,1)}, bf16[1024,384]{1,0:T(8,128)(2,1)}, bf16[1024,384]{1,0:T(8,128)(2,1)}, bf16[160,384]{1,0:T(8,128)(2,1)}, bf16[1...) custom-call(s32[160,128]{1,0:T(8,128)} %broadcast_in_dim.203.mask_ref, bf16[1024,1152]{1,0:T(8,128)(2,1)} %get-tuple-element.295.qi.ki.vi, ...), custom_call_target="tpu_custom_call" | custom-call | flops 5383127040 | bytes 11821056 | tf_op jit(solution)/shard_map/attn_bwd/pallas_call | solution.py:142
  1052.3 18.0 %grad.9 = bf16[2,1536,1152]{2,1,0:T(8,128)(2,1)} custom-call(bf16[1024,1536]{1,0:T(8,128)(2,1)} %get-tuple-element.442.refs_0_, bf16[1024,384]{1,0:T(8,128)(2,1)} %get-tuple-element.377.refs_0_.refs_1_, bf16[1024,384]{1,0:T(8,128)(2,1)} %get-tuple-element.378.refs_1_.refs_2_, bf16[1024,384]{1,0:T(8,128)(2,1)} %get-tuple-element.379.refs_2_.refs_3_, ...), custom_call_target="tpu_custom_call" | custom-call | flops 8380219392 | bytes 19808256 | tf_op jit(solution)/shard_map/grad/pallas_call | solution.py:510
  1086.6 18.4 %grad.11 = bf16[2,1536,1536]{2,1,0:T(8,128)(2,1)} custom-call(bf16[1024,1536]{1,0:T(8,128)(2,1)} %get-tuple-element.452.refs_0_, bf16[1024,1536]{1,0:T(8,128)(2,1)} %get-tuple-element.307.refs_0_.refs_1_, bf16[160,1536]{1,0:T(8,128)(2,1)} %get-tuple-element.453.refs_2_, bf16[160,1536]{1,0:T(8,128)(2,1)} %get-tuple-element.308.refs_1_.refs_3_, ...), custom_call_target="tpu_custom_call" | custom-call | flops 11173625856 | bytes 23986176 | tf_op jit(solution)/shard_map/grad/pallas_call | solution.py:510
  1105.5 18.4 %grad.10 = bf16[2,1536,1536]{2,1,0:T(8,128)(2,1)} custom-call(bf16[1024,1536]{1,0:T(8,128)(2,1)} %get-tuple-element.448.refs_0_, bf16[1024,1536]{1,0:T(8,128)(2,1)} %get-tuple-element.362.refs_0_.refs_1_, bf16[160,1536]{1,0:T(8,128)(2,1)} %get-tuple-element.449.refs_2_, bf16[160,1536]{1,0:T(8,128)(2,1)} %get-tuple-element.363.refs_1_.refs_3_, ...), custom_call_target="tpu_custom_call" | custom-call | flops 11173625856 | bytes 23986176 | tf_op jit(solution)/shard_map/grad/pallas_call | solution.py:510
  1336.9 64.7 %reduce-scatter.13.cloned.1.call-done = bf16[2,192,1536]{2,1,0:T(8,128)(2,1)} async-done(((bf16[2,1536,1536]{2,1,0:T(8,128)(2,1)}), bf16[2,192,1536]{2,1,0:T(8,128)(2,1)}) %reduce-scatter.13.cloned.1.call-update) | async-done | bytes 1179664 | tf_op jit(solution)/shard_map/reduce_scatter | solution.py:624
  1417.4 18.3 %grad.15 = bf16[2,1536,1536]{2,1,0:T(8,128)(2,1)} custom-call(bf16[1024,1536]{1,0:T(8,128)(2,1)} %get-tuple-element.532.refs_0_, bf16[1024,1536]{1,0:T(8,128)(2,1)} %get-tuple-element.285.refs_0_.refs_1_, bf16[160,1536]{1,0:T(8,128)(2,1)} %get-tuple-element.533.refs_2_, bf16[160,1536]{1,0:T(8,128)(2,1)} %get-tuple-element.286.refs_1_.refs_3_, ...), custom_call_target="tpu_custom_call" | custom-call | flops 11173625856 | bytes 23986176 | tf_op jit(solution)/shard_map/grad/pallas_call | solution.py:510
  1435.8 18.5 %grad.14 = bf16[2,1536,1536]{2,1,0:T(8,128)(2,1)} custom-call(bf16[1024,1536]{1,0:T(8,128)(2,1)} %get-tuple-element.527.refs_0_, bf16[1024,1536]{1,0:T(8,128)(2,1)} %get-tuple-element.394.refs_0_.refs_1_, bf16[160,1536]{1,0:T(8,128)(2,1)} %get-tuple-element.528.refs_2_, bf16[160,1536]{1,0:T(8,128)(2,1)} %get-tuple-element.395.refs_1_.refs_3_, ...), custom_call_target="tpu_custom_call" | custom-call | flops 11173625856 | bytes 23986176 | tf_op jit(solution)/shard_map/grad/pallas_call | solution.py:510
  1454.5 33.7 %attn_bwd.7 = (bf16[1024,384]{1,0:T(8,128)(2,1)}, bf16[1024,384]{1,0:T(8,128)(2,1)}, bf16[1024,384]{1,0:T(8,128)(2,1)}, bf16[160,384]{1,0:T(8,128)(2,1)}, bf16[1...) custom-call(s32[160,128]{1,0:T(8,128)} %broadcast_in_dim.208.mask_ref, bf16[1024,1152]{1,0:T(8,128)(2,1)} %get-tuple-element.316.qi.ki.vi, ...), custom_call_target="tpu_custom_call" | custom-call | flops 5383127040 | bytes 11821056 | tf_op jit(solution)/shard_map/attn_bwd/pallas_call | solution.py:142
  1488.2 33.6 %attn_bwd.6 = (bf16[1024,384]{1,0:T(8,128)(2,1)}, bf16[1024,384]{1,0:T(8,128)(2,1)}, bf16[1024,384]{1,0:T(8,128)(2,1)}, bf16[160,384]{1,0:T(8,128)(2,1)}, bf16[1...) custom-call(s32[160,128]{1,0:T(8,128)} %broadcast_in_dim.203.mask_ref, bf16[1024,1152]{1,0:T(8,128)(2,1)} %get-tuple-element.273.qi.ki.vi, ...), custom_call_target="tpu_custom_call" | custom-call | flops 5383127040 | bytes 11821056 | tf_op jit(solution)/shard_map/attn_bwd/pallas_call | solution.py:142
  1521.8 17.9 %grad.12 = bf16[2,1536,1152]{2,1,0:T(8,128)(2,1)} custom-call(bf16[1024,1536]{1,0:T(8,128)(2,1)} %get-tuple-element.517.refs_0_, bf16[1024,384]{1,0:T(8,128)(2,1)} %get-tuple-element.463.refs_0_.refs_1_, bf16[1024,384]{1,0:T(8,128)(2,1)} %get-tuple-element.464.refs_1_.refs_2_, bf16[1024,384]{1,0:T(8,128)(2,1)} %get-tuple-element.465.refs_2_.refs_3_, ...), custom_call_target="tpu_custom_call" | custom-call | flops 8380219392 | bytes 19808256 | tf_op jit(solution)/shard_map/grad/pallas_call | solution.py:510
  1643.7 33.6 %all-to-all-done.1 = f32[4,48,384]{2,1,0:T(8,128)S(1)} async-done(((f32[4,48,384]{2,1,0:T(8,128)}), f32[4,48,384]{2,1,0:T(8,128)S(1)}, u32[]{:S(2)}, u32[]{:S(2)}) %all-to-all-start.1) | async-done | bytes 294944 | tf_op jit(solution)/shard_map/all_to_all | solution.py:628
  1677.3 20.2 %all-gather.3 = f32[384,384]{1,0:T(8,128)S(1)} all-gather(f32[48,384]{1,0:T(8,128)S(1)} %reduce_sum.59), channel_id=5, replica_groups=mesh['dp'=8,'mp'=4] {'dp'}, dimensions={0}, use_global_device_ids=true | all-gather | bytes 663552 | tf_op jit(solution)/shard_map/all_gather | solution.py:735
  1717.9 18.2 %reduce-scatter.17.cloned.1.call-done = bf16[2,192,1152]{2,1,0:T(8,128)(2,1)} async-done(((bf16[2,1536,1152]{2,1,0:T(8,128)(2,1)}), bf16[2,192,1152]{2,1,0:T(8,128)(2,1)}) %reduce-scatter.17.cloned.1.call-update) | async-done | bytes 884752 | tf_op jit(solution)/shard_map/reduce_scatter | solution.py:624
  (953 shorter events, 1128.2 us)
Async XLA Ops:
  7.2 130.3 %all-gather.13.cloned.1.call-start = ((), (), s32[]{:S(2)}) async-start(), calls=%async_computation.10 | async-start | bytes 7962624 | tf_op jit(solution)/shard_map/all_gather | solution.py:614
  11.0 160.3 %all-gather.15.cloned.1.call-start = ((), (), s32[]{:S(2)}) async-start(), calls=%async_computation.11 | async-start | bytes 2654208 | tf_op jit(solution)/shard_map/all_gather | solution.py:614
  13.0 311.1 %all-gather.25.cloned.1.call-start = ((), (), s32[]{:S(2)}) async-start(), calls=%async_computation.24 | async-start | bytes 10616832 | tf_op jit(solution)/shard_map/all_gather | solution.py:614
  16.2 323.4 %all-gather.17.cloned.1.call-start = ((), (), s32[]{:S(2)}) async-start(), calls=%async_computation.12 | async-start | bytes 10616832 | tf_op jit(solution)/shard_map/all_gather | solution.py:614
  19.5 456.6 %all-gather.19.cloned.1.call-start = ((), (), s32[]{:S(2)}) async-start(), calls=%async_computation.13 | async-start | bytes 7962624 | tf_op jit(solution)/shard_map/all_gather | solution.py:614
  21.9 488.4 %all-gather.21.cloned.1.call-start = ((), (), s32[]{:S(2)}) async-start(), calls=%async_computation.14 | async-start | bytes 2654208 | tf_op jit(solution)/shard_map/all_gather | solution.py:614
  22.5 682.0 %all-gather.27.cloned.1.call-start = ((), (), s32[]{:S(2)}) async-start(), calls=%async_computation.25 | async-start | bytes 10616832 | tf_op jit(solution)/shard_map/all_gather | solution.py:614
  38.0 682.8 %all-gather.23.cloned.1.call-start = ((), (), s32[]{:S(2)}) async-start(), calls=%async_computation.15 | async-start | bytes 10616832 | tf_op jit(solution)/shard_map/all_gather | solution.py:614
  40.9 1296.0 %reduce-scatter.11.cloned.1.call-start = ((), (), s32[]{:S(2)}) async-start(), calls=%async_computation.17 | async-start | bytes 2654208 | tf_op jit(solution)/shard_map/reduce_scatter | solution.py:624
  622.8 58.5 %collective-permute-start.68 = (bf16[296,1536]{1,0:T(8,128)(2,1)S(1)}, bf16[296,1536]{1,0:T(8,128)(2,1)S(1)}, u32[]{:S(2)}, u32[]{:S(2)}) collective-permute-start(bf16[296,1536]{1,0:T(8,128)(2,1)S(1)} %copy-done.121), channel_id=1, source_target_pairs={{0,2},{1,0},{3,1},{2,3},{4,6},{5,4},{7,5},{6,7},{8,10},{9,8},{11,9... | collective-permute-start | bytes 2727944 | tf_op jit(solution)/shard_map/ppermute | solution.py:205
  696.8 81.1 %collective-permute-start.70 = (bf16[152,1536]{1,0:T(8,128)(2,1)}, bf16[152,1536]{1,0:T(8,128)(2,1)S(1)}, u32[]{:S(2)}, u32[]{:S(2)}) collective-permute-start(bf16[152,1536]{1,0:T(8,128)(2,1)} %slice.375), channel_id=1, source_target_pairs={{0,2},{1,0},{3,1},{2,3},{4,6},{5,4},{7,5},{6,7},{8,10},{9,8},{11,9... | collective-permute-start | bytes 1400840 | tf_op jit(solution)/shard_map/ppermute | solution.py:205
  701.6 75.1 %collective-permute-start.69 = (bf16[144,1536]{1,0:T(8,128)(2,1)}, bf16[144,1536]{1,0:T(8,128)(2,1)S(1)}, u32[]{:S(2)}, u32[]{:S(2)}) collective-permute-start(bf16[144,1536]{1,0:T(8,128)(2,1)} %slice.374), channel_id=1, source_target_pairs={{0,1},{1,3},{3,2},{2,0},{4,5},{5,7},{7,6},{6,4},{8,9},{9,11},{11,1... | collective-permute-start | bytes 1327112 | tf_op jit(solution)/shard_map/ppermute | solution.py:205
  745.7 72.0 %collective-permute-start.100 = (bf16[152,1536]{1,0:T(8,128)(2,1)}, bf16[152,1536]{1,0:T(8,128)(2,1)S(1)}, u32[]{:S(2)}, u32[]{:S(2)}) collective-permute-start(bf16[152,1536]{1,0:T(8,128)(2,1)} %get-tuple-element.415), channel_id=1, source_target_pairs={{0,2},{1,0},{3,1},{2,3},{4,6},{5,4},{7,5},{6,7},{8,10},{9,8},{11,9... | collective-permute-start | bytes 1400840 | tf_op jit(solution)/shard_map/ppermute | solution.py:205
  760.0 63.1 %collective-permute-start.62 = (bf16[152,1536]{1,0:T(8,128)(2,1)}, bf16[152,1536]{1,0:T(8,128)(2,1)S(1)}, u32[]{:S(2)}, u32[]{:S(2)}) collective-permute-start(bf16[152,1536]{1,0:T(8,128)(2,1)} %get-tuple-element.355), channel_id=1, source_target_pairs={{0,2},{1,0},{3,1},{2,3},{4,6},{5,4},{7,5},{6,7},{8,10},{9,8},{11,9... | collective-permute-start | bytes 1400840 | tf_op jit(solution)/shard_map/ppermute | solution.py:205
  934.8 60.7 %collective-permute-start.78 = (bf16[152,1536]{1,0:T(8,128)(2,1)S(1)}, bf16[152,1536]{1,0:T(8,128)(2,1)S(1)}, u32[]{:S(2)}, u32[]{:S(2)}) collective-permute-start(bf16[152,1536]{1,0:T(8,128)(2,1)S(1)} %slice.377), channel_id=1, source_target_pairs={{0,2},{1,0},{3,1},{2,3},{4,6},{5,4},{7,5},{6,7},{8,10},{9,8},{11,9... | collective-permute-start | bytes 1400840 | tf_op jit(solution)/shard_map/ppermute | solution.py:205
  935.9 59.5 %collective-permute-start.77 = (bf16[144,1536]{1,0:T(8,128)(2,1)S(1)}, bf16[144,1536]{1,0:T(8,128)(2,1)}, u32[]{:S(2)}, u32[]{:S(2)}) collective-permute-start(bf16[144,1536]{1,0:T(8,128)(2,1)S(1)} %slice.376), channel_id=1, source_target_pairs={{0,1},{1,3},{3,2},{2,0},{4,5},{5,7},{7,6},{6,4},{8,9},{9,11},{11,1... | collective-permute-start | bytes 1327112 | tf_op jit(solution)/shard_map/ppermute | solution.py:205
  1086.0 250.9 %reduce-scatter.9.cloned.1.call-start = ((), (), s32[]{:S(2)}) async-start(), calls=%async_computation.16 | async-start | bytes 7962624 | tf_op jit(solution)/shard_map/reduce_scatter | solution.py:624
  1086.6 250.4 %reduce-scatter.15.cloned.1.call-start = ((), (), s32[]{:S(2)}) async-start(), calls=%async_computation.19 | async-start | bytes 10616832 | tf_op jit(solution)/shard_map/reduce_scatter | solution.py:624
  1105.0 296.6 %reduce-scatter.13.cloned.1.call-start = ((), (), s32[]{:S(2)}) async-start(), calls=%async_computation.18 | async-start | bytes 10616832 | tf_op jit(solution)/shard_map/reduce_scatter | solution.py:624
  1123.9 584.1 %reduce-scatter.19.cloned.1.call-start = ((), (), s32[]{:S(2)}) async-start(), calls=%async_computation.21 | async-start | bytes 2654208 | tf_op jit(solution)/shard_map/reduce_scatter | solution.py:624
  1417.3 292.9 %reduce-scatter.23.cloned.1.call-start = ((), (), s32[]{:S(2)}) async-start(), calls=%async_computation.23 | async-start | bytes 10616832 | tf_op jit(solution)/shard_map/reduce_scatter | solution.py:624
  1435.7 278.4 %reduce-scatter.21.cloned.1.call-start = ((), (), s32[]{:S(2)}) async-start(), calls=%async_computation.22 | async-start | bytes 10616832 | tf_op jit(solution)/shard_map/reduce_scatter | solution.py:624
  1454.3 281.8 %reduce-scatter.17.cloned.1.call-start = ((), (), s32[]{:S(2)}) async-start(), calls=%async_computation.20 | async-start | bytes 7962624 | tf_op jit(solution)/shard_map/reduce_scatter | solution.py:624
  1636.5 66.6 %collective-permute-start.131 = (f32[296,1536]{1,0:T(8,128)}, f32[296,1536]{1,0:T(8,128)}, u32[]{:S(2)}, u32[]{:S(2)}) collective-permute-start(f32[296,1536]{1,0:T(8,128)} %broadcast_select_fusion.2), channel_id=1, source_target_pairs={{0,2},{1,3},{2,0},{3,1},{4,6},{5,7},{6,4},{7,5},{8,10},{9,11},{10,... | collective-permute-start | bytes 5455880 | tf_op jit(solution)/shard_map/ppermute | solution.py:661
  (352 other events, 6044.8 us)
Sparse Core Ops, SparseCore 0:
  11.1 86.3 all-gather.12
  99.1 29.9 all-gather.14
  131.2 89.9 all-gather.24
  223.3 89.1 all-gather.16
  313.9 69.6 all-gather.18
  385.0 29.9 all-gather.20
  417.2 89.9 all-gather.26
  508.8 89.1 all-gather.22
  1086.1 36.2 reduce-scatter.10
  1125.1 76.0 reduce-scatter.8
  1203.5 97.8 reduce-scatter.14
  1303.6 97.9 reduce-scatter.12
  1417.4 35.5 reduce-scatter.18
  1455.2 98.2 reduce-scatter.22
  1555.6 97.8 reduce-scatter.20
  1655.7 80.3 reduce-scatter.16
